TPU v7x, 32 devices: a whole 2x2x4 slice. The times are simulated.
32 devices in a mesh: seq: 16 (over z, y, x), head: 2 (over core).
Axes of the slice: x: 2, y: 2, z: 4, core: 2. Of those that a mesh axis runs over, the one named last changes fastest.
Arguments:
- query_vectors: bfloat16 [4096, 2560], P(('seq', 'head')), may hold values from -6 to 6
- address_vectors: bfloat16 [4096, 2560], P(('seq', 'head')), may hold values from -0.75 to 0.75
- payload_vectors: bfloat16 [4096, 2560], P(('seq', 'head')), may hold values from -6 to 6
- forget_logarithms: bfloat16 [4096, 2560], P(('seq', 'head')), may hold values from -1.5 to 0
- pre_sigmoid_filter: bfloat16 [4096, 2560], P(('seq', 'head')), may hold values from -6 to 6
- current_reward_table: float32 [40, 64], replicated, may hold values from -0.5 to 1.5
- cluster_standardize_weight: float32 [2560], replicated, may hold values from 0.25 to 1.75
- cluster_standardize_offset: float32 [2560], replicated, may hold values from -1.5 to 1.5
Outputs:
- mixed: bfloat16 [4096, 2560], P('seq', 'head')
All inputs are finite; a program needn't handle non-finite values.
Results may differ from a plain program's by a relative error of at most 0.001.
Values may be sent and summed in bfloat16 or wider, within the bound.
No kernel may reach another device: no remote copies, remote signals or barrier semaphores. Data moves between devices by JAX's collectives and lax.ppermute only.
A program may use at most 192 MiB of HBM per device.

v0:
```python
import math

import jax
import jax.numpy as jnp
from jax import lax
from jax.sharding import PartitionSpec as P

CHANNEL_COUNT = 64


def prefix_2(value, axis, join, neutral):
    count, mine = (lax.axis_size(axis), lax.axis_index(axis))
    pieces = jax.tree.map(lambda part: lax.all_gather(part, axis), value)
    so_far = jax.tree.map(
        lambda part, zero: jnp.full_like(part, 0) + jnp.asarray(zero, part.dtype), value, neutral
    )

    def step(position, so_far):
        longer = join(so_far, jax.tree.map(lambda part: part[position], pieces))
        return jax.tree.map(lambda new, old: jnp.where(position < mine, new, old), longer, so_far)

    return lax.fori_loop(0, count - 1, step, so_far)


def group_heads(array, groups):
    length, hosted_attenders, channels = array.shape
    return array.reshape(length, groups, hosted_attenders // groups, channels).transpose(1, 0, 2, 3)


def block_shares(
    query_vectors, address_vectors, payload_vectors, forget_logarithms, current_reward_piece
):
    length, width = query_vectors.shape
    hosted_attenders = width // CHANNEL_COUNT
    highest = lax.Precision.HIGHEST
    rows = lax.broadcasted_iota(jnp.int32, (length, length), 0)
    columns = lax.broadcasted_iota(jnp.int32, (length, length), 1)
    lower = (rows >= columns).astype(jnp.float32)
    strict = rows > columns
    forget_multiplier = forget_logarithms.astype(jnp.float32)
    cumul = jnp.dot(lower, forget_multiplier, precision=highest)
    before = (cumul - forget_multiplier).reshape(length, hosted_attenders, CHANNEL_COUNT)
    final = cumul[-1].reshape(hosted_attenders, CHANNEL_COUNT)
    cumul = cumul.reshape(length, hosted_attenders, CHANNEL_COUNT)
    incoming_memory = query_vectors.astype(jnp.float32).reshape(
        length, hosted_attenders, CHANNEL_COUNT
    )
    address_block = address_vectors.astype(jnp.float32).reshape(
        length, hosted_attenders, CHANNEL_COUNT
    )
    payload_block = payload_vectors.astype(jnp.float32).reshape(
        length, hosted_attenders, CHANNEL_COUNT
    )
    scaled_receptance = incoming_memory * jnp.exp(before)
    scaled_k = address_block * jnp.exp(-cumul)
    end_keys = address_block * jnp.exp(final[None] - cumul)
    group_size = math.gcd(hosted_attenders, 4)
    groups = hosted_attenders // group_size

    def group_output(pieces):
        receptance_group, keys_group, values_group = pieces
        scores = jnp.einsum("thc,shc->hts", receptance_group, keys_group, precision=highest)
        scores = jnp.where(strict[None], scores, jnp.float32(0.0))
        return jnp.einsum("hts,shj->thj", scores, values_group, precision=highest)

    grouped = lax.map(
        group_output,
        (
            group_heads(scaled_receptance, groups),
            group_heads(scaled_k, groups),
            group_heads(payload_block, groups),
        ),
    )
    within = grouped.transpose(1, 0, 2, 3).reshape(length, hosted_attenders, CHANNEL_COUNT)
    diagonal_piece = jnp.sum(incoming_memory * current_reward_piece[None] * address_block, axis=2)
    mixed_output = within + diagonal_piece[:, :, None] * payload_block
    slab_ends = jnp.einsum("shc,shj->hcj", end_keys, payload_block, precision=highest)
    return (mixed_output, scaled_receptance, jnp.exp(final), slab_ends)


def join_states(earlier, later):
    return (earlier[0] * later[0], later[0][:, :, None] * earlier[1] + later[1])


def finish(mixed_output, scaled_receptance, prefix, pre_sigmoid_filter, gain, bias):
    mixed_output = mixed_output + jnp.einsum(
        "thc,hcj->thj", scaled_receptance, prefix, precision=lax.Precision.HIGHEST
    )
    length = mixed_output.shape[0]
    center = mixed_output - jnp.mean(mixed_output, axis=2, keepdims=True)
    spread = jnp.mean(center * center, axis=2, keepdims=True)
    normed = (center * lax.rsqrt(spread + 1e-05)).reshape(length, -1)
    gate = pre_sigmoid_filter.astype(jnp.float32)
    return ((normed * gain[None] + bias[None]) * gate * jax.nn.sigmoid(gate)).astype(jnp.bfloat16)


def body(
    query_vectors,
    address_vectors,
    payload_vectors,
    forget_logarithms,
    pre_sigmoid_filter,
    current_reward_table,
    cluster_standardize_weight,
    cluster_standardize_offset,
):
    incoming_memory, address_block, payload_block, forget_multiplier, gate = (
        lax.all_to_all(query_vectors, "head", split_axis=1, concat_axis=0, tiled=True),
        lax.all_to_all(address_vectors, "head", split_axis=1, concat_axis=0, tiled=True),
        lax.all_to_all(payload_vectors, "head", split_axis=1, concat_axis=0, tiled=True),
        lax.all_to_all(forget_logarithms, "head", split_axis=1, concat_axis=0, tiled=True),
        lax.all_to_all(pre_sigmoid_filter, "head", split_axis=1, concat_axis=0, tiled=True),
    )
    width = incoming_memory.shape[1]
    hosted_attenders = width // CHANNEL_COUNT
    block_offset = lax.axis_index("head")
    current_reward_piece = lax.dynamic_slice_in_dim(
        current_reward_table, block_offset * hosted_attenders, hosted_attenders, 0
    )
    gain = lax.dynamic_slice_in_dim(cluster_standardize_weight, block_offset * width, width, 0)
    bias = lax.dynamic_slice_in_dim(cluster_standardize_offset, block_offset * width, width, 0)
    mixed_output, scaled_receptance, decay_total, slab_ends = block_shares(
        incoming_memory, address_block, payload_block, forget_multiplier, current_reward_piece
    )
    identity = (jnp.ones_like(decay_total), jnp.zeros_like(slab_ends))
    carried = prefix_2((decay_total, slab_ends), "seq", join_states, identity)
    return finish(mixed_output, scaled_receptance, carried[1], gate, gain, bias)


def solution(mesh):
    return jax.shard_map(
        body,
        mesh=mesh,
        in_specs=(
            P(("seq", "head"), None),
            P(("seq", "head"), None),
            P(("seq", "head"), None),
            P(("seq", "head"), None),
            P(("seq", "head"), None),
            P(),
            P(),
            P(),
        ),
        out_specs=P("seq", "head"),
        check_vma=False,
    )
```

profile of v0, /device:TPU:0, one launch (start us, length us, event | category | flops | bytes accessed | tf_op | source)
XLA Modules:
  0.0 217.2 jit_solution(4822067310482961612)
XLA Ops:
  8.6 3.5 %all-to-all-start.2 = ((bf16[128,2,1280]{2,0,1:T(8,128)(2,1)}), bf16[128,2,1280]{2,0,1:T(8,128)(2,1)S(1)}, u32[]{:S(2)}, u32[]{:S(2)}) async-start(bf16[128,2,1280]{2,0,1:T(8,128)(2,1)} %bitcast.92), calls=%async_computation.2 | async-start | bytes 1310720 | tf_op jit(solution)/shard_map/all_to_all | solution.py:111
  13.9 3.5 %all-to-all-start.3 = ((bf16[128,2,1280]{0,2,1:T(8,128)(2,1)}), bf16[128,2,1280]{0,2,1:T(8,128)(2,1)S(1)}, u32[]{:S(2)}, u32[]{:S(2)}) async-start(bf16[128,2,1280]{0,2,1:T(8,128)(2,1)} %bitcast.10), calls=%async_computation.3 | async-start | bytes 1310720 | tf_op jit(solution)/shard_map/all_to_all | solution.py:109
  22.0 3.5 %all-to-all-start = ((bf16[128,2,1280]{0,2,1:T(8,128)(2,1)}), bf16[128,2,1280]{0,2,1:T(8,128)(2,1)S(1)}, u32[]{:S(2)}, u32[]{:S(2)}) async-start(bf16[128,2,1280]{0,2,1:T(8,128)(2,1)} %bitcast), calls=%async_computation | async-start | bytes 1310720 | tf_op jit(solution)/shard_map/all_to_all | solution.py:110
  25.7 4.8 %copy.56 = f32[2,128,1280]{1,0,2:T(2,128)S(1)} copy(f32[2,128,1280]{1,2,0:T(8,128)S(1)} %convert_bitcast_fusion) | data formatting | bytes 2621440 | tf_op jit(solution)/shard_map/convert_element_type | solution.py:48
  32.4 6.1 %copy.60 = bf16[2,128,1280]{1,0,2:T(2,128)(2,1)} copy(bf16[2,128,1280]{1,2,0:T(8,128)(2,1)S(1)} %bitcast.110) | data formatting | bytes 1310720 | tf_op jit(solution)/shard_map/all_to_all | solution.py:110
  40.8 3.3 %fusion.22 = f32[20,64,64]{2,1,0:T(8,128)} fusion(bf16[256,20,64]{0,2,1:T(8,128)(2,1)S(1)} %all_to_all.69, f32[256,20,64]{0,2,1:T(8,128)S(1)} %reshape.91, f32[256,20,64]{0,2,1:T(8,128)} %bitcast.111, f32[20,64]{1,0:T(8,128)S(1)} %sub.22), kind=kOutput, calls=%fused_computation.32 | convolution fusion | flops 252313600 | bytes 3609600 | tf_op jit(solution)/shard_map/shc,shj->hcj/dot_general | solution.py:77
  46.3 3.7 %all-to-all-start.1 = ((bf16[128,2,1280]{0,2,1:T(8,128)(2,1)}), bf16[128,2,1280]{0,2,1:T(8,128)(2,1)S(1)}, u32[]{:S(2)}, u32[]{:S(2)}) async-start(bf16[128,2,1280]{0,2,1:T(8,128)(2,1)} %bitcast.3), calls=%async_computation.1 | async-start | bytes 1310720 | tf_op jit(solution)/shard_map/all_to_all | solution.py:108
  54.1 4.3 %all-to-all-start.4 = ((bf16[128,2,1280]{2,0,1:T(8,128)(2,1)}), bf16[128,2,1280]{2,0,1:T(8,128)(2,1)}, u32[]{:S(2)}, u32[]{:S(2)}) async-start(bf16[128,2,1280]{2,0,1:T(8,128)(2,1)} %bitcast.91), calls=%async_computation.4 | async-start | bytes 1310720 | tf_op jit(solution)/shard_map/all_to_all | solution.py:112
  58.5 4.8 %copy.52 = f32[2,128,1280]{1,0,2:T(2,128)S(1)} copy(f32[2,128,1280]{1,2,0:T(8,128)S(1)} %convert_bitcast_fusion.1) | data formatting | bytes 2621440 | tf_op jit(solution)/shard_map/convert_element_type | solution.py:45
  68.8 2.8 %copy.54 = f32[256,1280]{0,1:T(8,128)} copy(f32[256,1280]{1,0:T(8,128)} %get-tuple-element.191) | data formatting | bytes 2621440 | tf_op jit(solution)/shard_map/exp | solution.py:54
  71.6 2.8 %copy.57 = f32[256,1280]{0,1:T(8,128)} copy(f32[256,1280]{1,0:T(8,128)} %get-tuple-element.190) | data formatting | bytes 2621440 | tf_op jit(solution)/shard_map/exp | solution.py:55
  75.6 5.6 %copy.50 = f32[2,128,1280]{1,0,2:T(2,128)} copy(f32[2,128,1280]{1,2,0:T(8,128)S(1)} %bitcast_convert_fusion) | data formatting | bytes 2621440 | tf_op jit(solution)/shard_map/transpose | solution.py:27
  81.2 3.1 %reshape.93 = f32[256,5,4,64]{0,3,2,1:T(8,128)} reshape(f32[2,128,1280]{1,0,2:T(2,128)} %copy.50) | data formatting | bytes 2621440 | tf_op jit(solution)/shard_map/transpose | solution.py:27
  84.6 45.8 %all_gather.10 = f32[16,20,64]{2,1,0:T(8,128)S(1)} all-gather(f32[1,20,64]{2,1,0:T(8,128)S(1)} %exp.41), channel_id=1, replica_groups=mesh['seq'=16,'head'=2] {'seq'}, dimensions={0}, use_global_device_ids=true | all-gather | bytes 87040 | tf_op jit(solution)/shard_map/all_gather | solution.py:13
  130.4 3.2 %multiply_bitcast_fusion.1 = f32[5,256,4,64]{1,3,2,0:T(8,128)} fusion(f32[256,5,4,64]{0,3,2,1:T(8,128)} %reshape.88, f32[256,5,4,64]{0,3,2,1:T(8,128)} %bitcast.107), kind=kLoop, calls=%fused_computation.39 | loop fusion | flops 327680 | bytes 3932160 | tf_op jit(solution)/shard_map/transpose | solution.py:27
  134.8 24.7 %while.25 = (s32[]{:T(128)}, f32[5,256,4,64]{1,3,2,0:T(8,128)}, f32[5,256,4,64]{1,3,2,0:T(8,128)}, f32[5,256,4,64]{1,3,2,0:T(8,128)}, f32[5,256,4,64]{1,3,2,0:T(8,128)}, /*index=5*/s32[]{:T(128)}) while((s32[]{:T(128)}, f32[5,256,4,64]{1,3,2,0:T(8,128)}, f32[5,256,4,64]{1,3,2,0:T(8,128)}, f32[5,256,4,64]{1,3,2,0:T(8,128)}, ...), condition=%wide.region_1.2_spmd.clone, body=%wide.region_0.1_spmd.clone.sunk | while | flops 402980864 | bytes 3278917 | solution.py:66
  136.9 2.8 %fusion.44 = f32[5,256,4,64]{1,3,2,0:T(8,128)} fusion(f32[5,256,4,64]{1,3,2,0:T(8,128)} %get-tuple-element.264, s32[]{:T(128)} %get-tuple-element.263, f32[4,256,256]{2,1,0:T(8,128)S(1)} %convolution_select_fusion.2, f32[5,256,4,64]{1,3,2,0:T(8,128)} %get-tuple-element.271), kind=kOutput, calls=%fused_computation.3.clone.1 | convolution fusion | flops 201326592 | bytes 1573888 | tf_op jit(solution)/shard_map/while/body/eval_jaxpr/hts,shj->thj/dot_general | solution.py:64
  141.8 2.8 %fusion.44 = f32[5,256,4,64]{1,3,2,0:T(8,128)} fusion(f32[5,256,4,64]{1,3,2,0:T(8,128)} %get-tuple-element.264, s32[]{:T(128)} %get-tuple-element.263, f32[4,256,256]{2,1,0:T(8,128)S(1)} %convolution_select_fusion.2, f32[5,256,4,64]{1,3,2,0:T(8,128)} %get-tuple-element.271), kind=kOutput, calls=%fused_computation.3.clone.1 | convolution fusion | flops 201326592 | bytes 1573888 | tf_op jit(solution)/shard_map/while/body/eval_jaxpr/hts,shj->thj/dot_general | solution.py:64
  146.8 2.8 %fusion.44 = f32[5,256,4,64]{1,3,2,0:T(8,128)} fusion(f32[5,256,4,64]{1,3,2,0:T(8,128)} %get-tuple-element.264, s32[]{:T(128)} %get-tuple-element.263, f32[4,256,256]{2,1,0:T(8,128)S(1)} %convolution_select_fusion.2, f32[5,256,4,64]{1,3,2,0:T(8,128)} %get-tuple-element.271), kind=kOutput, calls=%fused_computation.3.clone.1 | convolution fusion | flops 201326592 | bytes 1573888 | tf_op jit(solution)/shard_map/while/body/eval_jaxpr/hts,shj->thj/dot_general | solution.py:64
  151.7 2.8 %fusion.44 = f32[5,256,4,64]{1,3,2,0:T(8,128)} fusion(f32[5,256,4,64]{1,3,2,0:T(8,128)} %get-tuple-element.264, s32[]{:T(128)} %get-tuple-element.263, f32[4,256,256]{2,1,0:T(8,128)S(1)} %convolution_select_fusion.2, f32[5,256,4,64]{1,3,2,0:T(8,128)} %get-tuple-element.271), kind=kOutput, calls=%fused_computation.3.clone.1 | convolution fusion | flops 201326592 | bytes 1573888 | tf_op jit(solution)/shard_map/while/body/eval_jaxpr/hts,shj->thj/dot_general | solution.py:64
  156.6 2.8 %fusion.44 = f32[5,256,4,64]{1,3,2,0:T(8,128)} fusion(f32[5,256,4,64]{1,3,2,0:T(8,128)} %get-tuple-element.264, s32[]{:T(128)} %get-tuple-element.263, f32[4,256,256]{2,1,0:T(8,128)S(1)} %convolution_select_fusion.2, f32[5,256,4,64]{1,3,2,0:T(8,128)} %get-tuple-element.271), kind=kOutput, calls=%fused_computation.3.clone.1 | convolution fusion | flops 201326592 | bytes 1573888 | tf_op jit(solution)/shard_map/while/body/eval_jaxpr/hts,shj->thj/dot_general | solution.py:64
  159.4 3.1 %fusion.15 = f32[256,20,64]{0,2,1:T(8,128)} fusion(f32[256,20,64]{0,2,1:T(8,128)} %bitcast.15, bf16[256,20,64]{0,2,1:T(8,128)(2,1)} %copy-done.3, f32[256,20,64]{0,2,1:T(8,128)S(1)} %reshape.91, f32[256,20,64]{0,2,1:T(8,128)S(1)} %reshape.90, f32[20,64]{1,0:T(8,128)S(1)} %constant_dynamic-slice_fusion), kind=kOutput, calls=%fused_computation.20 | output fusion | flops 1643583 | bytes 5903360 | tf_op jit(solution)/shard_map/mul | solution.py:76
  162.5 18.6 %all-gather.3.cloned.1.call-done = f32[320,64,64]{2,1,0:T(8,128)} async-done(((f32[20,64,64]{2,1,0:T(8,128)}), f32[320,64,64]{2,1,0:T(8,128)}) %all-gather.3.cloned.1.call-update) | async-done | bytes 5242896 | tf_op jit(solution)/shard_map/all_gather | solution.py:13
  181.1 23.3 %while.26 = (s32[]{:T(128)}, f32[20,64,64]{2,1,0:T(8,128)S(1)}, s32[]{:T(128)}, f32[16,20,64]{2,1,0:T(8,128)S(1)}, f32[16,20,64,64]{3,2,1,0:T(8,128)}, /*index=5*/s32[]{:T(128)}, s32[]{:T(128)}) while((s32[]{:T(128)}, f32[20,64,64]{2,1,0:T(8,128)S(1)}, s32[]{:T(128)}, f32[16,20,64]{2,1,0:T(8,128)S(1)}, ...), condition=%wide.region_4.5_spmd.clone, body=%wide.region_3.4_spmd.clone.sunk | while | flops 327684 | bytes 998505 | solution.py:22
  (100 shorter events, 66.6 us)
Async XLA Ops:
  6.5 123.8 %copy-start = (f32[40,64]{1,0:T(8,128)S(1)}, f32[40,64]{1,0:T(8,128)}, u32[]{:S(2)}) copy-start(f32[40,64]{1,0:T(8,128)} %param.17) | copy-start | bytes 30724
  6.5 5.6 %copy-start.7 = (bf16[128,2560]{1,0:T(8,128)(2,1)S(1)}, bf16[128,2560]{1,0:T(8,128)(2,1)}, u32[]{:S(2)}) copy-start(bf16[128,2560]{1,0:T(8,128)(2,1)} %param.13) | copy-start | bytes 1966084
  8.6 5.3 %all-to-all-start.2 = ((bf16[128,2,1280]{2,0,1:T(8,128)(2,1)}), bf16[128,2,1280]{2,0,1:T(8,128)(2,1)S(1)}, u32[]{:S(2)}, u32[]{:S(2)}) async-start(bf16[128,2,1280]{2,0,1:T(8,128)(2,1)} %bitcast.92), calls=%async_computation.2 | async-start | bytes 1310720 | tf_op jit(solution)/shard_map/all_to_all | solution.py:111
  13.9 8.1 %all-to-all-start.3 = ((bf16[128,2,1280]{0,2,1:T(8,128)(2,1)}), bf16[128,2,1280]{0,2,1:T(8,128)(2,1)S(1)}, u32[]{:S(2)}, u32[]{:S(2)}) async-start(bf16[128,2,1280]{0,2,1:T(8,128)(2,1)} %bitcast.10), calls=%async_computation.3 | async-start | bytes 1310720 | tf_op jit(solution)/shard_map/all_to_all | solution.py:109
  19.5 1.5 copy-start.8
  22.0 9.5 %all-to-all-start = ((bf16[128,2,1280]{0,2,1:T(8,128)(2,1)}), bf16[128,2,1280]{0,2,1:T(8,128)(2,1)S(1)}, u32[]{:S(2)}, u32[]{:S(2)}) async-start(bf16[128,2,1280]{0,2,1:T(8,128)(2,1)} %bitcast), calls=%async_computation | async-start | bytes 1310720 | tf_op jit(solution)/shard_map/all_to_all | solution.py:110
  25.6 155.6 %all-gather.3.cloned.1.call-start = ((), (), s32[]{:S(2)}) async-start(), calls=%async_computation.5 | async-start | bytes 11141120 | tf_op jit(solution)/shard_map/all_gather | solution.py:13
  31.5 0.8 copy-start.4
  40.7 3.4 %copy-start.3 = (bf16[256,20,64]{0,2,1:T(8,128)(2,1)}, bf16[256,20,64]{0,2,1:T(8,128)(2,1)S(1)}, u32[]{:S(2)}) copy-start(bf16[256,20,64]{0,2,1:T(8,128)(2,1)S(1)} %all_to_all.69) | copy-start | bytes 1966084
  46.3 7.8 %all-to-all-start.1 = ((bf16[128,2,1280]{0,2,1:T(8,128)(2,1)}), bf16[128,2,1280]{0,2,1:T(8,128)(2,1)S(1)}, u32[]{:S(2)}, u32[]{:S(2)}) async-start(bf16[128,2,1280]{0,2,1:T(8,128)(2,1)} %bitcast.3), calls=%async_computation.1 | async-start | bytes 1310720 | tf_op jit(solution)/shard_map/all_to_all | solution.py:108
  54.1 153.9 %all-to-all-start.4 = ((bf16[128,2,1280]{2,0,1:T(8,128)(2,1)}), bf16[128,2,1280]{2,0,1:T(8,128)(2,1)}, u32[]{:S(2)}, u32[]{:S(2)}) async-start(bf16[128,2,1280]{2,0,1:T(8,128)(2,1)} %bitcast.91), calls=%async_computation.4 | async-start | bytes 1310720 | tf_op jit(solution)/shard_map/all_to_all | solution.py:112
  63.2 1.1 copy-start.1
  81.2 3.2 %copy-start.9 = (f32[2560]{0:T(1024)S(1)}, f32[2560]{0:T(1024)}, u32[]{:S(2)}) copy-start(f32[2560]{0:T(1024)} %param.18) | copy-start | bytes 30724
  81.2 3.3 %copy-start.10 = (f32[2560]{0:T(1024)S(1)}, f32[2560]{0:T(1024)}, u32[]{:S(2)}) copy-start(f32[2560]{0:T(1024)} %param.19) | copy-start | bytes 30724
  130.4 3.2 %copy-start.5 = (f32[256,5,4,64]{0,3,2,1:T(8,128)S(1)}, f32[256,5,4,64]{0,3,2,1:T(8,128)}, u32[]{:S(2)}) copy-start(f32[256,5,4,64]{0,3,2,1:T(8,128)} %reshape.89) | copy-start | bytes 3932164
  130.4 3.2 %copy-start.6 = (f32[256,1280]{0,1:T(8,128)S(1)}, f32[256,1280]{0,1:T(8,128)}, u32[]{:S(2)}) copy-start(f32[256,1280]{0,1:T(8,128)} %copy.57) | copy-start | bytes 3932164
  181.1 23.3 %copy-start.2 = (f32[256,1280]{0,1:T(8,128)S(1)}, f32[256,1280]{0,1:T(8,128)}, u32[]{:S(2)}) copy-start(f32[256,1280]{0,1:T(8,128)} %copy.54) | copy-start | bytes 3932164
Sparse Core Ops, SparseCore 0:
  44.2 136.8 all-gather.2
where the time goes:
time: 219 us; the launch traced here: 217 us
  local copies, waits for them, and re-layouts  52.5 us (24%)
  blocking collectives  45.8 us (21%)
  other arithmetic  34.4 us (16%)
  matrix products  32.5 us (15%)
  waiting for transfers between devices  19.3 us (9%)
  starting transfers between devices  18.5 us (8%)
  between operations  13.7 us (6%)
    all_gather x1, blocking collectives, prefix_2(): pieces = jax.tree.map(lambda part: lax.all_gather(part, axis), value)  45.8 us
    select_n x15, other arithmetic, step(): jnp.where(position < mine, new, old)  22.7 us
    all_gather x1, waiting for transfers between devices, prefix_2(): pieces = jax.tree.map(lambda part: lax.all_gather(part, axis), value)  18.6 us
    dot_general x5, matrix products, group_output(): return jnp.einsum('hts,shj->thj', scores, values_group, precision=highest)  13.9 us
    dot_general x5, matrix products, group_output(): jnp.einsum('thc,shc->hts', receptance_group, keys_group, precision=highest)  10.6 us
    convert_element_type x3, local copies, waits for them, and re-layouts, block_shares(): query_vectors.astype(jnp.float32)  9.25 us
    transpose x2, local copies, waits for them, and re-layouts, group_heads(): array.reshape(length, groups, hosted_attenders // groups, channels)  8.76 us
    all_to_all x2, local copies, waits for them, and re-layouts, body(): lax.all_to_all(payload_vectors, 'head', split_axis=1, concat_axis=0, tile...  8.34 us
  transfers between devices with their start and end apart: 6, of which 2 were waited for; matrix products, arithmetic and copies ran while one was open for 47% of the time, Pallas kernels for 0%

commit v1 on v0

v1 whole, which is shorter than its diff:
```python
import functools

import jax
import jax.numpy as jnp
from jax import lax
from jax.experimental import pallas as pl
from jax.experimental.pallas import tpu as pltpu
from jax.sharding import PartitionSpec as P

CHANNELS = 64
LANES = 256
HEADS = LANES // CHANNELS
BLOCK = 64
PLANE = 4
F32 = jnp.float32
BF16 = jnp.bfloat16


def split(value):
    high = value.astype(BF16)
    return high, (value - high.astype(F32)).astype(BF16)


def dot(left, right):
    return lax.dot_general(left, right, (((1,), (0,)), ((), ())), preferred_element_type=F32)


def dot_nt(left, right):
    return lax.dot_general(left, right, (((1,), (1,)), ((), ())), preferred_element_type=F32)


def same_head(value):
    rows = lax.broadcasted_iota(jnp.int32, (LANES, LANES), 0) // CHANNELS
    columns = lax.broadcasted_iota(jnp.int32, (LANES, LANES), 1) // CHANNELS
    return jnp.where(rows == columns, F32(value), F32(0.0)).astype(BF16)


def head_of_lane(rows):
    return lax.broadcasted_iota(jnp.int32, (rows, LANES), 1) // CHANNELS


def own_blocks(stacked, rows):
    lane_head = head_of_lane(rows)
    picked = stacked[:rows]
    for head in range(1, HEADS):
        picked = jnp.where(lane_head == head, stacked[head * rows : (head + 1) * rows], picked)
    return picked


def cumulate(decay):
    length = decay.shape[0]
    rows = lax.broadcasted_iota(jnp.int32, (length, length), 0)
    columns = lax.broadcasted_iota(jnp.int32, (length, length), 1)
    lower = jnp.where(rows >= columns, F32(1.0), F32(0.0)).astype(BF16)
    return dot(lower, decay)


def ends_of(key, value, decay, out_ref):
    length = decay.shape[0]
    cumul = cumulate(decay)
    final = cumul[length - 1 : length]
    high, low = split(key.astype(F32) * jnp.exp(final - cumul))
    turned = value.astype(F32).T.astype(BF16)
    out_ref[0, :CHANNELS, :] = own_blocks(dot(turned, high) + dot(turned, low), CHANNELS)
    out_ref[0, CHANNELS:, :] = jnp.broadcast_to(jnp.exp(final), (8, LANES))


def ends_kernel(core_ref, km, vm, wm, kt, vt, wt, mine_ref, theirs_ref):
    ends_of(kt[...], vt[...], wt[...], theirs_ref)
    ends_of(km[...], vm[...], wm[...], mine_ref)


def within_kernel(core_ref, r_ref, k_ref, v_ref, w_ref, bonus_ref, out_ref):
    r, k, v, w = r_ref[...].astype(F32), k_ref[...].astype(F32), v_ref[...], w_ref[...]
    length = w.shape[0]
    cumul = cumulate(w)
    before = cumul - w.astype(F32)
    lane_head = head_of_lane(BLOCK)
    diagonal_high, diagonal_low = split(r * bonus_ref[...] * k)
    ones = same_head(1.0)
    diagonal = dot(diagonal_high, ones) + dot(diagonal_low, ones)
    pieces = []
    for start in range(0, length, BLOCK):
        stop = start + BLOCK
        middle = start + BLOCK // 2 - 1
        reference = cumul[middle : middle + 1]
        receptance = r[start:stop] * jnp.exp(before[start:stop] - reference)
        stacked = jnp.concatenate(
            [jnp.where(lane_head == head, receptance, F32(0.0)) for head in range(HEADS)], axis=0
        )
        r_high, r_low = split(stacked)
        k_high, k_low = split(k[:stop] * jnp.exp(reference - cumul[:stop]))
        scores = dot_nt(r_high, k_high) + dot_nt(r_low, k_high) + dot_nt(r_high, k_low)
        later = lax.broadcasted_iota(jnp.int32, scores.shape, 0) % BLOCK + start
        earlier = lax.broadcasted_iota(jnp.int32, scores.shape, 1)
        s_high, s_low = split(jnp.where(later > earlier, scores, F32(0.0)))
        pieces.append(own_blocks(dot(s_high, v[:stop]) + dot(s_low, v[:stop]), BLOCK))
    mixed = jnp.concatenate(pieces, axis=0) + diagonal * v.astype(F32)
    m_high, m_low = split(mixed)
    share = same_head(1.0 / CHANNELS)
    out_ref[0] = mixed - (dot(m_high, share) + dot(m_low, share))
    out_ref[1] = r * jnp.exp(before)


def finish_kernel(
    place_ref, p0, p1, p2, p3, ends_mine, ends_other, in_mine, in_other, g_mine, g_other,
    gain_ref, bias_ref, out_ref, state_ref,
):
    core, place = place_ref[0], place_ref[1]
    rows = CHANNELS // PLANE
    for step, piece in enumerate((p0, p1, p2, p3)):
        at = pl.multiple_of(lax.bitwise_xor(place, step) * rows, rows)
        state_ref[pl.ds(at, rows), :] = piece[...]
    length = in_mine.shape[1]
    first = core == 0
    share = same_head(1.0 / CHANNELS)
    mask_rows = lax.broadcasted_iota(jnp.int32, (LANES, LANES), 0) // CHANNELS
    mask = mask_rows == head_of_lane(LANES)
    early = jnp.where(first, ends_mine[0], ends_other[0])
    state = state_ref[...]
    for half in range(2):
        local = core == half
        if half == 1:
            state = early[CHANNELS : CHANNELS + 1] * state + early[:CHANNELS]
        centred = state - jnp.mean(state, axis=0, keepdims=True)
        wide = jnp.where(mask, jnp.concatenate([centred] * HEADS, axis=0), F32(0.0))
        s_high, s_low = split(wide)
        r_high, r_low = split(jnp.where(local, in_mine[1], in_other[1]))
        mixed = jnp.where(local, in_mine[0], in_other[0])
        mixed = mixed + (dot_nt(r_high, s_high) + dot_nt(r_low, s_high) + dot_nt(r_high, s_low))
        q_high, q_low = split(mixed * mixed)
        spread = dot(q_high, share) + dot(q_low, share)
        normed = mixed * lax.rsqrt(spread + 1e-5)
        gate = jnp.where(local, g_mine[...].astype(F32), g_other[...].astype(F32))
        gated = (normed * gain_ref[...] + bias_ref[...]) * gate / (1.0 + jnp.exp(-gate))
        out_ref[half * length : (half + 1) * length, :] = gated.astype(BF16)


def body(r, k, v, w, gate, bonus, gain, bias):
    length, width = r.shape
    cores, count = lax.axis_size("head"), lax.axis_size("seq")
    assert cores == 2 and count % PLANE == 0
    half = width // cores
    groups = half // LANES
    core, position = lax.axis_index("head"), lax.axis_index("seq")
    place = position % PLANE
    where = jnp.stack([core, place]).astype(jnp.int32)
    swap = [(0, 1), (1, 0)]

    def lanes(side):
        def index(g, ref):
            c = ref[0] if side == 0 else 1 - ref[0]
            return (0, c * groups + g)
        return index

    token = lambda side: pl.BlockSpec((length, LANES), lanes(side))
    row = lambda side: pl.BlockSpec((1, LANES), lanes(side))
    ends_spec = pl.BlockSpec((1, CHANNELS + 8, LANES), lambda g, ref: (g, 0, 0))
    ends_shape = jax.ShapeDtypeStruct((groups, CHANNELS + 8, LANES), F32)
    mine, theirs = pl.pallas_call(
        ends_kernel,
        out_shape=[ends_shape, ends_shape],
        grid_spec=pltpu.PrefetchScalarGridSpec(
            num_scalar_prefetch=1,
            grid=(groups,),
            in_specs=[token(0)] * 3 + [token(1)] * 3,
            out_specs=[ends_spec, ends_spec],
        ),
        name="ends",
    )(where, k, v, w, k, v, w)
    other = lax.ppermute(theirs, "head", swap)

    pair_spec = pl.BlockSpec((2, length, LANES), lambda g, ref: (0, 0, g))

    def within(side):
        return pl.pallas_call(
            within_kernel,
            out_shape=jax.ShapeDtypeStruct((2, length, half), F32),
            grid_spec=pltpu.PrefetchScalarGridSpec(
                num_scalar_prefetch=1,
                grid=(groups,),
                in_specs=[token(side)] * 4 + [row(side)],
                out_specs=pair_spec,
            ),
            name="within_other" if side else "within_mine",
        )(where, r, k, v, w, bonus.reshape(1, width))

    in_other = lax.ppermute(within(1), "head", swap)
    in_mine = within(0)
    gate_other = lax.ppermute(gate, "head", swap)

    first = jnp.where(core == 0, mine, other)
    second = jnp.where(core == 0, other, mine)
    chip = first[:, :CHANNELS] * second[:, CHANNELS : CHANNELS + 1] + second[:, :CHANNELS]
    chip_decay = first[:, CHANNELS] * second[:, CHANNELS]
    rows = CHANNELS // PLANE
    quarters = chip.reshape(groups, PLANE, rows, LANES)
    packed_rows = groups * rows

    def pack(state, decay):
        pad = jnp.zeros((-groups % 8, LANES), F32)
        return jnp.concatenate([state.reshape(packed_rows, LANES), decay, pad], axis=0)

    def unpack(packed):
        state = packed[:packed_rows].reshape(groups, rows, LANES)
        return state, packed[packed_rows : packed_rows + groups]

    def to_place(step):
        return [(i, i ^ step) for i in range(count)]

    def quarter(step):
        return pack(
            lax.dynamic_index_in_dim(quarters, place ^ step, 1, keepdims=False), chip_decay
        )

    got = [quarter(0)] + [
        lax.ppermute(quarter(step), "seq", to_place(step)) for step in range(1, PLANE)
    ]

    def choose(options, at):
        picked = options[0]
        for index in range(1, PLANE):
            picked = jnp.where(at == index, options[index], picked)
        return picked

    def join(earlier, later):
        return (later[1][:, None, :] * earlier[0] + later[0], earlier[1] * later[1])

    slabs = [unpack(choose(got, place ^ slab)) for slab in range(PLANE)]
    prefixes = [(jnp.zeros_like(slabs[0][0]), jnp.ones_like(slabs[0][1]))]
    for slab in slabs:
        prefixes.append(join(prefixes[-1], slab))
    window = prefixes.pop()
    before = None
    distance = 1
    while distance < count // PLANE:
        hop = distance * PLANE
        got = unpack(
            lax.ppermute(pack(*window), "seq", [(i, i + hop) for i in range(count - hop)])
        )
        before = got if before is None else join(got, before)
        window = join(got, window)
        distance *= 2
    if before is not None:
        finals = [join(before, prefix)[0] for prefix in prefixes]
    else:
        finals = [prefix[0] for prefix in prefixes]
    finals = [final.reshape(packed_rows, LANES) for final in finals]
    states = [choose(finals, place)] + [
        lax.ppermute(choose(finals, place ^ step), "seq", to_place(step))
        for step in range(1, PLANE)
    ]
    piece_spec = pl.BlockSpec((rows, LANES), lambda g, ref: (g, 0))
    return pl.pallas_call(
        finish_kernel,
        out_shape=jax.ShapeDtypeStruct((cores * length, half), BF16),
        grid_spec=pltpu.PrefetchScalarGridSpec(
            num_scalar_prefetch=1,
            grid=(groups,),
            in_specs=[piece_spec] * PLANE
            + [ends_spec] * 2
            + [pair_spec] * 2
            + [token(0)] * 2
            + [row(0)] * 2,
            out_specs=pl.BlockSpec((cores * length, LANES), lambda g, ref: (0, g)),
            scratch_shapes=[pltpu.VMEM((CHANNELS, LANES), F32)],
        ),
        name="finish",
    )(where, *states, mine, other, in_mine, in_other, gate, gate_other,
      gain.reshape(1, width), bias.reshape(1, width))


def solution(mesh):
    tokens = P(("seq", "head"), None)
    return jax.shard_map(
        body,
        mesh=mesh,
        in_specs=(tokens,) * 5 + (P(), P(), P()),
        out_specs=P("seq", "head"),
        check_vma=False,
    )
```

time: 219 us -> 63.6 us (0.29)
  the two profiles are of different devices: /device:TPU:0 before, /device:TPU:24 now
where the time goes in v1:
time: 63.6 us; the launch traced here: 62.9 us
  Pallas kernels  31.8 us (50%)
  waiting for transfers between devices  14.3 us (22%)
  starting transfers between devices  10.1 us (16%)
  local copies, waits for them, and re-layouts  3.29 us (5%)
  other arithmetic  3.13 us (5%)
    pallas_call x2, Pallas kernels, within(): pl.pallas_call(within_kernel, out_shape=jax.ShapeDtypeStruct((2, length,...  17.8 us
    ppermute x2, waiting for transfers between devices, body(): lax.ppermute(pack(*window), 'seq', [(i, i + hop) for i in range(count - h...  12.5 us
    pallas_call x1, Pallas kernels, body(): pl.pallas_call(finish_kernel, out_shape=jax.ShapeDtypeStruct((cores * len...  7.92 us
    pallas_call x1, Pallas kernels, body(): pl.pallas_call(ends_kernel, out_shape=[ends_shape, ends_shape], grid_spec...  6.05 us
    ppermute x3, starting transfers between devices, body(): lax.ppermute(quarter(step), 'seq', to_place(step))  3.55 us
    ppermute x3, starting transfers between devices, body(): lax.ppermute(choose(finals, place ^ step), 'seq', to_place(step))  3.49 us
    ppermute x2, starting transfers between devices, body(): lax.ppermute(pack(*window), 'seq', [(i, i + hop) for i in range(count - h...  2.58 us
    ppermute x1, waiting for transfers between devices, body(): other = lax.ppermute(theirs, 'head', swap)  1.77 us
  transfers between devices with their start and end apart: 11, of which 3 were waited for; matrix products, arithmetic and copies ran while one was open for 5% of the time, Pallas kernels for 28%

profile of v1, /device:TPU:24, one launch (start us, length us, event | category | flops | bytes accessed | tf_op | source)
XLA Modules:
  0.0 62.9 jit_solution(10383875070587114920)
XLA Ops:
  0.0 0.6 pad_add_fusion.core_ref.place_ref
  0.6 6.0 %ends.1 = (f32[5,72,256]{2,1,0:T(8,128)}, f32[5,72,256]{2,1,0:T(8,128)}) custom-call(s32[2]{0:T(128)} %pad_add_fusion.core_ref.place_ref, bf16[128,2560]{1,0:T(8,128)(2,1)} %k_ref.3, bf16[128,2560]{1,0:T(8,128)(2,1)} %v_ref.3, bf16[128,2560]{1,0:T(8,128)(2,1)} %w_ref.3, bf16[128,2560]{1,0:T(8,128)(2,1)} %k_ref.3, bf16[128,2560]{1,0:T(8,128)(2,1)} %v_ref.3, ...), custom_call_target="tpu_custom_call" | custom-call | tf_op jit(solution)/shard_map/ends/pallas_call | solution.py:160
  6.7 1.8 %collective-permute-done.ends_other = f32[5,72,256]{2,1,0:T(8,128)S(1)} collective-permute-done((f32[5,72,256]{2,1,0:T(8,128)}, f32[5,72,256]{2,1,0:T(8,128)S(1)}, u32[]{:S(2)}, u32[]{:S(2)}) %collective-permute-start) | collective-permute-done | bytes 368672 | tf_op jit(solution)/shard_map/ppermute | solution.py:171
  8.5 1.2 %broadcast_select_fusion = (f32[5,72,256]{2,1,0:T(8,128)S(1)}, f32[5,72,256]{2,1,0:T(8,128)S(1)}) fusion(f32[5,72,256]{2,1,0:T(8,128)S(1)} %collective-permute-done.ends_other, f32[5,72,256]{2,1,0:T(8,128)} %get-tuple-element.7.ends_mine, pred[]{:T(512)S(6)} %eq.55), kind=kLoop, calls=%fused_computation.6 | loop fusion | flops 184320 | bytes 1474561 | tf_op jit(solution)/shard_map/jit(_where)/select_n | solution.py:193
  10.0 2.5 %collective-permute-start.1 = (f32[88,256]{1,0:T(8,128)S(1)}, f32[88,256]{1,0:T(8,128)S(1)}, u32[]{:S(2)}, u32[]{:S(2)}) collective-permute-start(f32[88,256]{1,0:T(8,128)S(1)} %get-tuple-element.36), channel_id=1, source_target_pairs={{0,6},{2,4},{4,2},{6,0},{8,14},{10,12},{12,10},{14,8},{16,22},{18,... | collective-permute-start | bytes 270344 | tf_op jit(solution)/shard_map/ppermute | solution.py:217
  12.5 0.5 collective-permute-start.2
  13.0 0.5 collective-permute-start.3
  13.5 0.7 %reshape.76.bonus_ref = f32[1,2560]{1,0:T(1,128)} reshape(f32[40,64]{1,0:T(8,128)S(1)} %copy-done.7) | data formatting | bytes 20480 | tf_op jit(solution)/shard_map/reshape | solution.py:186
  14.2 8.9 %within_other.1 = f32[2,128,1280]{2,1,0:T(8,128)} custom-call(s32[2]{0:T(128)} %pad_add_fusion.core_ref.place_ref, bf16[128,2560]{1,0:T(8,128)(2,1)} %r_ref.3, bf16[128,2560]{1,0:T(8,128)(2,1)} %k_ref.3, bf16[128,2560]{1,0:T(8,128)(2,1)} %v_ref.3, bf16[128,2560]{1,0:T(8,128)(2,1)} %w_ref.3, f32[1,2560]{1,0:T(1,128)} %reshape.76.bonus_ref), custom_call_target="tpu_custom_call" | custom-call | tf_op jit(solution)/shard_map/within_other/pallas_call | solution.py:176
  23.6 1.3 %collective-permute-start.4 = (f32[88,256]{1,0:T(8,128)S(1)}, f32[88,256]{1,0:T(8,128)S(1)}, u32[]{:S(2)}, u32[]{:S(2)}) collective-permute-start(f32[88,256]{1,0:T(8,128)S(1)} %maximum_maximum_fusion), channel_id=1, source_target_pairs={{0,8},{2,10},{4,12},{6,14},{8,16},{10,18},{12,20},{14,22},{16,24},... | collective-permute-start | bytes 270344 | tf_op jit(solution)/shard_map/ppermute | solution.py:239
  24.9 0.5 collective-permute-start.10
  25.4 5.0 %collective-permute-done.4 = f32[88,256]{1,0:T(8,128)S(1)} collective-permute-done((f32[88,256]{1,0:T(8,128)S(1)}, f32[88,256]{1,0:T(8,128)S(1)}, u32[]{:S(2)}, u32[]{:S(2)}) %collective-permute-start.4) | collective-permute-done | bytes 90144 | tf_op jit(solution)/shard_map/ppermute | solution.py:239
  30.5 1.3 %collective-permute-start.5 = (f32[88,256]{1,0:T(8,128)S(1)}, f32[88,256]{1,0:T(8,128)S(1)}, u32[]{:S(2)}, u32[]{:S(2)}) collective-permute-start(f32[88,256]{1,0:T(8,128)S(1)} %maximum_maximum_fusion.1), channel_id=1, source_target_pairs={{0,16},{2,18},{4,20},{6,22},{8,24},{10,26},{12,28},{14,30},{1,17},... | collective-permute-start | bytes 270344 | tf_op jit(solution)/shard_map/ppermute | solution.py:239
  31.8 7.4 %collective-permute-done.5 = f32[88,256]{1,0:T(8,128)S(1)} collective-permute-done((f32[88,256]{1,0:T(8,128)S(1)}, f32[88,256]{1,0:T(8,128)S(1)}, u32[]{:S(2)}, u32[]{:S(2)}) %collective-permute-start.5) | collective-permute-done | bytes 90144 | tf_op jit(solution)/shard_map/ppermute | solution.py:239
  39.4 0.7 %fusion.9 = (f32[80,256]{1,0:T(8,128)S(1)}, f32[80,256]{1,0:T(8,128)}) fusion(f32[80,256]{1,0:T(8,128)S(1)} %get-tuple-element.10, f32[80,256]{1,0:T(8,128)S(1)} %get-tuple-element.14, f32[88,256]{1,0:T(8,128)S(1)} %get-tuple-element.19, f32[5,256]{1,0:T(8,128)S(1)} %get-tuple-element.32, f32[5,256]{1,0:T(8,128)S(1)} %get-tuple-element.12, ...), kind=kLoop, calls=%fused_computation.27 | loop fusion | flops 307200 | bytes 517126 | tf_op jit(solution)/shard_map/jit(_where)/select_n | solution.py:223
  40.1 1.5 %collective-permute-start.6 = (f32[80,256]{1,0:T(8,128)S(1)}, f32[80,256]{1,0:T(8,128)S(1)}, u32[]{:S(2)}, u32[]{:S(2)}) collective-permute-start(f32[80,256]{1,0:T(8,128)S(1)} %fusion.7), channel_id=1, source_target_pairs={{0,2},{2,0},{4,6},{6,4},{8,10},{10,8},{12,14},{14,12},{16,18},{18,... | collective-permute-start | bytes 245768 | tf_op jit(solution)/shard_map/ppermute | solution.py:250
  41.6 1.5 %collective-permute-start.7 = (f32[80,256]{1,0:T(8,128)S(1)}, f32[80,256]{1,0:T(8,128)S(1)}, u32[]{:S(2)}, u32[]{:S(2)}) collective-permute-start(f32[80,256]{1,0:T(8,128)S(1)} %get-tuple-element.17), channel_id=1, source_target_pairs={{0,4},{2,6},{4,0},{6,2},{8,12},{10,14},{12,8},{14,10},{16,20},{18,... | collective-permute-start | bytes 245768 | tf_op jit(solution)/shard_map/ppermute | solution.py:250
  43.1 0.5 collective-permute-start.8
  43.6 8.9 %within_mine.1.in_mine = f32[2,128,1280]{2,1,0:T(8,128)} custom-call(s32[2]{0:T(128)} %pad_add_fusion.core_ref.place_ref, bf16[128,2560]{1,0:T(8,128)(2,1)} %r_ref.3, bf16[128,2560]{1,0:T(8,128)(2,1)} %k_ref.3, bf16[128,2560]{1,0:T(8,128)(2,1)} %v_ref.3, bf16[128,2560]{1,0:T(8,128)(2,1)} %w_ref.3, f32[1,2560]{1,0:T(1,128)} %reshape.76.bonus_ref), custom_call_target="tpu_custom_call" | custom-call | tf_op jit(solution)/shard_map/within_mine/pallas_call | solution.py:176
  52.5 0.6 reshape.77.gain_ref
  53.1 0.6 reshape.78.bias_ref
  53.7 0.7 %copy-done.3 = bf16[128,2560]{1,0:T(8,128)(2,1)} copy-done((bf16[128,2560]{1,0:T(8,128)(2,1)}, bf16[128,2560]{1,0:T(8,128)(2,1)S(1)}, u32[]{:S(2)}) %copy-start.3) | copy-done | bytes 655384
  54.6 0.4 copy-done.1
  55.0 7.9 %finish.1 = bf16[256,1280]{1,0:T(8,128)(2,1)} custom-call(s32[2]{0:T(128)} %pad_add_fusion.core_ref.place_ref, f32[80,256]{1,0:T(8,128)} %get-tuple-element.18.p0, f32[80,256]{1,0:T(8,128)} %copy-done.4, f32[80,256]{1,0:T(8,128)} %copy-done.5, f32[80,256]{1,0:T(8,128)} %copy-done.6, f32[5,72,256]{2,1,0:T(8,128)} %get-tuple-element.7.ends_mine, ...), custom_call_target="tpu_custom_call" | custom-call | tf_op jit(solution)/shard_map/finish/pallas_call | solution.py:254
  (48 shorter events, 1.0 us)
Async XLA Ops:
  6.6 1.9 %collective-permute-start = (f32[5,72,256]{2,1,0:T(8,128)}, f32[5,72,256]{2,1,0:T(8,128)S(1)}, u32[]{:S(2)}, u32[]{:S(2)}) collective-permute-start(f32[5,72,256]{2,1,0:T(8,128)} %get-tuple-element.8), channel_id=1, source_target_pairs={{0,1},{1,0},{2,3},{3,2},{4,5},{5,4},{6,7},{7,6},{8,9},{9,8},{10,11... | collective-permute-start | bytes 1105928 | tf_op jit(solution)/shard_map/ppermute | solution.py:171
  8.5 1.4 %copy-start = (f32[5,72,256]{2,1,0:T(8,128)}, f32[5,72,256]{2,1,0:T(8,128)S(1)}, u32[]{:S(2)}) copy-start(f32[5,72,256]{2,1,0:T(8,128)S(1)} %collective-permute-done.ends_other) | copy-start | bytes 1105924
  9.7 3.8 %copy-start.7 = (f32[40,64]{1,0:T(8,128)S(1)}, f32[40,64]{1,0:T(8,128)}, u32[]{:S(2)}) copy-start(f32[40,64]{1,0:T(8,128)} %param.13) | copy-start | bytes 30724
  10.0 13.2 %collective-permute-start.1 = (f32[88,256]{1,0:T(8,128)S(1)}, f32[88,256]{1,0:T(8,128)S(1)}, u32[]{:S(2)}, u32[]{:S(2)}) collective-permute-start(f32[88,256]{1,0:T(8,128)S(1)} %get-tuple-element.36), channel_id=1, source_target_pairs={{0,6},{2,4},{4,2},{6,0},{8,14},{10,12},{12,10},{14,8},{16,22},{18,... | collective-permute-start | bytes 270344 | tf_op jit(solution)/shard_map/ppermute | solution.py:217
  12.5 10.7 %collective-permute-start.2 = (f32[88,256]{1,0:T(8,128)S(1)}, f32[88,256]{1,0:T(8,128)S(1)}, u32[]{:S(2)}, u32[]{:S(2)}) collective-permute-start(f32[88,256]{1,0:T(8,128)S(1)} %get-tuple-element.35), channel_id=1, source_target_pairs={{0,4},{2,6},{4,0},{6,2},{8,12},{10,14},{12,8},{14,10},{16,20},{18,... | collective-permute-start | bytes 270344 | tf_op jit(solution)/shard_map/ppermute | solution.py:217
  13.0 10.2 %collective-permute-start.3 = (f32[88,256]{1,0:T(8,128)S(1)}, f32[88,256]{1,0:T(8,128)S(1)}, u32[]{:S(2)}, u32[]{:S(2)}) collective-permute-start(f32[88,256]{1,0:T(8,128)S(1)} %get-tuple-element.34), channel_id=1, source_target_pairs={{0,2},{2,0},{4,6},{6,4},{8,10},{10,8},{12,14},{14,12},{16,18},{18,... | collective-permute-start | bytes 270344 | tf_op jit(solution)/shard_map/ppermute | solution.py:217
  23.1 1.7 %copy-start.2 = (bf16[128,2560]{1,0:T(8,128)(2,1)S(1)}, bf16[128,2560]{1,0:T(8,128)(2,1)}, u32[]{:S(2)}) copy-start(bf16[128,2560]{1,0:T(8,128)(2,1)} %g_mine.1) | copy-start | bytes 1966084
  23.1 30.6 %collective-permute-start.9 = (f32[2,128,1280]{2,1,0:T(8,128)}, f32[2,128,1280]{2,1,0:T(8,128)S(1)}, u32[]{:S(2)}, u32[]{:S(2)}) collective-permute-start(f32[2,128,1280]{2,1,0:T(8,128)} %within_other.1), channel_id=1, source_target_pairs={{0,1},{1,0},{2,3},{3,2},{4,5},{5,4},{6,7},{7,6},{8,9},{9,8},{10,11... | collective-permute-start | bytes 3932168 | tf_op jit(solution)/shard_map/ppermute | solution.py:188
  23.6 6.9 %collective-permute-start.4 = (f32[88,256]{1,0:T(8,128)S(1)}, f32[88,256]{1,0:T(8,128)S(1)}, u32[]{:S(2)}, u32[]{:S(2)}) collective-permute-start(f32[88,256]{1,0:T(8,128)S(1)} %maximum_maximum_fusion), channel_id=1, source_target_pairs={{0,8},{2,10},{4,12},{6,14},{8,16},{10,18},{12,20},{14,22},{16,24},... | collective-permute-start | bytes 270344 | tf_op jit(solution)/shard_map/ppermute | solution.py:239
  24.9 28.8 %collective-permute-start.10 = (bf16[128,2560]{1,0:T(8,128)(2,1)S(1)}, bf16[128,2560]{1,0:T(8,128)(2,1)S(1)}, u32[]{:S(2)}, u32[]{:S(2)}) collective-permute-start(bf16[128,2560]{1,0:T(8,128)(2,1)S(1)} %copy-done.2), channel_id=1, source_target_pairs={{0,1},{1,0},{2,3},{3,2},{4,5},{5,4},{6,7},{7,6},{8,9},{9,8},{10,11... | collective-permute-start | bytes 1966088 | tf_op jit(solution)/shard_map/ppermute | solution.py:190
  30.5 8.7 %collective-permute-start.5 = (f32[88,256]{1,0:T(8,128)S(1)}, f32[88,256]{1,0:T(8,128)S(1)}, u32[]{:S(2)}, u32[]{:S(2)}) collective-permute-start(f32[88,256]{1,0:T(8,128)S(1)} %maximum_maximum_fusion.1), channel_id=1, source_target_pairs={{0,16},{2,18},{4,20},{6,22},{8,24},{10,26},{12,28},{14,30},{1,17},... | collective-permute-start | bytes 270344 | tf_op jit(solution)/shard_map/ppermute | solution.py:239
  40.1 13.6 %collective-permute-start.6 = (f32[80,256]{1,0:T(8,128)S(1)}, f32[80,256]{1,0:T(8,128)S(1)}, u32[]{:S(2)}, u32[]{:S(2)}) collective-permute-start(f32[80,256]{1,0:T(8,128)S(1)} %fusion.7), channel_id=1, source_target_pairs={{0,2},{2,0},{4,6},{6,4},{8,10},{10,8},{12,14},{14,12},{16,18},{18,... | collective-permute-start | bytes 245768 | tf_op jit(solution)/shard_map/ppermute | solution.py:250
  41.6 12.1 %collective-permute-start.7 = (f32[80,256]{1,0:T(8,128)S(1)}, f32[80,256]{1,0:T(8,128)S(1)}, u32[]{:S(2)}, u32[]{:S(2)}) collective-permute-start(f32[80,256]{1,0:T(8,128)S(1)} %get-tuple-element.17), channel_id=1, source_target_pairs={{0,4},{2,6},{4,0},{6,2},{8,12},{10,14},{12,8},{14,10},{16,20},{18,... | collective-permute-start | bytes 245768 | tf_op jit(solution)/shard_map/ppermute | solution.py:250
  43.1 9.4 %copy-start.8 = (f32[2560]{0:T(1024)S(1)}, f32[2560]{0:T(1024)}, u32[]{:S(2)}) copy-start(f32[2560]{0:T(1024)} %param.14) | copy-start | bytes 30724
  43.1 10.0 %copy-start.9 = (f32[2560]{0:T(1024)S(1)}, f32[2560]{0:T(1024)}, u32[]{:S(2)}) copy-start(f32[2560]{0:T(1024)} %param.15) | copy-start | bytes 30724
  43.1 10.6 %collective-permute-start.8 = (f32[80,256]{1,0:T(8,128)S(1)}, f32[80,256]{1,0:T(8,128)S(1)}, u32[]{:S(2)}, u32[]{:S(2)}) collective-permute-start(f32[80,256]{1,0:T(8,128)S(1)} %get-tuple-element.9), channel_id=1, source_target_pairs={{0,6},{2,4},{4,2},{6,0},{8,14},{10,12},{12,10},{14,8},{16,22},{18,... | collective-permute-start | bytes 245768 | tf_op jit(solution)/shard_map/ppermute | solution.py:250
  53.7 0.8 %copy-start.3 = (bf16[128,2560]{1,0:T(8,128)(2,1)}, bf16[128,2560]{1,0:T(8,128)(2,1)S(1)}, u32[]{:S(2)}) copy-start(bf16[128,2560]{1,0:T(8,128)(2,1)S(1)} %collective-permute-done.10.g_other) | copy-start | bytes 1966084
  53.7 0.9 %copy-start.4 = (f32[80,256]{1,0:T(8,128)}, f32[80,256]{1,0:T(8,128)S(1)}, u32[]{:S(2)}) copy-start(f32[80,256]{1,0:T(8,128)S(1)} %collective-permute-done.6.p1) | copy-start | bytes 245764
  53.7 0.9 %copy-start.5 = (f32[80,256]{1,0:T(8,128)}, f32[80,256]{1,0:T(8,128)S(1)}, u32[]{:S(2)}) copy-start(f32[80,256]{1,0:T(8,128)S(1)} %collective-permute-done.7.p2) | copy-start | bytes 245764
  53.7 0.9 %copy-start.6 = (f32[80,256]{1,0:T(8,128)}, f32[80,256]{1,0:T(8,128)S(1)}, u32[]{:S(2)}) copy-start(f32[80,256]{1,0:T(8,128)S(1)} %collective-permute-done.8.p3) | copy-start | bytes 245764
  53.7 1.3 %copy-start.1 = (f32[2,128,1280]{2,1,0:T(8,128)}, f32[2,128,1280]{2,1,0:T(8,128)S(1)}, u32[]{:S(2)}) copy-start(f32[2,128,1280]{2,1,0:T(8,128)S(1)} %collective-permute-done.9.in_other) | copy-start | bytes 3932164

commit v2 on v1

v2 whole, which is shorter than its diff:
```python
import functools

import jax
import jax.numpy as jnp
from jax import lax
from jax.experimental import pallas as pl
from jax.experimental.pallas import tpu as pltpu
from jax.sharding import PartitionSpec as P

CHANNELS = 64
LANES = 256
HEADS = LANES // CHANNELS
BLOCK = 64
PLANE = 4
VMEM_LIMIT = 16 * 2**20
F32 = jnp.float32
BF16 = jnp.bfloat16


def split(value):
    high = value.astype(BF16)
    return high, (value - high.astype(F32)).astype(BF16)


def dot(left, right):
    return lax.dot_general(left, right, (((1,), (0,)), ((), ())), preferred_element_type=F32)


def dot_nt(left, right):
    return lax.dot_general(left, right, (((1,), (1,)), ((), ())), preferred_element_type=F32)


def same_head(value):
    rows = lax.broadcasted_iota(jnp.int32, (LANES, LANES), 0) // CHANNELS
    columns = lax.broadcasted_iota(jnp.int32, (LANES, LANES), 1) // CHANNELS
    return jnp.where(rows == columns, F32(value), F32(0.0)).astype(BF16)


def head_of_lane(rows):
    return lax.broadcasted_iota(jnp.int32, (rows, LANES), 1) // CHANNELS


def own_blocks(stacked, rows):
    lane_head = head_of_lane(rows)
    picked = stacked[:rows]
    for head in range(1, HEADS):
        picked = jnp.where(lane_head == head, stacked[head * rows : (head + 1) * rows], picked)
    return picked


def cumulate(decay):
    length = decay.shape[0]
    rows = lax.broadcasted_iota(jnp.int32, (length, length), 0)
    columns = lax.broadcasted_iota(jnp.int32, (length, length), 1)
    lower = jnp.where(rows >= columns, F32(1.0), F32(0.0)).astype(BF16)
    return dot(lower, decay)


def ends_of(key, value, decay):
    length = decay.shape[0]
    cumul = cumulate(decay)
    final = cumul[length - 1 : length]
    high, low = split(key.astype(F32) * jnp.exp(final - cumul))
    turned = value.astype(F32).T.astype(BF16)
    wide = dot(
        jnp.concatenate([turned, turned], axis=1), jnp.concatenate([high, low], axis=0)
    )
    return own_blocks(wide, CHANNELS), jnp.broadcast_to(jnp.exp(final), (8, LANES))


def ends_kernel(k_ref, v_ref, w_ref, mine_ref, theirs_ref):
    groups = mine_ref.shape[0]
    for side, out_ref in ((1, theirs_ref), (0, mine_ref)):
        for group in range(groups):
            at = lanes_at(side, group, groups)
            state, decay = ends_of(k_ref[:, at], v_ref[:, at], w_ref[:, at])
            out_ref[group, :CHANNELS, :] = state
            out_ref[group, CHANNELS:, :] = decay


def lanes_at(side, group, groups):
    core = lax.axis_index("head")
    core = core if side == 0 else 1 - core
    return pl.ds(pl.multiple_of((core * groups + group) * LANES, LANES), LANES)


def within_kernel(side, r_ref, k_ref, v_ref, w_ref, table_ref, out_ref):
    groups = out_ref.shape[2] // LANES
    length = w_ref.shape[0]
    lane_head = head_of_lane(BLOCK)
    ones = same_head(1.0)
    share = same_head(1.0 / CHANNELS)
    shape = (HEADS * length, length)
    row = lax.broadcasted_iota(jnp.int32, shape, 0)
    later = row // (HEADS * BLOCK) * BLOCK + row % BLOCK
    strict = later > lax.broadcasted_iota(jnp.int32, shape, 1)
    for group in range(groups):
        at = lanes_at(side, group, groups)
        out = pl.ds(group * LANES, LANES)
        r, k, v, w = r_ref[:, at].astype(F32), k_ref[:, at].astype(F32), v_ref[:, at], w_ref[:, at]
        cumul = cumulate(w)
        before = cumul - w.astype(F32)
        out_ref[1, :, out] = r * jnp.exp(before)
        diagonal_high, diagonal_low = split(r * table_ref[0:1, at] * k)
        diagonal = dot(diagonal_high, ones) + dot(diagonal_low, ones)
        pieces = []
        for start in range(0, length, BLOCK):
            stop = start + BLOCK
            middle = start + BLOCK // 2 - 1
            reference = cumul[middle : middle + 1]
            receptance = r[start:stop] * jnp.exp(before[start:stop] - reference)
            stacked = jnp.concatenate(
                [jnp.where(lane_head == head, receptance, F32(0.0)) for head in range(HEADS)],
                axis=0,
            )
            keys = k[:stop] * jnp.exp(reference - cumul[:stop])
            if stop < length:
                keys = jnp.concatenate([keys, jnp.zeros((length - stop, LANES), F32)], axis=0)
            r_high, r_low = split(stacked)
            k_high, k_low = split(keys)
            pieces.append(dot_nt(r_high, k_high) + dot_nt(r_low, k_high) + dot_nt(r_high, k_low))
        s_high, s_low = split(jnp.where(strict, jnp.concatenate(pieces, axis=0), F32(0.0)))
        wide = dot(jnp.concatenate([s_high, s_low], axis=1), jnp.concatenate([v, v], axis=0))
        step = HEADS * BLOCK
        mixed = jnp.concatenate(
            [own_blocks(wide[i * step : (i + 1) * step], BLOCK) for i in range(length // BLOCK)],
            axis=0,
        )
        mixed = mixed + diagonal * v.astype(F32)
        m_high, m_low = split(mixed)
        out_ref[0, :, out] = mixed - (dot(m_high, share) + dot(m_low, share))


def finish_kernel(
    p0, p1, p2, p3, ends_mine, ends_other, in_mine, in_other, g_mine, g_other, table_ref,
    out_ref, state_ref,
):
    core = lax.axis_index("head")
    place = lax.axis_index("seq") % PLANE
    groups = ends_mine.shape[0]
    rows = CHANNELS // PLANE
    length = in_mine.shape[1]
    first = core == 0
    share = same_head(1.0 / CHANNELS)
    mask = lax.broadcasted_iota(jnp.int32, (LANES, LANES), 0) // CHANNELS == head_of_lane(LANES)
    for step, piece in enumerate((p0, p1, p2, p3)):
        source = lax.bitwise_xor(place, step) * rows
        for group in range(groups):
            at = pl.multiple_of(source + group * CHANNELS, rows)
            state_ref[pl.ds(at, rows), :] = piece[group * rows : (group + 1) * rows, :]
    for group in range(groups):
        at = lanes_at(0, group, groups)
        out = pl.ds(group * LANES, LANES)
        early = jnp.where(first, ends_mine[group], ends_other[group])
        state = state_ref[group * CHANNELS : (group + 1) * CHANNELS, :]
        for half in range(2):
            local = core == half
            if half == 1:
                state = early[CHANNELS : CHANNELS + 1] * state + early[:CHANNELS]
            centred = state - jnp.mean(state, axis=0, keepdims=True)
            wide = jnp.where(mask, jnp.concatenate([centred] * HEADS, axis=0), F32(0.0))
            s_high, s_low = split(wide)
            r_high, r_low = split(jnp.where(local, in_mine[1, :, out], in_other[1, :, out]))
            mixed = jnp.where(local, in_mine[0, :, out], in_other[0, :, out])
            mixed = mixed + (
                dot_nt(r_high, s_high) + dot_nt(r_low, s_high) + dot_nt(r_high, s_low)
            )
            q_high, q_low = split(mixed * mixed)
            spread = dot(q_high, share) + dot(q_low, share)
            normed = mixed * lax.rsqrt(spread + 1e-5)
            gate = jnp.where(local, g_mine[:, at].astype(F32), g_other[:, at].astype(F32))
            gated = (normed * table_ref[1:2, at] + table_ref[2:3, at]) * gate
            gated = gated / (1.0 + jnp.exp(-gate))
            out_ref[half * length : (half + 1) * length, out] = gated.astype(BF16)


def body(r, k, v, w, gate, bonus, gain, bias):
    length, width = r.shape
    cores, count = lax.axis_size("head"), lax.axis_size("seq")
    assert cores == 2 and count % PLANE == 0
    half = width // cores
    groups = half // LANES
    core, position = lax.axis_index("head"), lax.axis_index("seq")
    place = position % PLANE
    swap = [(0, 1), (1, 0)]
    params = pltpu.CompilerParams(vmem_limit_bytes=VMEM_LIMIT)
    table = jnp.stack([bonus.reshape(width), gain, bias])

    ends_shape = jax.ShapeDtypeStruct((groups, CHANNELS + 8, LANES), F32)
    mine, theirs = pl.pallas_call(
        ends_kernel, out_shape=[ends_shape, ends_shape], compiler_params=params, name="ends"
    )(k, v, w)
    other = lax.ppermute(theirs, "head", swap)

    def within(side):
        return pl.pallas_call(
            functools.partial(within_kernel, side),
            out_shape=jax.ShapeDtypeStruct((2, length, half), F32),
            compiler_params=params,
            name="within_other" if side else "within_mine",
        )(r, k, v, w, table)

    in_other = lax.ppermute(within(1), "head", swap)
    in_mine = within(0)
    gate_other = lax.ppermute(gate, "head", swap)

    first = jnp.where(core == 0, mine, other)
    second = jnp.where(core == 0, other, mine)
    chip = first[:, :CHANNELS] * second[:, CHANNELS : CHANNELS + 1] + second[:, :CHANNELS]
    chip_decay = first[:, CHANNELS] * second[:, CHANNELS]
    rows = CHANNELS // PLANE
    quarters = chip.reshape(groups, PLANE, rows, LANES)
    packed_rows = groups * rows

    def pack(state, decay):
        pad = jnp.zeros((-groups % 8, LANES), F32)
        return jnp.concatenate([state.reshape(packed_rows, LANES), decay, pad], axis=0)

    def unpack(packed):
        state = packed[:packed_rows].reshape(groups, rows, LANES)
        return state, packed[packed_rows : packed_rows + groups]

    def to_place(step):
        return [(i, i ^ step) for i in range(count)]

    def quarter(step):
        return pack(
            lax.dynamic_index_in_dim(quarters, place ^ step, 1, keepdims=False), chip_decay
        )

    got = [quarter(0)] + [
        lax.ppermute(quarter(step), "seq", to_place(step)) for step in range(1, PLANE)
    ]

    def choose(options, at):
        picked = options[0]
        for index in range(1, PLANE):
            picked = jnp.where(at == index, options[index], picked)
        return picked

    def join(earlier, later):
        return (later[1][:, None, :] * earlier[0] + later[0], earlier[1] * later[1])

    slabs = [unpack(choose(got, place ^ slab)) for slab in range(PLANE)]
    prefixes = [(jnp.zeros_like(slabs[0][0]), jnp.ones_like(slabs[0][1]))]
    for slab in slabs:
        prefixes.append(join(prefixes[-1], slab))
    window = prefixes.pop()
    before = None
    distance = 1
    while distance < count // PLANE:
        hop = distance * PLANE
        got = unpack(
            lax.ppermute(pack(*window), "seq", [(i, i + hop) for i in range(count - hop)])
        )
        before = got if before is None else join(got, before)
        window = join(got, window)
        distance *= 2
    if before is not None:
        finals = [join(before, prefix)[0] for prefix in prefixes]
    else:
        finals = [prefix[0] for prefix in prefixes]
    finals = [final.reshape(packed_rows, LANES) for final in finals]
    states = [choose(finals, place)] + [
        lax.ppermute(choose(finals, place ^ step), "seq", to_place(step))
        for step in range(1, PLANE)
    ]
    return pl.pallas_call(
        finish_kernel,
        out_shape=jax.ShapeDtypeStruct((cores * length, half), BF16),
        scratch_shapes=[pltpu.VMEM((groups * CHANNELS, LANES), F32)],
        compiler_params=params,
        name="finish",
    )(*states, mine, other, in_mine, in_other, gate, gate_other, table)


def solution(mesh):
    tokens = P(("seq", "head"), None)
    return jax.shard_map(
        body,
        mesh=mesh,
        in_specs=(tokens,) * 5 + (P(), P(), P()),
        out_specs=P("seq", "head"),
        check_vma=False,
    )
```

time: 63.6 us -> 49.5 us (0.78)
  Pallas kernels: 31.8 us -> 16.5 us
    pallas_call x3, Pallas kernels: 23.9 us -> 10.4 us  [the longest x2 8.75 us: within(): pl.pallas_call(functools.partial(within_kernel, side), out_shape=jax.Shap...]
    unnamed x21 -> x23, local copies, waits for them, and re-layouts: 1.3 us -> 3.3 us
    reshape x3 -> x0, local copies, waits for them, and re-layouts: 1.88 us -> none  [the longest x1 0.68 us: within(): bonus.reshape(1, width)]
    pallas_call x1, Pallas kernels: 7.92 us -> 6.13 us  [body(): pl.pallas_call(finish_kernel, out_shape=jax.ShapeDtypeStruct((cores * len...]
    select_n x5, other arithmetic: 1 us -> 2.31 us  [choose(): picked = jnp.where(at == index, options[index], picked)]
    select_n x1, other arithmetic: 1.17 us -> 0.05 us  [body(): second = jnp.where(core == 0, other, mine)]
    ppermute x3, waiting for transfers between devices: 0.01 us -> 1 us  [body(): lax.ppermute(choose(finals, place ^ step), 'seq', to_place(step))]
    concatenate x3, other arithmetic: 0.24 us -> 0.94 us  [pack(): jnp.concatenate([state.reshape(packed_rows, LANES), decay, pad], axis=0)]
  transfers between devices with their start and end apart: 11 -> 11, of which waited for: 3 -> 4; matrix products, arithmetic and copies ran while one was open for 5% -> 6% of each run, Pallas kernels for 28% -> 18%
where the time goes in v2:
time: 49.5 us; the launch traced here: 49.1 us
  Pallas kernels  16.5 us (33%)
  waiting for transfers between devices  14.9 us (30%)
  starting transfers between devices  10.3 us (21%)
  local copies, waits for them, and re-layouts  3.52 us (7%)
  other arithmetic  3.49 us (7%)
    ppermute x2, waiting for transfers between devices, body(): lax.ppermute(pack(*window), 'seq', [(i, i + hop) for i in range(count - h...  12.5 us
    pallas_call x2, Pallas kernels, within(): pl.pallas_call(functools.partial(within_kernel, side), out_shape=jax.Shap...  8.75 us
    pallas_call x1, Pallas kernels, body(): pl.pallas_call(finish_kernel, out_shape=jax.ShapeDtypeStruct((cores * len...  6.13 us
    ppermute x3, starting transfers between devices, body(): lax.ppermute(choose(finals, place ^ step), 'seq', to_place(step))  3.55 us
    ppermute x3, starting transfers between devices, body(): lax.ppermute(quarter(step), 'seq', to_place(step))  3.49 us
    unnamed x23, local copies, waits for them, and re-layouts  3.3 us
    ppermute x2, starting transfers between devices, body(): lax.ppermute(pack(*window), 'seq', [(i, i + hop) for i in range(count - h...  2.58 us
    select_n x5, other arithmetic, choose(): picked = jnp.where(at == index, options[index], picked)  2.31 us
  transfers between devices with their start and end apart: 11, of which 4 were waited for; matrix products, arithmetic and copies ran while one was open for 6% of the time, Pallas kernels for 18%

profile of v2, /device:TPU:24, one launch (start us, length us, event | category | flops | bytes accessed | tf_op | source)
XLA Modules:
  0.0 49.1 jit_solution(5310503512381112379)
XLA Ops:
  0.0 1.1 %copy-done = bf16[128,2560]{1,0:T(8,128)(2,1)S(1)} copy-done((bf16[128,2560]{1,0:T(8,128)(2,1)S(1)}, bf16[128,2560]{1,0:T(8,128)(2,1)}, u32[]{:S(2)}) %copy-start) | copy-done | bytes 655384
  1.1 1.1 %copy-done.2 = bf16[128,2560]{1,0:T(8,128)(2,1)S(1)} copy-done((bf16[128,2560]{1,0:T(8,128)(2,1)S(1)}, bf16[128,2560]{1,0:T(8,128)(2,1)}, u32[]{:S(2)}) %copy-start.2) | copy-done | bytes 655384
  2.2 1.1 %copy-done.4 = bf16[128,2560]{1,0:T(8,128)(2,1)S(1)} copy-done((bf16[128,2560]{1,0:T(8,128)(2,1)S(1)}, bf16[128,2560]{1,0:T(8,128)(2,1)}, u32[]{:S(2)}) %copy-start.4) | copy-done | bytes 655384
  3.3 1.7 %ends.1 = (f32[5,72,256]{2,1,0:T(8,128)S(1)}, f32[5,72,256]{2,1,0:T(8,128)S(1)}) custom-call(bf16[128,2560]{1,0:T(8,128)(2,1)S(1)} %copy-done, bf16[128,2560]{1,0:T(8,128)(2,1)S(1)} %copy-done.2, bf16[128,2560]{1,0:T(8,128)(2,1)S(1)} %copy-done.4), custom_call_target="tpu_custom_call" | custom-call | tf_op jit(solution)/shard_map/ends/pallas_call | solution.py:190
  5.3 1.4 %collective-permute-done.ends_other = f32[5,72,256]{2,1,0:T(8,128)S(1)} collective-permute-done((f32[5,72,256]{2,1,0:T(8,128)S(1)}, f32[5,72,256]{2,1,0:T(8,128)S(1)}, u32[]{:S(2)}, u32[]{:S(2)}) %collective-permute-start) | collective-permute-done | bytes 368672 | tf_op jit(solution)/shard_map/ppermute | solution.py:193
  6.8 0.1 slice_add_fusion
  7.0 0.8 %fusion.2 = (f32[88,256]{1,0:T(8,128)}, f32[88,256]{1,0:T(8,128)}, f32[88,256]{1,0:T(8,128)}) fusion(f32[5,256]{1,0:T(8,128)S(1)} %bitcast_multiply_fusion.6, f32[80,256]{1,0:T(8,128)S(1)} %bitcast.103, f32[88]{0:T(128)S(1)} %pad.20.clone, f32[80,256]{1,0:T(8,128)S(1)} %bitcast.104, f32[80,256]{1,0:T(8,128)S(1)} %bitcast.105), kind=kLoop, calls=%fused_computation.14 | loop fusion | flops 135168 | bytes 521568 | tf_op jit(solution)/shard_map/concatenate | solution.py:217
  7.7 2.4 %collective-permute-start.1 = (f32[88,256]{1,0:T(8,128)}, f32[88,256]{1,0:T(8,128)}, u32[]{:S(2)}, u32[]{:S(2)}) collective-permute-start(f32[88,256]{1,0:T(8,128)} %get-tuple-element.36), channel_id=1, source_target_pairs={{0,6},{2,4},{4,2},{6,0},{8,14},{10,12},{12,10},{14,8},{16,22},{18,... | collective-permute-start | bytes 270344 | tf_op jit(solution)/shard_map/ppermute | solution.py:232
  10.2 0.5 %collective-permute-start.2 = (f32[88,256]{1,0:T(8,128)}, f32[88,256]{1,0:T(8,128)}, u32[]{:S(2)}, u32[]{:S(2)}) collective-permute-start(f32[88,256]{1,0:T(8,128)} %get-tuple-element.35), channel_id=1, source_target_pairs={{0,4},{2,6},{4,0},{6,2},{8,12},{10,14},{12,8},{14,10},{16,20},{18,... | collective-permute-start | bytes 270344 | tf_op jit(solution)/shard_map/ppermute | solution.py:232
  10.7 0.5 %collective-permute-start.3 = (f32[88,256]{1,0:T(8,128)}, f32[88,256]{1,0:T(8,128)}, u32[]{:S(2)}, u32[]{:S(2)}) collective-permute-start(f32[88,256]{1,0:T(8,128)} %get-tuple-element.34), channel_id=1, source_target_pairs={{0,2},{2,0},{4,6},{6,4},{8,10},{10,8},{12,14},{14,12},{16,18},{18,... | collective-permute-start | bytes 270344 | tf_op jit(solution)/shard_map/ppermute | solution.py:232
  11.3 4.9 %within_other.1 = f32[2,128,1280]{2,1,0:T(8,128)} custom-call(bf16[128,2560]{1,0:T(8,128)(2,1)S(1)} %copy-done.6, bf16[128,2560]{1,0:T(8,128)(2,1)S(1)} %copy-done.1, bf16[128,2560]{1,0:T(8,128)(2,1)S(1)} %copy-done.3, bf16[128,2560]{1,0:T(8,128)(2,1)S(1)} %copy-done.5, f32[3,2560]{1,0:T(4,128)S(1)} %pad_maximum_fusion.4.table_ref), custom_call_target="tpu_custom_call" | custom-call | tf_op jit(solution)/shard_map/within_other/pallas_call | solution.py:196
  16.3 1.1 %select_select_fusion.2 = f32[88,256]{1,0:T(8,128)S(1)} fusion(f32[88,256]{1,0:T(8,128)} %collective-permute-done.1, f32[88,256]{1,0:T(8,128)} %collective-permute-done.2, f32[88,256]{1,0:T(8,128)} %collective-permute-done.3, pred[]{:T(512)S(6)} %eq.60, pred[]{:T(512)S(6)} %eq.59, pred[]{:T(512)S(6)} %eq.58, f32[88]{0:T(128)S(1)} %pad.20.clone, ...), kind=kLoop, calls=%fused_computation.20 | loop fusion | flops 112640 | bytes 447843 | tf_op jit(solution)/shard_map/jit(_where)/select_n | solution.py:238
  17.3 1.1 %select_select_fusion.3 = (f32[88,256]{1,0:T(8,128)S(1)}, f32[88,256]{1,0:T(8,128)S(1)}, f32[88,256]{1,0:T(8,128)S(1)}) fusion(f32[88,256]{1,0:T(8,128)} %collective-permute-done.1, f32[88,256]{1,0:T(8,128)} %collective-permute-done.2, f32[88,256]{1,0:T(8,128)} %collective-permute-done.3, pred[]{:T(512)S(6)} %eq.57, pred[]{:T(512)S(6)} %eq.56, pred[]{:T(512)S(6)} %eq.54, ...), kind=kLoop, calls=%fused_computation.21 | loop fusion | flops 247808 | bytes 628073 | tf_op jit(solution)/shard_map/jit(_where)/select_n | solution.py:238
  18.6 1.3 %collective-permute-start.4 = (f32[88,256]{1,0:T(8,128)S(1)}, f32[88,256]{1,0:T(8,128)S(1)}, u32[]{:S(2)}, u32[]{:S(2)}) collective-permute-start(f32[88,256]{1,0:T(8,128)S(1)} %maximum_maximum_fusion), channel_id=1, source_target_pairs={{0,8},{2,10},{4,12},{6,14},{8,16},{10,18},{12,20},{14,22},{16,24},... | collective-permute-start | bytes 270344 | tf_op jit(solution)/shard_map/ppermute | solution.py:254
  19.9 0.6 %collective-permute-start.10 = (bf16[128,2560]{1,0:T(8,128)(2,1)S(1)}, bf16[128,2560]{1,0:T(8,128)(2,1)S(1)}, u32[]{:S(2)}, u32[]{:S(2)}) collective-permute-start(bf16[128,2560]{1,0:T(8,128)(2,1)S(1)} %copy-done.7), channel_id=1, source_target_pairs={{0,1},{1,0},{2,3},{3,2},{4,5},{5,4},{6,7},{7,6},{8,9},{9,8},{10,11... | collective-permute-start | bytes 1966088 | tf_op jit(solution)/shard_map/ppermute | solution.py:205
  20.4 5.0 %collective-permute-done.4 = f32[88,256]{1,0:T(8,128)S(1)} collective-permute-done((f32[88,256]{1,0:T(8,128)S(1)}, f32[88,256]{1,0:T(8,128)S(1)}, u32[]{:S(2)}, u32[]{:S(2)}) %collective-permute-start.4) | collective-permute-done | bytes 90144 | tf_op jit(solution)/shard_map/ppermute | solution.py:254
  25.6 1.3 %collective-permute-start.5 = (f32[88,256]{1,0:T(8,128)S(1)}, f32[88,256]{1,0:T(8,128)S(1)}, u32[]{:S(2)}, u32[]{:S(2)}) collective-permute-start(f32[88,256]{1,0:T(8,128)S(1)} %maximum_maximum_fusion.1), channel_id=1, source_target_pairs={{0,16},{2,18},{4,20},{6,22},{8,24},{10,26},{12,28},{14,30},{1,17},... | collective-permute-start | bytes 270344 | tf_op jit(solution)/shard_map/ppermute | solution.py:254
  26.9 7.5 %collective-permute-done.5 = f32[88,256]{1,0:T(8,128)S(1)} collective-permute-done((f32[88,256]{1,0:T(8,128)S(1)}, f32[88,256]{1,0:T(8,128)S(1)}, u32[]{:S(2)}, u32[]{:S(2)}) %collective-permute-start.5) | collective-permute-done | bytes 90144 | tf_op jit(solution)/shard_map/ppermute | solution.py:254
  34.5 0.7 %collective-permute-start.6 = (f32[80,256]{1,0:T(8,128)S(1)}, f32[80,256]{1,0:T(8,128)S(1)}, u32[]{:S(2)}, u32[]{:S(2)}) collective-permute-start(f32[80,256]{1,0:T(8,128)S(1)} %fusion.7), channel_id=1, source_target_pairs={{0,2},{2,0},{4,6},{6,4},{8,10},{10,8},{12,14},{14,12},{16,18},{18,... | collective-permute-start | bytes 245768 | tf_op jit(solution)/shard_map/ppermute | solution.py:265
  35.2 2.4 %collective-permute-start.7 = (f32[80,256]{1,0:T(8,128)S(1)}, f32[80,256]{1,0:T(8,128)S(1)}, u32[]{:S(2)}, u32[]{:S(2)}) collective-permute-start(f32[80,256]{1,0:T(8,128)S(1)} %get-tuple-element.17), channel_id=1, source_target_pairs={{0,4},{2,6},{4,0},{6,2},{8,12},{10,14},{12,8},{14,10},{16,20},{18,... | collective-permute-start | bytes 245768 | tf_op jit(solution)/shard_map/ppermute | solution.py:265
  37.6 0.5 collective-permute-start.8
  38.1 3.8 %within_mine.1.in_mine = f32[2,128,1280]{2,1,0:T(8,128)S(1)} custom-call(bf16[128,2560]{1,0:T(8,128)(2,1)S(1)} %copy-done.6, bf16[128,2560]{1,0:T(8,128)(2,1)S(1)} %copy-done.1, bf16[128,2560]{1,0:T(8,128)(2,1)S(1)} %copy-done.3, bf16[128,2560]{1,0:T(8,128)(2,1)S(1)} %copy-done.5, f32[3,2560]{1,0:T(4,128)S(1)} %pad_maximum_fusion.4.table_ref), custom_call_target="tpu_custom_call" | custom-call | tf_op jit(solution)/shard_map/within_mine/pallas_call | solution.py:196
  42.0 1.0 %collective-permute-done.8.p3 = f32[80,256]{1,0:T(8,128)S(1)} collective-permute-done((f32[80,256]{1,0:T(8,128)S(1)}, f32[80,256]{1,0:T(8,128)S(1)}, u32[]{:S(2)}, u32[]{:S(2)}) %collective-permute-start.8) | collective-permute-done | bytes 81952 | tf_op jit(solution)/shard_map/ppermute | solution.py:265
  43.0 6.1 %finish.1 = bf16[256,1280]{1,0:T(8,128)(2,1)} custom-call(f32[80,256]{1,0:T(8,128)S(1)} %get-tuple-element.18.p0, f32[80,256]{1,0:T(8,128)S(1)} %collective-permute-done.6.p1, f32[80,256]{1,0:T(8,128)S(1)} %collective-permute-done.7.p2, f32[80,256]{1,0:T(8,128)S(1)} %collective-permute-done.8.p3, f32[5,72,256]{2,1,0:T(8,128)S(1)} %get-tuple-element.7.ends_mine, ...), custom_call_target="tpu_custom_call" | custom-call | tf_op jit(solution)/shard_map/finish/pallas_call | solution.py:268
  (50 shorter events, 0.8 us)
Async XLA Ops:
  0.0 1.1 %copy-start = (bf16[128,2560]{1,0:T(8,128)(2,1)S(1)}, bf16[128,2560]{1,0:T(8,128)(2,1)}, u32[]{:S(2)}) copy-start(bf16[128,2560]{1,0:T(8,128)(2,1)} %k_ref.5) | copy-start | bytes 1966084
  1.1 1.1 %copy-start.2 = (bf16[128,2560]{1,0:T(8,128)(2,1)S(1)}, bf16[128,2560]{1,0:T(8,128)(2,1)}, u32[]{:S(2)}) copy-start(bf16[128,2560]{1,0:T(8,128)(2,1)} %v_ref.5) | copy-start | bytes 1966084
  2.2 1.1 %copy-start.4 = (bf16[128,2560]{1,0:T(8,128)(2,1)S(1)}, bf16[128,2560]{1,0:T(8,128)(2,1)}, u32[]{:S(2)}) copy-start(bf16[128,2560]{1,0:T(8,128)(2,1)} %w_ref.5) | copy-start | bytes 1966084
  3.3 1.8 %copy-start.9 = (f32[2560]{0:T(1024)S(1)}, f32[2560]{0:T(1024)}, u32[]{:S(2)}) copy-start(f32[2560]{0:T(1024)} %param.15) | copy-start | bytes 30724
  3.3 1.8 %copy-start.10 = (f32[2560]{0:T(1024)S(1)}, f32[2560]{0:T(1024)}, u32[]{:S(2)}) copy-start(f32[2560]{0:T(1024)} %param.14) | copy-start | bytes 30724
  3.3 1.8 %copy-start.8 = (f32[40,64]{1,0:T(8,128)S(1)}, f32[40,64]{1,0:T(8,128)}, u32[]{:S(2)}) copy-start(f32[40,64]{1,0:T(8,128)} %param.13) | copy-start | bytes 30724
  4.9 1.8 %collective-permute-start = (f32[5,72,256]{2,1,0:T(8,128)S(1)}, f32[5,72,256]{2,1,0:T(8,128)S(1)}, u32[]{:S(2)}, u32[]{:S(2)}) collective-permute-start(f32[5,72,256]{2,1,0:T(8,128)S(1)} %get-tuple-element.8), channel_id=1, source_target_pairs={{0,1},{1,0},{2,3},{3,2},{4,5},{5,4},{6,7},{7,6},{8,9},{9,8},{10,11... | collective-permute-start | bytes 1105928 | tf_op jit(solution)/shard_map/ppermute | solution.py:193
  6.7 4.6 %copy-start.6 = (bf16[128,2560]{1,0:T(8,128)(2,1)S(1)}, bf16[128,2560]{1,0:T(8,128)(2,1)}, u32[]{:S(2)}) copy-start(bf16[128,2560]{1,0:T(8,128)(2,1)} %r_ref.3) | copy-start | bytes 1966084
  6.8 4.5 %copy-start.1 = (bf16[128,2560]{1,0:T(8,128)(2,1)S(1)}, bf16[128,2560]{1,0:T(8,128)(2,1)}, u32[]{:S(2)}) copy-start(bf16[128,2560]{1,0:T(8,128)(2,1)} %k_ref.5) | copy-start | bytes 1966084
  6.8 4.5 %copy-start.3 = (bf16[128,2560]{1,0:T(8,128)(2,1)S(1)}, bf16[128,2560]{1,0:T(8,128)(2,1)}, u32[]{:S(2)}) copy-start(bf16[128,2560]{1,0:T(8,128)(2,1)} %v_ref.5) | copy-start | bytes 1966084
  6.8 4.5 %copy-start.5 = (bf16[128,2560]{1,0:T(8,128)(2,1)S(1)}, bf16[128,2560]{1,0:T(8,128)(2,1)}, u32[]{:S(2)}) copy-start(bf16[128,2560]{1,0:T(8,128)(2,1)} %w_ref.5) | copy-start | bytes 1966084
  7.7 8.5 %collective-permute-start.1 = (f32[88,256]{1,0:T(8,128)}, f32[88,256]{1,0:T(8,128)}, u32[]{:S(2)}, u32[]{:S(2)}) collective-permute-start(f32[88,256]{1,0:T(8,128)} %get-tuple-element.36), channel_id=1, source_target_pairs={{0,6},{2,4},{4,2},{6,0},{8,14},{10,12},{12,10},{14,8},{16,22},{18,... | collective-permute-start | bytes 270344 | tf_op jit(solution)/shard_map/ppermute | solution.py:232
  10.2 6.1 %collective-permute-start.2 = (f32[88,256]{1,0:T(8,128)}, f32[88,256]{1,0:T(8,128)}, u32[]{:S(2)}, u32[]{:S(2)}) collective-permute-start(f32[88,256]{1,0:T(8,128)} %get-tuple-element.35), channel_id=1, source_target_pairs={{0,4},{2,6},{4,0},{6,2},{8,12},{10,14},{12,8},{14,10},{16,20},{18,... | collective-permute-start | bytes 270344 | tf_op jit(solution)/shard_map/ppermute | solution.py:232
  10.7 5.6 %collective-permute-start.3 = (f32[88,256]{1,0:T(8,128)}, f32[88,256]{1,0:T(8,128)}, u32[]{:S(2)}, u32[]{:S(2)}) collective-permute-start(f32[88,256]{1,0:T(8,128)} %get-tuple-element.34), channel_id=1, source_target_pairs={{0,2},{2,0},{4,6},{6,4},{8,10},{10,8},{12,14},{14,12},{16,18},{18,... | collective-permute-start | bytes 270344 | tf_op jit(solution)/shard_map/ppermute | solution.py:232
  16.2 26.7 %collective-permute-start.9 = (f32[2,128,1280]{2,1,0:T(8,128)}, f32[2,128,1280]{2,1,0:T(8,128)}, u32[]{:S(2)}, u32[]{:S(2)}) collective-permute-start(f32[2,128,1280]{2,1,0:T(8,128)} %within_other.1), channel_id=1, source_target_pairs={{0,1},{1,0},{2,3},{3,2},{4,5},{5,4},{6,7},{7,6},{8,9},{9,8},{10,11... | collective-permute-start | bytes 3932168 | tf_op jit(solution)/shard_map/ppermute | solution.py:203
  16.2 3.6 %copy-start.7 = (bf16[128,2560]{1,0:T(8,128)(2,1)S(1)}, bf16[128,2560]{1,0:T(8,128)(2,1)}, u32[]{:S(2)}) copy-start(bf16[128,2560]{1,0:T(8,128)(2,1)} %g_mine.1) | copy-start | bytes 1966084
  18.6 6.9 %collective-permute-start.4 = (f32[88,256]{1,0:T(8,128)S(1)}, f32[88,256]{1,0:T(8,128)S(1)}, u32[]{:S(2)}, u32[]{:S(2)}) collective-permute-start(f32[88,256]{1,0:T(8,128)S(1)} %maximum_maximum_fusion), channel_id=1, source_target_pairs={{0,8},{2,10},{4,12},{6,14},{8,16},{10,18},{12,20},{14,22},{16,24},... | collective-permute-start | bytes 270344 | tf_op jit(solution)/shard_map/ppermute | solution.py:254
  19.9 22.1 %collective-permute-start.10 = (bf16[128,2560]{1,0:T(8,128)(2,1)S(1)}, bf16[128,2560]{1,0:T(8,128)(2,1)S(1)}, u32[]{:S(2)}, u32[]{:S(2)}) collective-permute-start(bf16[128,2560]{1,0:T(8,128)(2,1)S(1)} %copy-done.7), channel_id=1, source_target_pairs={{0,1},{1,0},{2,3},{3,2},{4,5},{5,4},{6,7},{7,6},{8,9},{9,8},{10,11... | collective-permute-start | bytes 1966088 | tf_op jit(solution)/shard_map/ppermute | solution.py:205
  25.6 8.8 %collective-permute-start.5 = (f32[88,256]{1,0:T(8,128)S(1)}, f32[88,256]{1,0:T(8,128)S(1)}, u32[]{:S(2)}, u32[]{:S(2)}) collective-permute-start(f32[88,256]{1,0:T(8,128)S(1)} %maximum_maximum_fusion.1), channel_id=1, source_target_pairs={{0,16},{2,18},{4,20},{6,22},{8,24},{10,26},{12,28},{14,30},{1,17},... | collective-permute-start | bytes 270344 | tf_op jit(solution)/shard_map/ppermute | solution.py:254
  34.5 7.4 %collective-permute-start.6 = (f32[80,256]{1,0:T(8,128)S(1)}, f32[80,256]{1,0:T(8,128)S(1)}, u32[]{:S(2)}, u32[]{:S(2)}) collective-permute-start(f32[80,256]{1,0:T(8,128)S(1)} %fusion.7), channel_id=1, source_target_pairs={{0,2},{2,0},{4,6},{6,4},{8,10},{10,8},{12,14},{14,12},{16,18},{18,... | collective-permute-start | bytes 245768 | tf_op jit(solution)/shard_map/ppermute | solution.py:265
  35.2 6.7 %collective-permute-start.7 = (f32[80,256]{1,0:T(8,128)S(1)}, f32[80,256]{1,0:T(8,128)S(1)}, u32[]{:S(2)}, u32[]{:S(2)}) collective-permute-start(f32[80,256]{1,0:T(8,128)S(1)} %get-tuple-element.17), channel_id=1, source_target_pairs={{0,4},{2,6},{4,0},{6,2},{8,12},{10,14},{12,8},{14,10},{16,20},{18,... | collective-permute-start | bytes 245768 | tf_op jit(solution)/shard_map/ppermute | solution.py:265
  37.6 5.3 %collective-permute-start.8 = (f32[80,256]{1,0:T(8,128)S(1)}, f32[80,256]{1,0:T(8,128)S(1)}, u32[]{:S(2)}, u32[]{:S(2)}) collective-permute-start(f32[80,256]{1,0:T(8,128)S(1)} %get-tuple-element.9), channel_id=1, source_target_pairs={{0,6},{2,4},{4,2},{6,0},{8,14},{10,12},{12,10},{14,8},{16,22},{18,... | collective-permute-start | bytes 245768 | tf_op jit(solution)/shard_map/ppermute | solution.py:265

commit v3 on v2

v3 whole, which is shorter than its diff:
```python
import functools

import jax
import jax.numpy as jnp
from jax import lax
from jax.experimental import pallas as pl
from jax.experimental.pallas import tpu as pltpu
from jax.sharding import PartitionSpec as P


CHANNELS = 64
TILE = 128
LANES = 256
HEADS = LANES // CHANNELS
BLOCK = 64
PLANE = 4
ROWS = CHANNELS // PLANE
VMEM_LIMIT = 12 * 2**20
F32 = jnp.float32
BF16 = jnp.bfloat16


def split(value):
    high = value.astype(BF16)
    return high, (value - high.astype(F32)).astype(BF16)


def dot(left, right):
    return lax.dot_general(left, right, (((1,), (0,)), ((), ())), preferred_element_type=F32)


def dot_nt(left, right):
    return lax.dot_general(left, right, (((1,), (1,)), ((), ())), preferred_element_type=F32)


def same_head(value):
    rows = lax.broadcasted_iota(jnp.int32, (LANES, LANES), 0) // CHANNELS
    columns = lax.broadcasted_iota(jnp.int32, (LANES, LANES), 1) // CHANNELS
    return jnp.where(rows == columns, F32(value), F32(0.0)).astype(BF16)


def half_masks(rows):
    left = lax.broadcasted_iota(jnp.int32, (rows, TILE), 1) < CHANNELS
    one, zero = F32(1.0), F32(0.0)
    return jnp.where(left, one, zero).astype(BF16), jnp.where(left, zero, one).astype(BF16)


def spread_heads(value, masks):
    zero = jnp.zeros((value.shape[0], TILE), value.dtype)
    pieces = []
    for head in range(HEADS):
        tile = head // 2
        kept = value[:, tile * TILE : (tile + 1) * TILE] * masks[head % 2]
        pieces.append(
            jnp.concatenate([kept if i == tile else zero for i in range(LANES // TILE)], axis=1)
        )
    return jnp.concatenate(pieces, axis=0)


def own_blocks(stacked, rows):
    left = lax.broadcasted_iota(jnp.int32, (rows, TILE), 1) < CHANNELS
    pieces = []
    for tile in range(LANES // TILE):
        part = stacked[:, tile * TILE : (tile + 1) * TILE]
        head = 2 * tile
        pieces.append(
            jnp.where(
                left,
                part[head * rows : (head + 1) * rows],
                part[(head + 1) * rows : (head + 2) * rows],
            )
        )
    return jnp.concatenate(pieces, axis=1)


def cumulate(decay):
    length = decay.shape[0]
    rows = lax.broadcasted_iota(jnp.int32, (length, length), 0)
    columns = lax.broadcasted_iota(jnp.int32, (length, length), 1)
    lower = jnp.where(rows >= columns, F32(1.0), F32(0.0)).astype(BF16)
    return dot(lower, decay)


def lanes_at(side, group, groups):
    core = lax.axis_index("head")
    core = core if side == 0 else 1 - core
    return pl.ds(pl.multiple_of((core * groups + group) * LANES, LANES), LANES)


def half_at(side, half):
    core = lax.axis_index("head")
    core = core if side == 0 else 1 - core
    return pl.ds(pl.multiple_of(core * half, LANES), half)


def ends_of(key, value, decay):
    length = decay.shape[0]
    cumul = cumulate(decay)
    final = cumul[length - 1 : length]
    high, low = split(key.astype(F32) * jnp.exp(final - cumul))
    turned = value.astype(F32).T.astype(BF16)
    wide = dot(
        jnp.concatenate([turned, turned], axis=1), jnp.concatenate([high, low], axis=0)
    )
    return own_blocks(wide, CHANNELS), jnp.broadcast_to(jnp.exp(final), (8, LANES))


def ends_kernel(k_ref, v_ref, w_ref, mine_ref, theirs_ref, k_buf, v_buf, w_buf, sems):
    groups = mine_ref.shape[0]
    half = groups * LANES
    copies = {}
    for side in (1, 0):
        at = half_at(side, half)
        for index, (ref, buf) in enumerate(((w_ref, w_buf), (k_ref, k_buf), (v_ref, v_buf))):
            copies[side, index] = pltpu.make_async_copy(
                ref.at[:, at], buf.at[side], sems.at[side, index]
            )
            copies[side, index].start()
    for side, out_ref in ((1, theirs_ref), (0, mine_ref)):
        for index in range(3):
            copies[side, index].wait()
        for group in range(groups):
            at = pl.ds(group * LANES, LANES)
            state, decay = ends_of(k_buf[side, :, at], v_buf[side, :, at], w_buf[side, :, at])
            out_ref[group, :CHANNELS, :] = state
            out_ref[group, CHANNELS:, :] = decay


def combine_kernel(mine_ref, other_ref, q0, q1, q2, q3, state_ref):
    core = lax.axis_index("head")
    place = lax.axis_index("seq") % PLANE
    groups = mine_ref.shape[0]
    first = core == 0
    outs = (q0, q1, q2, q3)
    for out in outs:
        out[...] = jnp.zeros_like(out)
    for group in range(groups):
        mine, other = mine_ref[group], other_ref[group]
        early, late = jnp.where(first, mine, other), jnp.where(first, other, mine)
        decay = late[CHANNELS : CHANNELS + 1]
        state_ref[...] = early[:CHANNELS] * decay + late[:CHANNELS]
        both = early[CHANNELS : CHANNELS + 1] * decay
        for step, out in enumerate(outs):
            at = pl.multiple_of(lax.bitwise_xor(place, step) * ROWS, ROWS)
            out[group * ROWS : (group + 1) * ROWS, :] = state_ref[pl.ds(at, ROWS), :]
            at = groups * ROWS + group
            out[at : at + 1, :] = both


def plane_kernel(q0, q1, q2, q3, total_ref, prefix_ref, slab_ref):
    place = lax.axis_index("seq") % PLANE
    groups = total_ref.shape[0] // ROWS
    for step, piece in enumerate((q0, q1, q2, q3)):
        slab_ref[lax.bitwise_xor(place, step)] = piece[...]
    total_ref[...] = jnp.zeros_like(total_ref)
    for group in range(groups):
        rows = slice(group * ROWS, (group + 1) * ROWS)
        at = groups * ROWS + group
        row = slice(at, at + 1)
        state = jnp.zeros((ROWS, LANES), F32)
        decay = jnp.ones((1, LANES), F32)
        for slab in range(PLANE):
            prefix_ref[slab, rows, :] = state
            prefix_ref[slab, row, :] = decay
            step = slab_ref[slab, row, :]
            state = step * state + slab_ref[slab, rows, :]
            decay = step * decay
        total_ref[rows, :] = state
        total_ref[row, :] = decay


def round_kernel(bit, first_round, total_ref, got_ref, before_ref, total_out, before_out):
    plane = lax.axis_index("seq") // PLANE
    upper = lax.bitwise_and(plane, bit) != 0
    groups = total_ref.shape[0] // ROWS
    total_out[...] = jnp.zeros_like(total_out)
    before_out[...] = jnp.zeros_like(before_out)
    for group in range(groups):
        rows = slice(group * ROWS, (group + 1) * ROWS)
        at = groups * ROWS + group
        row = slice(at, at + 1)
        total, got = total_ref[rows, :], got_ref[rows, :]
        total_decay, got_decay = total_ref[row, :], got_ref[row, :]
        low, high = jnp.where(upper, got, total), jnp.where(upper, total, got)
        total_out[rows, :] = jnp.where(upper, total_decay, got_decay) * low + high
        total_out[row, :] = total_decay * got_decay
        if first_round:
            before = jnp.where(upper, got, F32(0.0))
            before_decay = jnp.where(upper, got_decay, F32(1.0))
        else:
            decay = before_ref[row, :]
            before = before_ref[rows, :]
            before = jnp.where(upper, decay * got + before, before)
            before_decay = jnp.where(upper, got_decay * decay, decay)
        before_out[rows, :] = before
        before_out[row, :] = before_decay


def back_kernel(bit, prefix_ref, before_ref, got_ref, p0, p1, p2, p3):
    seq = lax.axis_index("seq")
    place = seq % PLANE
    upper = lax.bitwise_and(seq // PLANE, bit) != 0
    groups = p0.shape[0] // ROWS
    for group in range(groups):
        rows = slice(group * ROWS, (group + 1) * ROWS)
        at = groups * ROWS + group
        row = slice(at, at + 1)
        before = before_ref[rows, :]
        before = jnp.where(upper, before_ref[row, :] * got_ref[rows, :] + before, before)
        for step, out in enumerate((p0, p1, p2, p3)):
            to = lax.bitwise_xor(place, step)
            out[rows, :] = prefix_ref[to, row, :] * before + prefix_ref[to, rows, :]


def within_kernel(side, r_ref, k_ref, v_ref, w_ref, g_ref, table_ref, out_ref):
    groups = out_ref.shape[2] // LANES
    length = w_ref.shape[0]
    ones = same_head(1.0)
    share = same_head(1.0 / CHANNELS)
    masks = half_masks(BLOCK)
    shape = (HEADS * length, length)
    row = lax.broadcasted_iota(jnp.int32, shape, 0)
    later = row // (HEADS * BLOCK) * BLOCK + row % BLOCK
    strict = later > lax.broadcasted_iota(jnp.int32, shape, 1)
    for group in range(groups):
        at = lanes_at(side, group, groups)
        out = pl.ds(group * LANES, LANES)
        r, k, v, w = r_ref[:, at].astype(F32), k_ref[:, at].astype(F32), v_ref[:, at], w_ref[:, at]
        gate = g_ref[:, at].astype(F32)
        out_ref[2, :, out] = gate / (1.0 + jnp.exp(-gate))
        cumul = cumulate(w)
        before = cumul - w.astype(F32)
        out_ref[1, :, out] = r * jnp.exp(before)
        diagonal_high, diagonal_low = split(r * table_ref[0:1, at] * k)
        diagonal = dot(diagonal_high, ones) + dot(diagonal_low, ones)
        pieces = []
        for start in range(0, length, BLOCK):
            stop = start + BLOCK
            middle = start + BLOCK // 2 - 1
            reference = cumul[middle : middle + 1]
            r_high, r_low = split(r[start:stop] * jnp.exp(before[start:stop] - reference))
            k_high, k_low = split(k[:stop] * jnp.exp(reference - cumul[:stop]))
            if stop < length:
                rest = jnp.zeros((length - stop, LANES), BF16)
                k_high = jnp.concatenate([k_high, rest], axis=0)
                k_low = jnp.concatenate([k_low, rest], axis=0)
            r_high, r_low = spread_heads(r_high, masks), spread_heads(r_low, masks)
            pieces.append(dot_nt(r_high, k_high) + dot_nt(r_low, k_high) + dot_nt(r_high, k_low))
        s_high, s_low = split(jnp.where(strict, jnp.concatenate(pieces, axis=0), F32(0.0)))
        wide = dot(jnp.concatenate([s_high, s_low], axis=1), jnp.concatenate([v, v], axis=0))
        step = HEADS * BLOCK
        mixed = jnp.concatenate(
            [own_blocks(wide[i * step : (i + 1) * step], BLOCK) for i in range(length // BLOCK)],
            axis=0,
        )
        mixed = mixed + diagonal * v.astype(F32)
        m_high, m_low = split(mixed)
        out_ref[0, :, out] = mixed - (dot(m_high, share) + dot(m_low, share))


def finish_kernel(
    p0, p1, p2, p3, ends_mine, ends_other, in_mine, in_other, table_ref, out_ref,
    state_ref, buf, sems,
):
    core = lax.axis_index("head")
    place = lax.axis_index("seq") % PLANE
    groups = ends_mine.shape[0]
    length = in_mine.shape[1]
    first = core == 0
    share = same_head(1.0 / CHANNELS)
    masks = half_masks(CHANNELS)
    for step, piece in enumerate((p0, p1, p2, p3)):
        source = lax.bitwise_xor(place, step) * ROWS
        for group in range(groups):
            at = pl.multiple_of(source + group * CHANNELS, ROWS)
            state_ref[pl.ds(at, ROWS), :] = piece[group * ROWS : (group + 1) * ROWS, :]
    copies = []
    for group in range(groups):
        at = lanes_at(0, group, groups)
        out = pl.ds(group * LANES, LANES)
        early = jnp.where(first, ends_mine[group], ends_other[group])
        state = state_ref[group * CHANNELS : (group + 1) * CHANNELS, :]
        for half in range(2):
            local = core == half
            if half == 1:
                state = early[CHANNELS : CHANNELS + 1] * state + early[:CHANNELS]
            s_high, s_low = split(state - jnp.mean(state, axis=0, keepdims=True))
            s_high, s_low = spread_heads(s_high, masks), spread_heads(s_low, masks)
            r_high, r_low = split(jnp.where(local, in_mine[1, :, out], in_other[1, :, out]))
            mixed = jnp.where(local, in_mine[0, :, out], in_other[0, :, out])
            mixed = mixed + (
                dot_nt(r_high, s_high) + dot_nt(r_low, s_high) + dot_nt(r_high, s_low)
            )
            q_high, q_low = split(mixed * mixed)
            spread = dot(q_high, share) + dot(q_low, share)
            normed = mixed * lax.rsqrt(spread + 1e-5)
            gate = jnp.where(local, in_mine[2, :, out], in_other[2, :, out])
            gated = (normed * table_ref[1:2, at] + table_ref[2:3, at]) * gate
            buf[half * length : (half + 1) * length, out] = gated.astype(BF16)
        copies.append(
            pltpu.make_async_copy(buf.at[:, out], out_ref.at[:, out], sems.at[group])
        )
        copies[-1].start()
    for copy in copies:
        copy.wait()


def program(r, k, v, w, gate, bonus, gain, bias):
    length, width = r.shape
    cores, count = lax.axis_size("head"), lax.axis_size("seq")
    planes = count // PLANE
    assert cores == 2 and count == planes * PLANE
    assert planes > 1 and planes & (planes - 1) == 0
    half = width // cores
    groups = half // LANES
    swap = [(0, 1), (1, 0)]
    hbm = pl.BlockSpec(memory_space=pltpu.HBM)
    table = jnp.stack([bonus.reshape(width), gain, bias])

    def call(kernel, outs, **options):
        return pl.pallas_call(
            kernel,
            out_shape=outs,
            compiler_params=pltpu.CompilerParams(vmem_limit_bytes=VMEM_LIMIT),
            **options,
        )

    ends_shape = jax.ShapeDtypeStruct((groups, CHANNELS + 8, LANES), F32)
    packed = jax.ShapeDtypeStruct((groups * ROWS + -(-groups // 8) * 8, LANES), F32)
    piece = jax.ShapeDtypeStruct((groups * ROWS, LANES), F32)
    half_buffer = pltpu.VMEM((cores, length, half), BF16)
    mine, theirs = call(
        ends_kernel,
        [ends_shape] * 2,
        in_specs=[hbm] * 3,
        scratch_shapes=[half_buffer] * 3 + [pltpu.SemaphoreType.DMA((cores, 3))],
    )(*(pltpu.with_memory_space_constraint(x, pltpu.HBM) for x in (k, v, w)))
    other = lax.ppermute(theirs, "head", swap)

    def within(side):
        return call(
            functools.partial(within_kernel, side), jax.ShapeDtypeStruct((3, length, half), F32)
        )(r, k, v, w, gate, table)

    def to_places(pieces):
        return [pieces[0]] + [
            lax.ppermute(pieces[step], "seq", [(i, i ^ step) for i in range(count)])
            for step in range(1, PLANE)
        ]

    def mirror(value, bit):
        flip = (2 * bit - 1) * PLANE
        return lax.ppermute(value, "seq", [(i, i ^ flip) for i in range(count)])

    quarters = call(
        combine_kernel, [packed] * PLANE, scratch_shapes=[pltpu.VMEM((CHANNELS, LANES), F32)]
    )(mine, other)
    in_other = lax.ppermute(within(1), "head", swap)
    total, prefix = call(
        plane_kernel,
        [packed, jax.ShapeDtypeStruct((PLANE,) + packed.shape, F32)],
        scratch_shapes=[pltpu.VMEM((PLANE,) + packed.shape, F32)],
    )(*to_places(quarters))
    in_mine = within(0)
    before = total
    bit = 1
    while 2 * bit < planes:
        total, before = call(
            functools.partial(round_kernel, bit, bit == 1), [packed] * 2
        )(total, mirror(total, bit), before)
        bit *= 2
    states = call(functools.partial(back_kernel, bit), [piece] * PLANE)(
        prefix, before, mirror(total, bit)
    )
    return call(
        finish_kernel,
        jax.ShapeDtypeStruct((cores * length, half), BF16),
        out_specs=hbm,
        scratch_shapes=[
            pltpu.VMEM((groups * CHANNELS, LANES), F32),
            pltpu.VMEM((cores * length, half), BF16),
            pltpu.SemaphoreType.DMA((groups,)),
        ],
    )(*to_places(states), mine, other, in_mine, in_other, table)


def solution(mesh):
    tokens = P(("seq", "head"), None)
    return jax.shard_map(
        program,
        mesh=mesh,
        in_specs=(tokens,) * 5 + (P(), P(), P()),
        out_specs=P("seq", "head"),
        check_vma=False,
    )
```

time: 49.5 us -> 50.7 us (1.024)
  the two profiles are of different devices: /device:TPU:24 before, /device:TPU:0 now
where the time goes in v3:
time: 50.7 us; the launch traced here: 50.2 us
  Pallas kernels  15.8 us (31%)
  starting transfers between devices  13.8 us (27%)
  waiting for transfers between devices  12.7 us (25%)
  local copies, waits for them, and re-layouts  7.68 us (15%)
    pallas_call x2, Pallas kernels, within(): call(functools.partial(within_kernel, side), jax.ShapeDtypeStruct((3, len...  7.77 us
    ppermute x6, starting transfers between devices, to_places(): lax.ppermute(pieces[step], 'seq', [(i, i ^ step) for i in range(count)])  7.77 us
    ppermute x2, waiting for transfers between devices, mirror(): return lax.ppermute(value, 'seq', [(i, i ^ flip) for i in range(count)])  5.78 us
    unnamed x16, local copies, waits for them, and re-layouts  5.45 us
    ppermute x6, waiting for transfers between devices, to_places(): lax.ppermute(pieces[step], 'seq', [(i, i ^ step) for i in range(count)])  5.42 us
    ppermute x2, starting transfers between devices, mirror(): return lax.ppermute(value, 'seq', [(i, i ^ flip) for i in range(count)])  5.31 us
    pallas_call x1, Pallas kernels, program(): call(finish_kernel, jax.ShapeDtypeStruct((cores * length, half), BF16), o...  4.67 us
    pallas_call x1, Pallas kernels, program(): call(ends_kernel, [ends_shape] * 2, in_specs=[hbm] * 3, scratch_shapes=[h...  3.09 us
  transfers between devices with their start and end apart: 10, of which 6 were waited for; matrix products, arithmetic and copies ran while one was open for 0% of the time, Pallas kernels for 14%

profile of v3, /device:TPU:0, one launch (start us, length us, event | category | flops | bytes accessed | tf_op | source)
XLA Modules:
  0.0 50.2 jit_solution(8644569389064129178)
XLA Ops:
  0.0 0.7 %stack.10 = f32[1,2560]{1,0:T(1,128)S(1)} reshape(f32[2560]{0:T(1024)} %param.15) | data formatting | bytes 20480 | tf_op jit(solution)/shard_map/stack | solution.py:318
  1.4 0.8 %stack_reshape.3 = f32[1,2560]{1,0:T(1,128)S(1)} reshape(f32[40,64]{1,0:T(8,128)} %param.13) | data formatting | bytes 20480 | tf_op jit(solution)/shard_map/stack;reshape | solution.py:318
  2.3 1.1 %copy-done = bf16[128,2560]{1,0:T(8,128)(2,1)S(1)} copy-done((bf16[128,2560]{1,0:T(8,128)(2,1)S(1)}, bf16[128,2560]{1,0:T(8,128)(2,1)}, u32[]{:S(2)}) %copy-start) | copy-done | bytes 655384
  3.4 1.1 %copy-done.2 = bf16[128,2560]{1,0:T(8,128)(2,1)S(1)} copy-done((bf16[128,2560]{1,0:T(8,128)(2,1)S(1)}, bf16[128,2560]{1,0:T(8,128)(2,1)}, u32[]{:S(2)}) %copy-start.2) | copy-done | bytes 655384
  4.5 1.1 %copy-done.4 = bf16[128,2560]{1,0:T(8,128)(2,1)S(1)} copy-done((bf16[128,2560]{1,0:T(8,128)(2,1)S(1)}, bf16[128,2560]{1,0:T(8,128)(2,1)}, u32[]{:S(2)}) %copy-start.4) | copy-done | bytes 655384
  5.5 1.1 %copy-done.6 = bf16[128,2560]{1,0:T(8,128)(2,1)S(1)} copy-done((bf16[128,2560]{1,0:T(8,128)(2,1)S(1)}, bf16[128,2560]{1,0:T(8,128)(2,1)}, u32[]{:S(2)}) %copy-start.6) | copy-done | bytes 655384
  6.6 1.1 %copy-done.7 = bf16[128,2560]{1,0:T(8,128)(2,1)S(1)} copy-done((bf16[128,2560]{1,0:T(8,128)(2,1)S(1)}, bf16[128,2560]{1,0:T(8,128)(2,1)}, u32[]{:S(2)}) %copy-start.7) | copy-done | bytes 655384
  7.7 3.9 %shard_map.88 = f32[3,128,1280]{2,1,0:T(8,128)S(1)} custom-call(bf16[128,2560]{1,0:T(8,128)(2,1)S(1)} %copy-done.6, bf16[128,2560]{1,0:T(8,128)(2,1)S(1)} %copy-done, bf16[128,2560]{1,0:T(8,128)(2,1)S(1)} %copy-done.2, bf16[128,2560]{1,0:T(8,128)(2,1)S(1)} %copy-done.4, bf16[128,2560]{1,0:T(8,128)(2,1)S(1)} %copy-done.7, f32[3,2560]{1,0:T(4,128)S(1)} %pad_maximum_fusion.table_ref), custom_call_target="tpu_custom_call" | custom-call | tf_op jit(solution)/shard_map/pallas_call | solution.py:341
  12.2 3.1 %shard_map.82 = (f32[5,72,256]{2,1,0:T(8,128)S(1)}, f32[5,72,256]{2,1,0:T(8,128)S(1)}) custom-call(bf16[128,2560]{1,0:T(8,128)(2,1)} %k_ref.5, bf16[128,2560]{1,0:T(8,128)(2,1)} %v_ref.5, bf16[128,2560]{1,0:T(8,128)(2,1)} %w_ref.5), custom_call_target="tpu_custom_call" | custom-call | tf_op jit(solution)/shard_map/pallas_call | solution.py:332
  15.5 1.5 %collective-permute-done.other_ref.ends_other = f32[5,72,256]{2,1,0:T(8,128)S(1)} collective-permute-done((f32[5,72,256]{2,1,0:T(8,128)S(1)}, f32[5,72,256]{2,1,0:T(8,128)S(1)}, u32[]{:S(2)}, u32[]{:S(2)}) %collective-permute-start) | collective-permute-done | bytes 368672 | tf_op jit(solution)/shard_map/ppermute | solution.py:338
  17.2 2.7 %collective-permute-start.1 = (f32[88,256]{1,0:T(8,128)S(1)}, f32[88,256]{1,0:T(8,128)S(1)}, u32[]{:S(2)}, u32[]{:S(2)}) collective-permute-start(f32[88,256]{1,0:T(8,128)S(1)} %get-tuple-element.22), channel_id=1, source_target_pairs={{0,2},{2,0},{4,6},{6,4},{8,10},{10,8},{12,14},{14,12},{16,18},{18,... | collective-permute-start | bytes 270344 | tf_op jit(solution)/shard_map/ppermute | solution.py:347
  19.8 1.5 %collective-permute-start.2 = (f32[88,256]{1,0:T(8,128)S(1)}, f32[88,256]{1,0:T(8,128)S(1)}, u32[]{:S(2)}, u32[]{:S(2)}) collective-permute-start(f32[88,256]{1,0:T(8,128)S(1)} %get-tuple-element.23), channel_id=1, source_target_pairs={{0,4},{2,6},{4,0},{6,2},{8,12},{10,14},{12,8},{14,10},{16,20},{18,... | collective-permute-start | bytes 270344 | tf_op jit(solution)/shard_map/ppermute | solution.py:347
  21.4 1.6 %collective-permute-done.1.q1 = f32[88,256]{1,0:T(8,128)S(1)} collective-permute-done((f32[88,256]{1,0:T(8,128)S(1)}, f32[88,256]{1,0:T(8,128)S(1)}, u32[]{:S(2)}, u32[]{:S(2)}) %collective-permute-start.1) | collective-permute-done | bytes 90144 | tf_op jit(solution)/shard_map/ppermute | solution.py:347
  23.0 2.5 %collective-permute-done.2.q2 = f32[88,256]{1,0:T(8,128)S(1)} collective-permute-done((f32[88,256]{1,0:T(8,128)S(1)}, f32[88,256]{1,0:T(8,128)S(1)}, u32[]{:S(2)}, u32[]{:S(2)}) %collective-permute-start.2) | collective-permute-done | bytes 90144 | tf_op jit(solution)/shard_map/ppermute | solution.py:347
  25.5 1.3 %collective-permute-done.3.q3 = f32[88,256]{1,0:T(8,128)S(1)} collective-permute-done((f32[88,256]{1,0:T(8,128)S(1)}, f32[88,256]{1,0:T(8,128)S(1)}, u32[]{:S(2)}, u32[]{:S(2)}) %collective-permute-start.3) | collective-permute-done | bytes 90144 | tf_op jit(solution)/shard_map/ppermute | solution.py:347
  26.9 1.6 %collective-permute-start.4 = (f32[88,256]{1,0:T(8,128)S(1)}, f32[88,256]{1,0:T(8,128)S(1)}, u32[]{:S(2)}, u32[]{:S(2)}) collective-permute-start(f32[88,256]{1,0:T(8,128)S(1)} %get-tuple-element.26.total_ref.before_ref), channel_id=1, source_target_pairs={{0,8},{2,10},{4,12},{6,14},{8,0},{10,2},{12,4},{14,6},{16,24},{18,... | collective-permute-start | bytes 270344 | tf_op jit(solution)/shard_map/ppermute | solution.py:353
  28.5 3.0 %collective-permute-done.4.got_ref = f32[88,256]{1,0:T(8,128)S(1)} collective-permute-done((f32[88,256]{1,0:T(8,128)S(1)}, f32[88,256]{1,0:T(8,128)S(1)}, u32[]{:S(2)}, u32[]{:S(2)}) %collective-permute-start.4) | collective-permute-done | bytes 90144 | tf_op jit(solution)/shard_map/ppermute | solution.py:353
  31.5 3.7 %collective-permute-start.5 = (f32[88,256]{1,0:T(8,128)S(1)}, f32[88,256]{1,0:T(8,128)S(1)}, u32[]{:S(2)}, u32[]{:S(2)}) collective-permute-start(f32[88,256]{1,0:T(8,128)S(1)} %get-tuple-element.28), channel_id=1, source_target_pairs={{0,24},{2,26},{4,28},{6,30},{8,16},{10,18},{12,20},{14,22},{16,8},... | collective-permute-start | bytes 270344 | tf_op jit(solution)/shard_map/ppermute | solution.py:353
  35.2 2.8 %collective-permute-done.5.got_ref = f32[88,256]{1,0:T(8,128)S(1)} collective-permute-done((f32[88,256]{1,0:T(8,128)S(1)}, f32[88,256]{1,0:T(8,128)S(1)}, u32[]{:S(2)}, u32[]{:S(2)}) %collective-permute-start.5) | collective-permute-done | bytes 90144 | tf_op jit(solution)/shard_map/ppermute | solution.py:353
  38.1 0.9 %collective-permute-start.6 = (f32[80,256]{1,0:T(8,128)S(1)}, f32[80,256]{1,0:T(8,128)S(1)}, u32[]{:S(2)}, u32[]{:S(2)}) collective-permute-start(f32[80,256]{1,0:T(8,128)S(1)} %get-tuple-element.30), channel_id=1, source_target_pairs={{0,2},{2,0},{4,6},{6,4},{8,10},{10,8},{12,14},{14,12},{16,18},{18,... | collective-permute-start | bytes 245768 | tf_op jit(solution)/shard_map/ppermute | solution.py:347
  39.0 0.8 %collective-permute-start.7 = (f32[80,256]{1,0:T(8,128)S(1)}, f32[80,256]{1,0:T(8,128)S(1)}, u32[]{:S(2)}, u32[]{:S(2)}) collective-permute-start(f32[80,256]{1,0:T(8,128)S(1)} %get-tuple-element.31), channel_id=1, source_target_pairs={{0,4},{2,6},{4,0},{6,2},{8,12},{10,14},{12,8},{14,10},{16,20},{18,... | collective-permute-start | bytes 245768 | tf_op jit(solution)/shard_map/ppermute | solution.py:347
  39.8 1.8 %collective-permute-start.8 = (f32[80,256]{1,0:T(8,128)S(1)}, f32[80,256]{1,0:T(8,128)S(1)}, u32[]{:S(2)}, u32[]{:S(2)}) collective-permute-start(f32[80,256]{1,0:T(8,128)S(1)} %get-tuple-element.32), channel_id=1, source_target_pairs={{0,6},{2,4},{4,2},{6,0},{8,14},{10,12},{12,10},{14,8},{16,22},{18,... | collective-permute-start | bytes 245768 | tf_op jit(solution)/shard_map/ppermute | solution.py:347
  41.6 3.9 %shard_map.87.in_mine = f32[3,128,1280]{2,1,0:T(8,128)S(1)} custom-call(bf16[128,2560]{1,0:T(8,128)(2,1)S(1)} %copy-done.6, bf16[128,2560]{1,0:T(8,128)(2,1)S(1)} %copy-done.1, bf16[128,2560]{1,0:T(8,128)(2,1)S(1)} %copy-done.3, bf16[128,2560]{1,0:T(8,128)(2,1)S(1)} %copy-done.5, bf16[128,2560]{1,0:T(8,128)(2,1)S(1)} %copy-done.7, ...), custom_call_target="tpu_custom_call" | custom-call | tf_op jit(solution)/shard_map/pallas_call | solution.py:341
  45.6 4.7 %shard_map.89 = bf16[256,1280]{1,0:T(8,128)(2,1)} custom-call(f32[80,256]{1,0:T(8,128)S(1)} %get-tuple-element.29.p0, f32[80,256]{1,0:T(8,128)S(1)} %collective-permute-done.6.p1, f32[80,256]{1,0:T(8,128)S(1)} %collective-permute-done.7.p2, f32[80,256]{1,0:T(8,128)S(1)} %collective-permute-done.8.p3, f32[5,72,256]{2,1,0:T(8,128)S(1)} %get-tuple-element.19.mine_ref.ends_mine, ...), custom_call_target="tpu_custom_call" | custom-call | tf_op jit(solution)/shard_map/pallas_call | solution.py:375
  (24 shorter events, 1.8 us)
Async XLA Ops:
  2.3 1.1 %copy-start = (bf16[128,2560]{1,0:T(8,128)(2,1)S(1)}, bf16[128,2560]{1,0:T(8,128)(2,1)}, u32[]{:S(2)}) copy-start(bf16[128,2560]{1,0:T(8,128)(2,1)} %k_ref.5) | copy-start | bytes 1966084
  3.4 1.1 %copy-start.2 = (bf16[128,2560]{1,0:T(8,128)(2,1)S(1)}, bf16[128,2560]{1,0:T(8,128)(2,1)}, u32[]{:S(2)}) copy-start(bf16[128,2560]{1,0:T(8,128)(2,1)} %v_ref.5) | copy-start | bytes 1966084
  4.5 1.1 %copy-start.4 = (bf16[128,2560]{1,0:T(8,128)(2,1)S(1)}, bf16[128,2560]{1,0:T(8,128)(2,1)}, u32[]{:S(2)}) copy-start(bf16[128,2560]{1,0:T(8,128)(2,1)} %w_ref.5) | copy-start | bytes 1966084
  5.5 1.1 %copy-start.6 = (bf16[128,2560]{1,0:T(8,128)(2,1)S(1)}, bf16[128,2560]{1,0:T(8,128)(2,1)}, u32[]{:S(2)}) copy-start(bf16[128,2560]{1,0:T(8,128)(2,1)} %r_ref.3) | copy-start | bytes 1966084
  6.6 1.1 %copy-start.7 = (bf16[128,2560]{1,0:T(8,128)(2,1)S(1)}, bf16[128,2560]{1,0:T(8,128)(2,1)}, u32[]{:S(2)}) copy-start(bf16[128,2560]{1,0:T(8,128)(2,1)} %g_ref.3) | copy-start | bytes 1966084
  11.6 30.0 %copy-start.1 = (bf16[128,2560]{1,0:T(8,128)(2,1)S(1)}, bf16[128,2560]{1,0:T(8,128)(2,1)}, u32[]{:S(2)}) copy-start(bf16[128,2560]{1,0:T(8,128)(2,1)} %k_ref.5) | copy-start | bytes 1966084
  11.6 30.0 %copy-start.3 = (bf16[128,2560]{1,0:T(8,128)(2,1)S(1)}, bf16[128,2560]{1,0:T(8,128)(2,1)}, u32[]{:S(2)}) copy-start(bf16[128,2560]{1,0:T(8,128)(2,1)} %v_ref.5) | copy-start | bytes 1966084
  11.6 30.0 %copy-start.5 = (bf16[128,2560]{1,0:T(8,128)(2,1)S(1)}, bf16[128,2560]{1,0:T(8,128)(2,1)}, u32[]{:S(2)}) copy-start(bf16[128,2560]{1,0:T(8,128)(2,1)} %w_ref.5) | copy-start | bytes 1966084
  11.6 33.9 %collective-permute-start.9 = (f32[3,128,1280]{2,1,0:T(8,128)S(1)}, f32[3,128,1280]{2,1,0:T(8,128)S(1)}, u32[]{:S(2)}, u32[]{:S(2)}) collective-permute-start(f32[3,128,1280]{2,1,0:T(8,128)S(1)} %shard_map.88), channel_id=1, source_target_pairs={{0,1},{1,0},{2,3},{3,2},{4,5},{5,4},{6,7},{7,6},{8,9},{9,8},{10,11... | collective-permute-start | bytes 5898248 | tf_op jit(solution)/shard_map/ppermute | solution.py:358
  15.3 1.8 %collective-permute-start = (f32[5,72,256]{2,1,0:T(8,128)S(1)}, f32[5,72,256]{2,1,0:T(8,128)S(1)}, u32[]{:S(2)}, u32[]{:S(2)}) collective-permute-start(f32[5,72,256]{2,1,0:T(8,128)S(1)} %get-tuple-element.20), channel_id=1, source_target_pairs={{0,1},{1,0},{2,3},{3,2},{4,5},{5,4},{6,7},{7,6},{8,9},{9,8},{10,11... | collective-permute-start | bytes 1105928 | tf_op jit(solution)/shard_map/ppermute | solution.py:338
  17.2 5.8 %collective-permute-start.1 = (f32[88,256]{1,0:T(8,128)S(1)}, f32[88,256]{1,0:T(8,128)S(1)}, u32[]{:S(2)}, u32[]{:S(2)}) collective-permute-start(f32[88,256]{1,0:T(8,128)S(1)} %get-tuple-element.22), channel_id=1, source_target_pairs={{0,2},{2,0},{4,6},{6,4},{8,10},{10,8},{12,14},{14,12},{16,18},{18,... | collective-permute-start | bytes 270344 | tf_op jit(solution)/shard_map/ppermute | solution.py:347
  19.8 5.6 %collective-permute-start.2 = (f32[88,256]{1,0:T(8,128)S(1)}, f32[88,256]{1,0:T(8,128)S(1)}, u32[]{:S(2)}, u32[]{:S(2)}) collective-permute-start(f32[88,256]{1,0:T(8,128)S(1)} %get-tuple-element.23), channel_id=1, source_target_pairs={{0,4},{2,6},{4,0},{6,2},{8,12},{10,14},{12,8},{14,10},{16,20},{18,... | collective-permute-start | bytes 270344 | tf_op jit(solution)/shard_map/ppermute | solution.py:347
  21.4 5.4 %collective-permute-start.3 = (f32[88,256]{1,0:T(8,128)S(1)}, f32[88,256]{1,0:T(8,128)S(1)}, u32[]{:S(2)}, u32[]{:S(2)}) collective-permute-start(f32[88,256]{1,0:T(8,128)S(1)} %get-tuple-element.24), channel_id=1, source_target_pairs={{0,6},{2,4},{4,2},{6,0},{8,14},{10,12},{12,10},{14,8},{16,22},{18,... | collective-permute-start | bytes 270344 | tf_op jit(solution)/shard_map/ppermute | solution.py:347
  26.9 4.6 %collective-permute-start.4 = (f32[88,256]{1,0:T(8,128)S(1)}, f32[88,256]{1,0:T(8,128)S(1)}, u32[]{:S(2)}, u32[]{:S(2)}) collective-permute-start(f32[88,256]{1,0:T(8,128)S(1)} %get-tuple-element.26.total_ref.before_ref), channel_id=1, source_target_pairs={{0,8},{2,10},{4,12},{6,14},{8,0},{10,2},{12,4},{14,6},{16,24},{18,... | collective-permute-start | bytes 270344 | tf_op jit(solution)/shard_map/ppermute | solution.py:353
  31.5 6.5 %collective-permute-start.5 = (f32[88,256]{1,0:T(8,128)S(1)}, f32[88,256]{1,0:T(8,128)S(1)}, u32[]{:S(2)}, u32[]{:S(2)}) collective-permute-start(f32[88,256]{1,0:T(8,128)S(1)} %get-tuple-element.28), channel_id=1, source_target_pairs={{0,24},{2,26},{4,28},{6,30},{8,16},{10,18},{12,20},{14,22},{16,8},... | collective-permute-start | bytes 270344 | tf_op jit(solution)/shard_map/ppermute | solution.py:353
  38.1 7.5 %collective-permute-start.6 = (f32[80,256]{1,0:T(8,128)S(1)}, f32[80,256]{1,0:T(8,128)S(1)}, u32[]{:S(2)}, u32[]{:S(2)}) collective-permute-start(f32[80,256]{1,0:T(8,128)S(1)} %get-tuple-element.30), channel_id=1, source_target_pairs={{0,2},{2,0},{4,6},{6,4},{8,10},{10,8},{12,14},{14,12},{16,18},{18,... | collective-permute-start | bytes 245768 | tf_op jit(solution)/shard_map/ppermute | solution.py:347
  39.0 6.6 %collective-permute-start.7 = (f32[80,256]{1,0:T(8,128)S(1)}, f32[80,256]{1,0:T(8,128)S(1)}, u32[]{:S(2)}, u32[]{:S(2)}) collective-permute-start(f32[80,256]{1,0:T(8,128)S(1)} %get-tuple-element.31), channel_id=1, source_target_pairs={{0,4},{2,6},{4,0},{6,2},{8,12},{10,14},{12,8},{14,10},{16,20},{18,... | collective-permute-start | bytes 245768 | tf_op jit(solution)/shard_map/ppermute | solution.py:347
  39.8 5.8 %collective-permute-start.8 = (f32[80,256]{1,0:T(8,128)S(1)}, f32[80,256]{1,0:T(8,128)S(1)}, u32[]{:S(2)}, u32[]{:S(2)}) collective-permute-start(f32[80,256]{1,0:T(8,128)S(1)} %get-tuple-element.32), channel_id=1, source_target_pairs={{0,6},{2,4},{4,2},{6,0},{8,14},{10,12},{12,10},{14,8},{16,22},{18,... | collective-permute-start | bytes 245768 | tf_op jit(solution)/shard_map/ppermute | solution.py:347

commit v4 on v3

--- a/solution.py
+++ b/solution.py
@@ -15,6 +15,7 @@
 BLOCK = 64
 PLANE = 4
 ROWS = CHANNELS // PLANE
+STATE_STEP = 0.75 * 6.0
 VMEM_LIMIT = 12 * 2**20
 F32 = jnp.float32
 BF16 = jnp.bfloat16
@@ -102,96 +103,103 @@
     wide = dot(
         jnp.concatenate([turned, turned], axis=1), jnp.concatenate([high, low], axis=0)
     )
-    return own_blocks(wide, CHANNELS), jnp.broadcast_to(jnp.exp(final), (8, LANES))
-
-
-def ends_kernel(k_ref, v_ref, w_ref, mine_ref, theirs_ref, k_buf, v_buf, w_buf, sems):
-    groups = mine_ref.shape[0]
-    half = groups * LANES
-    copies = {}
-    for side in (1, 0):
-        at = half_at(side, half)
-        for index, (ref, buf) in enumerate(((w_ref, w_buf), (k_ref, k_buf), (v_ref, v_buf))):
-            copies[side, index] = pltpu.make_async_copy(
-                ref.at[:, at], buf.at[side], sems.at[side, index]
-            )
-            copies[side, index].start()
-    for side, out_ref in ((1, theirs_ref), (0, mine_ref)):
-        for index in range(3):
-            copies[side, index].wait()
-        for group in range(groups):
-            at = pl.ds(group * LANES, LANES)
-            state, decay = ends_of(k_buf[side, :, at], v_buf[side, :, at], w_buf[side, :, at])
-            out_ref[group, :CHANNELS, :] = state
-            out_ref[group, CHANNELS:, :] = decay
-
-
-def combine_kernel(mine_ref, other_ref, q0, q1, q2, q3, state_ref):
+    return own_blocks(wide, CHANNELS), jnp.broadcast_to(final, (8, LANES))
+
+
+def ends_kernel(side, k_ref, v_ref, w_ref, out_ref, k_buf, v_buf, w_buf, sems):
+    groups = out_ref.shape[0]
+    copies = []
+    for index, (ref, buf) in enumerate(((w_ref, w_buf), (k_ref, k_buf), (v_ref, v_buf))):
+        at = half_at(side, groups * LANES)
+        copies.append(pltpu.make_async_copy(ref.at[:, at], buf, sems.at[index]))
+        copies[-1].start()
+    for copy in copies:
+        copy.wait()
+    for group in range(groups):
+        at = pl.ds(group * LANES, LANES)
+        state, decay = ends_of(k_buf[:, at], v_buf[:, at], w_buf[:, at])
+        out_ref[group, :CHANNELS, :] = state
+        out_ref[group, CHANNELS:, :] = decay
+
+
+def log_rows(groups, group):
+    at = groups * ROWS + group
+    return slice(at, at + 1), slice(at + groups, at + groups + 1)
+
+
+def put_log(ref, groups, group, value):
+    high, low = log_rows(groups, group)
+    rounded = value.astype(BF16).astype(F32)
+    ref[high, :] = rounded
+    ref[low, :] = value - rounded
+
+
+def get_log(ref, groups, group):
+    high, low = log_rows(groups, group)
+    return ref[high, :] + ref[low, :]
+
+
+def combine_kernel(scale, mine_ref, other_ref, q0, q1, q2, q3, state_ref):
     core = lax.axis_index("head")
     place = lax.axis_index("seq") % PLANE
     groups = mine_ref.shape[0]
     first = core == 0
     outs = (q0, q1, q2, q3)
     for out in outs:
-        out[...] = jnp.zeros_like(out)
+        out[groups * ROWS :, :] = jnp.zeros((out.shape[0] - groups * ROWS, LANES), F32)
     for group in range(groups):
         mine, other = mine_ref[group], other_ref[group]
         early, late = jnp.where(first, mine, other), jnp.where(first, other, mine)
-        decay = late[CHANNELS : CHANNELS + 1]
-        state_ref[...] = early[:CHANNELS] * decay + late[:CHANNELS]
-        both = early[CHANNELS : CHANNELS + 1] * decay
+        late_log = late[CHANNELS : CHANNELS + 1]
+        state = early[:CHANNELS] * jnp.exp(late_log) + late[:CHANNELS]
+        state_ref[...] = state if scale == 1.0 else state * F32(scale)
+        both = early[CHANNELS : CHANNELS + 1] + late_log
         for step, out in enumerate(outs):
             at = pl.multiple_of(lax.bitwise_xor(place, step) * ROWS, ROWS)
             out[group * ROWS : (group + 1) * ROWS, :] = state_ref[pl.ds(at, ROWS), :]
-            at = groups * ROWS + group
-            out[at : at + 1, :] = both
-
-
-def plane_kernel(q0, q1, q2, q3, total_ref, prefix_ref, slab_ref):
+            put_log(out, groups, group, both)
+
+
+def plane_kernel(groups, q0, q1, q2, q3, total_ref, prefix_ref, slab_ref):
     place = lax.axis_index("seq") % PLANE
-    groups = total_ref.shape[0] // ROWS
     for step, piece in enumerate((q0, q1, q2, q3)):
         slab_ref[lax.bitwise_xor(place, step)] = piece[...]
-    total_ref[...] = jnp.zeros_like(total_ref)
+    total_ref[groups * ROWS :, :] = jnp.zeros((total_ref.shape[0] - groups * ROWS, LANES), F32)
     for group in range(groups):
         rows = slice(group * ROWS, (group + 1) * ROWS)
-        at = groups * ROWS + group
-        row = slice(at, at + 1)
+        row, _ = log_rows(groups, group)
         state = jnp.zeros((ROWS, LANES), F32)
-        decay = jnp.ones((1, LANES), F32)
+        log = jnp.zeros((1, LANES), F32)
         for slab in range(PLANE):
             prefix_ref[slab, rows, :] = state
-            prefix_ref[slab, row, :] = decay
-            step = slab_ref[slab, row, :]
-            state = step * state + slab_ref[slab, rows, :]
-            decay = step * decay
+            prefix_ref[slab, row, :] = jnp.exp(log)
+            step = get_log(slab_ref.at[slab], groups, group)
+            state = jnp.exp(step) * state + slab_ref[slab, rows, :]
+            log = log + step
         total_ref[rows, :] = state
-        total_ref[row, :] = decay
-
-
-def round_kernel(bit, first_round, total_ref, got_ref, before_ref, total_out, before_out):
+        put_log(total_ref, groups, group, log)
+
+
+def round_kernel(groups, bit, first_round, total_ref, got_ref, before_ref, total_out, before_out):
     plane = lax.axis_index("seq") // PLANE
     upper = lax.bitwise_and(plane, bit) != 0
-    groups = total_ref.shape[0] // ROWS
-    total_out[...] = jnp.zeros_like(total_out)
-    before_out[...] = jnp.zeros_like(before_out)
+    total_out[groups * ROWS :, :] = jnp.zeros((total_out.shape[0] - groups * ROWS, LANES), F32)
     for group in range(groups):
         rows = slice(group * ROWS, (group + 1) * ROWS)
-        at = groups * ROWS + group
-        row = slice(at, at + 1)
+        row, _ = log_rows(groups, group)
         total, got = total_ref[rows, :], got_ref[rows, :]
-        total_decay, got_decay = total_ref[row, :], got_ref[row, :]
+        total_log, got_log = get_log(total_ref, groups, group), get_log(got_ref, groups, group)
         low, high = jnp.where(upper, got, total), jnp.where(upper, total, got)
-        total_out[rows, :] = jnp.where(upper, total_decay, got_decay) * low + high
-        total_out[row, :] = total_decay * got_decay
+        total_out[rows, :] = jnp.exp(jnp.where(upper, total_log, got_log)) * low + high
+        put_log(total_out, groups, group, total_log + got_log)
         if first_round:
             before = jnp.where(upper, got, F32(0.0))
-            before_decay = jnp.where(upper, got_decay, F32(1.0))
+            before_decay = jnp.where(upper, jnp.exp(got_log), F32(1.0))
         else:
             decay = before_ref[row, :]
             before = before_ref[rows, :]
             before = jnp.where(upper, decay * got + before, before)
-            before_decay = jnp.where(upper, got_decay * decay, decay)
+            before_decay = jnp.where(upper, jnp.exp(got_log) * decay, decay)
         before_out[rows, :] = before
         before_out[row, :] = before_decay
 
@@ -203,8 +211,7 @@
     groups = p0.shape[0] // ROWS
     for group in range(groups):
         rows = slice(group * ROWS, (group + 1) * ROWS)
-        at = groups * ROWS + group
-        row = slice(at, at + 1)
+        row, _ = log_rows(groups, group)
         before = before_ref[rows, :]
         before = jnp.where(upper, before_ref[row, :] * got_ref[rows, :] + before, before)
         for step, out in enumerate((p0, p1, p2, p3)):
@@ -259,7 +266,7 @@
 
 
 def finish_kernel(
-    p0, p1, p2, p3, ends_mine, ends_other, in_mine, in_other, table_ref, out_ref,
+    scale, p0, p1, p2, p3, ends_mine, ends_other, in_mine, in_other, table_ref, out_ref,
     state_ref, buf, sems,
 ):
     core = lax.axis_index("head")
@@ -273,7 +280,7 @@
         source = lax.bitwise_xor(place, step) * ROWS
         for group in range(groups):
             at = pl.multiple_of(source + group * CHANNELS, ROWS)
-            state_ref[pl.ds(at, ROWS), :] = piece[group * ROWS : (group + 1) * ROWS, :]
+            state_ref[pl.ds(at, ROWS), :] = piece[group * ROWS : (group + 1) * ROWS, :] * F32(1.0 / scale)
     copies = []
     for group in range(groups):
         at = lanes_at(0, group, groups)
@@ -283,7 +290,7 @@
         for half in range(2):
             local = core == half
             if half == 1:
-                state = early[CHANNELS : CHANNELS + 1] * state + early[:CHANNELS]
+                state = jnp.exp(early[CHANNELS : CHANNELS + 1]) * state + early[:CHANNELS]
             s_high, s_low = split(state - jnp.mean(state, axis=0, keepdims=True))
             s_high, s_low = spread_heads(s_high, masks), spread_heads(s_low, masks)
             r_high, r_low = split(jnp.where(local, in_mine[1, :, out], in_other[1, :, out]))
@@ -326,38 +333,48 @@
         )
 
     ends_shape = jax.ShapeDtypeStruct((groups, CHANNELS + 8, LANES), F32)
-    packed = jax.ShapeDtypeStruct((groups * ROWS + -(-groups // 8) * 8, LANES), F32)
+    packed_rows = -(-groups * (ROWS + 2) // 16) * 16
+    packed = jax.ShapeDtypeStruct((packed_rows, LANES), F32)
     piece = jax.ShapeDtypeStruct((groups * ROWS, LANES), F32)
-    half_buffer = pltpu.VMEM((cores, length, half), BF16)
-    mine, theirs = call(
-        ends_kernel,
-        [ends_shape] * 2,
-        in_specs=[hbm] * 3,
-        scratch_shapes=[half_buffer] * 3 + [pltpu.SemaphoreType.DMA((cores, 3))],
-    )(*(pltpu.with_memory_space_constraint(x, pltpu.HBM) for x in (k, v, w)))
-    other = lax.ppermute(theirs, "head", swap)
+    scale = 1.0
+    while STATE_STEP * length * cores * count * scale > 2.0**15:
+        scale *= 0.5
+
+    def ends(side):
+        return call(
+            functools.partial(ends_kernel, side),
+            ends_shape,
+            in_specs=[hbm] * 3,
+            scratch_shapes=[pltpu.VMEM((length, half), BF16)] * 3
+            + [pltpu.SemaphoreType.DMA((3,))],
+        )(*(pltpu.with_memory_space_constraint(x, pltpu.HBM) for x in (k, v, w)))
+
+    other = lax.ppermute(ends(1), "head", swap)
+    mine = ends(0)
 
     def within(side):
         return call(
             functools.partial(within_kernel, side), jax.ShapeDtypeStruct((3, length, half), F32)
         )(r, k, v, w, gate, table)
 
+    def over_seq(value, flip):
+        pairs = [(i, i ^ flip) for i in range(count)]
+        return lax.ppermute(value.astype(jnp.float16), "seq", pairs).astype(F32)
+
     def to_places(pieces):
-        return [pieces[0]] + [
-            lax.ppermute(pieces[step], "seq", [(i, i ^ step) for i in range(count)])
-            for step in range(1, PLANE)
-        ]
+        return [pieces[0]] + [over_seq(pieces[step], step) for step in range(1, PLANE)]
 
     def mirror(value, bit):
-        flip = (2 * bit - 1) * PLANE
-        return lax.ppermute(value, "seq", [(i, i ^ flip) for i in range(count)])
+        return over_seq(value, (2 * bit - 1) * PLANE)
 
     quarters = call(
-        combine_kernel, [packed] * PLANE, scratch_shapes=[pltpu.VMEM((CHANNELS, LANES), F32)]
+        functools.partial(combine_kernel, scale),
+        [packed] * PLANE,
+        scratch_shapes=[pltpu.VMEM((CHANNELS, LANES), F32)],
     )(mine, other)
     in_other = lax.ppermute(within(1), "head", swap)
     total, prefix = call(
-        plane_kernel,
+        functools.partial(plane_kernel, groups),
         [packed, jax.ShapeDtypeStruct((PLANE,) + packed.shape, F32)],
         scratch_shapes=[pltpu.VMEM((PLANE,) + packed.shape, F32)],
     )(*to_places(quarters))
@@ -366,14 +383,14 @@
     bit = 1
     while 2 * bit < planes:
         total, before = call(
-            functools.partial(round_kernel, bit, bit == 1), [packed] * 2
+            functools.partial(round_kernel, groups, bit, bit == 1), [packed] * 2
         )(total, mirror(total, bit), before)
         bit *= 2
     states = call(functools.partial(back_kernel, bit), [piece] * PLANE)(
         prefix, before, mirror(total, bit)
     )
     return call(
-        finish_kernel,
+        functools.partial(finish_kernel, scale),
         jax.ShapeDtypeStruct((cores * length, half), BF16),
         out_specs=hbm,
         scratch_shapes=[

time: 50.7 us -> 49.8 us (0.982)
  waiting for transfers between devices: 12.7 us -> 9.77 us
  Pallas kernels: 15.8 us -> 17.1 us
    ppermute x9, waiting for transfers between devices: 12.7 us -> 9.77 us  [the longest x8 9.76 us: over_seq(): return lax.ppermute(value.astype(jnp.float16), 'seq', pairs).astype(F32)]
    pallas_call x5 -> x6, Pallas kernels: 7.96 us -> 9.23 us  [the longest x1 4.68 us: program(): call(functools.partial(finish_kernel, scale), jax.ShapeDtypeStruct((cores...]
  transfers between devices with their start and end apart: 10 -> 10, of which waited for: 6 -> 5; matrix products, arithmetic and copies ran while one was open for 0% -> 0% of each run, Pallas kernels for 14% -> 17%
where the time goes in v4:
time: 49.8 us; the launch traced here: 49.2 us
  Pallas kernels  17.1 us (34%)
  starting transfers between devices  14.3 us (29%)
  waiting for transfers between devices  9.77 us (20%)
  local copies, waits for them, and re-layouts  7.68 us (15%)
    ppermute x8, starting transfers between devices, over_seq(): return lax.ppermute(value.astype(jnp.float16), 'seq', pairs).astype(F32)  13.7 us
    ppermute x8, waiting for transfers between devices, over_seq(): return lax.ppermute(value.astype(jnp.float16), 'seq', pairs).astype(F32)  9.76 us
    pallas_call x2, Pallas kernels, within(): call(functools.partial(within_kernel, side), jax.ShapeDtypeStruct((3, len...  7.78 us
    unnamed x16, local copies, waits for them, and re-layouts  5.45 us
    pallas_call x1, Pallas kernels, program(): call(functools.partial(finish_kernel, scale), jax.ShapeDtypeStruct((cores...  4.68 us
    pallas_call x2, Pallas kernels, ends(): call(functools.partial(ends_kernel, side), ends_shape, in_specs=[hbm] * 3...  4.26 us
    another operation x3, local copies, waits for them, and re-layouts, program(): table = jnp.stack([bonus.reshape(width), gain, bias])  2.23 us
  transfers between devices with their start and end apart: 10, of which 5 were waited for; matrix products, arithmetic and copies ran while one was open for 0% of the time, Pallas kernels for 17%

profile of v4, /device:TPU:0, one launch (start us, length us, event | category | flops | bytes accessed | tf_op | source)
XLA Modules:
  0.0 49.2 jit_solution(16092560440155824286)
XLA Ops:
  0.0 0.7 %stack.10 = f32[1,2560]{1,0:T(1,128)S(1)} reshape(f32[2560]{0:T(1024)} %param.15) | data formatting | bytes 20480 | tf_op jit(solution)/shard_map/stack | solution.py:325
  0.7 0.7 %stack.9 = f32[1,2560]{1,0:T(1,128)S(1)} reshape(f32[2560]{0:T(1024)} %param.14) | data formatting | bytes 20480 | tf_op jit(solution)/shard_map/stack | solution.py:325
  1.4 0.8 %stack_reshape.3 = f32[1,2560]{1,0:T(1,128)S(1)} reshape(f32[40,64]{1,0:T(8,128)} %param.13) | data formatting | bytes 20480 | tf_op jit(solution)/shard_map/stack;reshape | solution.py:325
  2.3 1.1 %copy-done = bf16[128,2560]{1,0:T(8,128)(2,1)S(1)} copy-done((bf16[128,2560]{1,0:T(8,128)(2,1)S(1)}, bf16[128,2560]{1,0:T(8,128)(2,1)}, u32[]{:S(2)}) %copy-start) | copy-done | bytes 655384
  3.4 1.1 %copy-done.2 = bf16[128,2560]{1,0:T(8,128)(2,1)S(1)} copy-done((bf16[128,2560]{1,0:T(8,128)(2,1)S(1)}, bf16[128,2560]{1,0:T(8,128)(2,1)}, u32[]{:S(2)}) %copy-start.2) | copy-done | bytes 655384
  4.5 1.1 %copy-done.4 = bf16[128,2560]{1,0:T(8,128)(2,1)S(1)} copy-done((bf16[128,2560]{1,0:T(8,128)(2,1)S(1)}, bf16[128,2560]{1,0:T(8,128)(2,1)}, u32[]{:S(2)}) %copy-start.4) | copy-done | bytes 655384
  5.5 1.1 %copy-done.6 = bf16[128,2560]{1,0:T(8,128)(2,1)S(1)} copy-done((bf16[128,2560]{1,0:T(8,128)(2,1)S(1)}, bf16[128,2560]{1,0:T(8,128)(2,1)}, u32[]{:S(2)}) %copy-start.6) | copy-done | bytes 655384
  6.6 1.1 %copy-done.7 = bf16[128,2560]{1,0:T(8,128)(2,1)S(1)} copy-done((bf16[128,2560]{1,0:T(8,128)(2,1)S(1)}, bf16[128,2560]{1,0:T(8,128)(2,1)}, u32[]{:S(2)}) %copy-start.7) | copy-done | bytes 655384
  7.7 3.9 %shard_map.89 = f32[3,128,1280]{2,1,0:T(8,128)S(1)} custom-call(bf16[128,2560]{1,0:T(8,128)(2,1)S(1)} %copy-done.6, bf16[128,2560]{1,0:T(8,128)(2,1)S(1)} %copy-done, bf16[128,2560]{1,0:T(8,128)(2,1)S(1)} %copy-done.2, bf16[128,2560]{1,0:T(8,128)(2,1)S(1)} %copy-done.4, bf16[128,2560]{1,0:T(8,128)(2,1)S(1)} %copy-done.7, f32[3,2560]{1,0:T(4,128)S(1)} %pad_maximum_fusion.table_ref), custom_call_target="tpu_custom_call" | custom-call | tf_op jit(solution)/shard_map/pallas_call | solution.py:356
  11.6 0.6 %collective-permute-start.9 = (f32[3,128,1280]{2,1,0:T(8,128)S(1)}, f32[3,128,1280]{2,1,0:T(8,128)S(1)}, u32[]{:S(2)}, u32[]{:S(2)}) collective-permute-start(f32[3,128,1280]{2,1,0:T(8,128)S(1)} %shard_map.89), channel_id=1, source_target_pairs={{0,1},{1,0},{2,3},{3,2},{4,5},{5,4},{6,7},{7,6},{8,9},{9,8},{10,11... | collective-permute-start | bytes 5898248 | tf_op jit(solution)/shard_map/ppermute | solution.py:375
  12.2 2.1 %shard_map.83 = f32[5,72,256]{2,1,0:T(8,128)S(1)} custom-call(bf16[128,2560]{1,0:T(8,128)(2,1)} %k_ref.7, bf16[128,2560]{1,0:T(8,128)(2,1)} %v_ref.7, bf16[128,2560]{1,0:T(8,128)(2,1)} %w_ref.7), custom_call_target="tpu_custom_call" | custom-call | tf_op jit(solution)/shard_map/pallas_call | solution.py:344
  14.4 2.1 %shard_map.82.mine_ref.ends_mine = f32[5,72,256]{2,1,0:T(8,128)S(1)} custom-call(bf16[128,2560]{1,0:T(8,128)(2,1)} %k_ref.7, bf16[128,2560]{1,0:T(8,128)(2,1)} %v_ref.7, bf16[128,2560]{1,0:T(8,128)(2,1)} %w_ref.7), custom_call_target="tpu_custom_call" | custom-call | tf_op jit(solution)/shard_map/pallas_call | solution.py:344
  16.7 3.0 %collective-permute-start.1 = (f16[96,256]{1,0:T(8,128)(2,1)S(1)}, f16[96,256]{1,0:T(8,128)(2,1)S(1)}, u32[]{:S(2)}, u32[]{:S(2)}) collective-permute-start(f16[96,256]{1,0:T(8,128)(2,1)S(1)} %convert_element_type.48), channel_id=1, source_target_pairs={{0,2},{2,0},{4,6},{6,4},{8,10},{10,8},{12,14},{14,12},{16,18},{18,... | collective-permute-start | bytes 147464 | tf_op jit(solution)/shard_map/ppermute | solution.py:362
  19.8 1.6 %collective-permute-start.2 = (f16[96,256]{1,0:T(8,128)(2,1)S(1)}, f16[96,256]{1,0:T(8,128)(2,1)S(1)}, u32[]{:S(2)}, u32[]{:S(2)}) collective-permute-start(f16[96,256]{1,0:T(8,128)(2,1)S(1)} %convert_element_type.50), channel_id=1, source_target_pairs={{0,4},{2,6},{4,0},{6,2},{8,12},{10,14},{12,8},{14,10},{16,20},{18,... | collective-permute-start | bytes 147464 | tf_op jit(solution)/shard_map/ppermute | solution.py:362
  21.8 2.1 %collective-permute-done.2 = f16[96,256]{1,0:T(8,128)(2,1)S(1)} collective-permute-done((f16[96,256]{1,0:T(8,128)(2,1)S(1)}, f16[96,256]{1,0:T(8,128)(2,1)S(1)}, u32[]{:S(2)}, u32[]{:S(2)}) %collective-permute-start.2) | collective-permute-done | bytes 49184 | tf_op jit(solution)/shard_map/ppermute | solution.py:362
  23.9 2.5 %collective-permute-done.3 = f16[96,256]{1,0:T(8,128)(2,1)S(1)} collective-permute-done((f16[96,256]{1,0:T(8,128)(2,1)S(1)}, f16[96,256]{1,0:T(8,128)(2,1)S(1)}, u32[]{:S(2)}, u32[]{:S(2)}) %collective-permute-start.3) | collective-permute-done | bytes 49184 | tf_op jit(solution)/shard_map/ppermute | solution.py:362
  26.6 1.6 %collective-permute-start.4 = (f16[96,256]{1,0:T(8,128)(2,1)S(1)}, f16[96,256]{1,0:T(8,128)(2,1)S(1)}, u32[]{:S(2)}, u32[]{:S(2)}) collective-permute-start(f16[96,256]{1,0:T(8,128)(2,1)S(1)} %convert_element_type.54), channel_id=1, source_target_pairs={{0,8},{2,10},{4,12},{6,14},{8,0},{10,2},{12,4},{14,6},{16,24},{18,... | collective-permute-start | bytes 147464 | tf_op jit(solution)/shard_map/ppermute | solution.py:362
  28.2 2.5 %collective-permute-done.4 = f16[96,256]{1,0:T(8,128)(2,1)S(1)} collective-permute-done((f16[96,256]{1,0:T(8,128)(2,1)S(1)}, f16[96,256]{1,0:T(8,128)(2,1)S(1)}, u32[]{:S(2)}, u32[]{:S(2)}) %collective-permute-start.4) | collective-permute-done | bytes 49184 | tf_op jit(solution)/shard_map/ppermute | solution.py:362
  30.8 3.7 %collective-permute-start.5 = (f16[96,256]{1,0:T(8,128)(2,1)S(1)}, f16[96,256]{1,0:T(8,128)(2,1)S(1)}, u32[]{:S(2)}, u32[]{:S(2)}) collective-permute-start(f16[96,256]{1,0:T(8,128)(2,1)S(1)} %convert_element_type.56), channel_id=1, source_target_pairs={{0,24},{2,26},{4,28},{6,30},{8,16},{10,18},{12,20},{14,22},{16,8},... | collective-permute-start | bytes 147464 | tf_op jit(solution)/shard_map/ppermute | solution.py:362
  34.5 2.3 %collective-permute-done.5 = f16[96,256]{1,0:T(8,128)(2,1)S(1)} collective-permute-done((f16[96,256]{1,0:T(8,128)(2,1)S(1)}, f16[96,256]{1,0:T(8,128)(2,1)S(1)}, u32[]{:S(2)}, u32[]{:S(2)}) %collective-permute-start.5) | collective-permute-done | bytes 49184 | tf_op jit(solution)/shard_map/ppermute | solution.py:362
  36.9 0.6 %collective-permute-start.6 = (f16[80,256]{1,0:T(8,128)(2,1)S(1)}, f16[80,256]{1,0:T(8,128)(2,1)S(1)}, u32[]{:S(2)}, u32[]{:S(2)}) collective-permute-start(f16[80,256]{1,0:T(8,128)(2,1)S(1)} %convert_element_type.58), channel_id=1, source_target_pairs={{0,2},{2,0},{4,6},{6,4},{8,10},{10,8},{12,14},{14,12},{16,18},{18,... | collective-permute-start | bytes 122888 | tf_op jit(solution)/shard_map/ppermute | solution.py:362
  37.8 2.7 %collective-permute-start.8 = (f16[80,256]{1,0:T(8,128)(2,1)S(1)}, f16[80,256]{1,0:T(8,128)(2,1)S(1)}, u32[]{:S(2)}, u32[]{:S(2)}) collective-permute-start(f16[80,256]{1,0:T(8,128)(2,1)S(1)} %convert_element_type.62), channel_id=1, source_target_pairs={{0,6},{2,4},{4,2},{6,0},{8,14},{10,12},{12,10},{14,8},{16,22},{18,... | collective-permute-start | bytes 122888 | tf_op jit(solution)/shard_map/ppermute | solution.py:362
  40.6 3.9 %shard_map.88.in_mine = f32[3,128,1280]{2,1,0:T(8,128)S(1)} custom-call(bf16[128,2560]{1,0:T(8,128)(2,1)S(1)} %copy-done.6, bf16[128,2560]{1,0:T(8,128)(2,1)S(1)} %copy-done.1, bf16[128,2560]{1,0:T(8,128)(2,1)S(1)} %copy-done.3, bf16[128,2560]{1,0:T(8,128)(2,1)S(1)} %copy-done.5, bf16[128,2560]{1,0:T(8,128)(2,1)S(1)} %copy-done.7, ...), custom_call_target="tpu_custom_call" | custom-call | tf_op jit(solution)/shard_map/pallas_call | solution.py:356
  44.5 4.7 %shard_map.90 = bf16[256,1280]{1,0:T(8,128)(2,1)} custom-call(f32[80,256]{1,0:T(8,128)S(1)} %get-tuple-element.25.p0, f32[80,256]{1,0:T(8,128)S(1)} %convert_element_type.59.p1, f32[80,256]{1,0:T(8,128)S(1)} %convert_element_type.61.p2, f32[80,256]{1,0:T(8,128)S(1)} %convert_element_type.63.p3, f32[5,72,256]{2,1,0:T(8,128)S(1)} %shard_map.82.mine_ref.ends_mine, ...), custom_call_target="tpu_custom_call" | custom-call | tf_op jit(solution)/shard_map/pallas_call | solution.py:392
  (41 shorter events, 1.4 us)
Async XLA Ops:
  2.3 1.1 %copy-start = (bf16[128,2560]{1,0:T(8,128)(2,1)S(1)}, bf16[128,2560]{1,0:T(8,128)(2,1)}, u32[]{:S(2)}) copy-start(bf16[128,2560]{1,0:T(8,128)(2,1)} %k_ref.7) | copy-start | bytes 1966084
  3.4 1.1 %copy-start.2 = (bf16[128,2560]{1,0:T(8,128)(2,1)S(1)}, bf16[128,2560]{1,0:T(8,128)(2,1)}, u32[]{:S(2)}) copy-start(bf16[128,2560]{1,0:T(8,128)(2,1)} %v_ref.7) | copy-start | bytes 1966084
  4.5 1.1 %copy-start.4 = (bf16[128,2560]{1,0:T(8,128)(2,1)S(1)}, bf16[128,2560]{1,0:T(8,128)(2,1)}, u32[]{:S(2)}) copy-start(bf16[128,2560]{1,0:T(8,128)(2,1)} %w_ref.7) | copy-start | bytes 1966084
  5.5 1.1 %copy-start.6 = (bf16[128,2560]{1,0:T(8,128)(2,1)S(1)}, bf16[128,2560]{1,0:T(8,128)(2,1)}, u32[]{:S(2)}) copy-start(bf16[128,2560]{1,0:T(8,128)(2,1)} %r_ref.3) | copy-start | bytes 1966084
  6.6 1.1 %copy-start.7 = (bf16[128,2560]{1,0:T(8,128)(2,1)S(1)}, bf16[128,2560]{1,0:T(8,128)(2,1)}, u32[]{:S(2)}) copy-start(bf16[128,2560]{1,0:T(8,128)(2,1)} %g_ref.3) | copy-start | bytes 1966084
  11.6 32.9 %collective-permute-start.9 = (f32[3,128,1280]{2,1,0:T(8,128)S(1)}, f32[3,128,1280]{2,1,0:T(8,128)S(1)}, u32[]{:S(2)}, u32[]{:S(2)}) collective-permute-start(f32[3,128,1280]{2,1,0:T(8,128)S(1)} %shard_map.89), channel_id=1, source_target_pairs={{0,1},{1,0},{2,3},{3,2},{4,5},{5,4},{6,7},{7,6},{8,9},{9,8},{10,11... | collective-permute-start | bytes 5898248 | tf_op jit(solution)/shard_map/ppermute | solution.py:375
  14.3 2.3 %collective-permute-start = (f32[5,72,256]{2,1,0:T(8,128)S(1)}, f32[5,72,256]{2,1,0:T(8,128)S(1)}, u32[]{:S(2)}, u32[]{:S(2)}) collective-permute-start(f32[5,72,256]{2,1,0:T(8,128)S(1)} %shard_map.83), channel_id=1, source_target_pairs={{0,1},{1,0},{2,3},{3,2},{4,5},{5,4},{6,7},{7,6},{8,9},{9,8},{10,11... | collective-permute-start | bytes 1105928 | tf_op jit(solution)/shard_map/ppermute | solution.py:352
  16.5 24.0 %copy-start.1 = (bf16[128,2560]{1,0:T(8,128)(2,1)S(1)}, bf16[128,2560]{1,0:T(8,128)(2,1)}, u32[]{:S(2)}) copy-start(bf16[128,2560]{1,0:T(8,128)(2,1)} %k_ref.7) | copy-start | bytes 1966084
  16.6 24.0 %copy-start.3 = (bf16[128,2560]{1,0:T(8,128)(2,1)S(1)}, bf16[128,2560]{1,0:T(8,128)(2,1)}, u32[]{:S(2)}) copy-start(bf16[128,2560]{1,0:T(8,128)(2,1)} %v_ref.7) | copy-start | bytes 1966084
  16.6 24.0 %copy-start.5 = (bf16[128,2560]{1,0:T(8,128)(2,1)S(1)}, bf16[128,2560]{1,0:T(8,128)(2,1)}, u32[]{:S(2)}) copy-start(bf16[128,2560]{1,0:T(8,128)(2,1)} %w_ref.7) | copy-start | bytes 1966084
  16.7 5.1 %collective-permute-start.1 = (f16[96,256]{1,0:T(8,128)(2,1)S(1)}, f16[96,256]{1,0:T(8,128)(2,1)S(1)}, u32[]{:S(2)}, u32[]{:S(2)}) collective-permute-start(f16[96,256]{1,0:T(8,128)(2,1)S(1)} %convert_element_type.48), channel_id=1, source_target_pairs={{0,2},{2,0},{4,6},{6,4},{8,10},{10,8},{12,14},{14,12},{16,18},{18,... | collective-permute-start | bytes 147464 | tf_op jit(solution)/shard_map/ppermute | solution.py:362
  19.8 4.2 %collective-permute-start.2 = (f16[96,256]{1,0:T(8,128)(2,1)S(1)}, f16[96,256]{1,0:T(8,128)(2,1)S(1)}, u32[]{:S(2)}, u32[]{:S(2)}) collective-permute-start(f16[96,256]{1,0:T(8,128)(2,1)S(1)} %convert_element_type.50), channel_id=1, source_target_pairs={{0,4},{2,6},{4,0},{6,2},{8,12},{10,14},{12,8},{14,10},{16,20},{18,... | collective-permute-start | bytes 147464 | tf_op jit(solution)/shard_map/ppermute | solution.py:362
  21.4 5.1 %collective-permute-start.3 = (f16[96,256]{1,0:T(8,128)(2,1)S(1)}, f16[96,256]{1,0:T(8,128)(2,1)S(1)}, u32[]{:S(2)}, u32[]{:S(2)}) collective-permute-start(f16[96,256]{1,0:T(8,128)(2,1)S(1)} %convert_element_type.52), channel_id=1, source_target_pairs={{0,6},{2,4},{4,2},{6,0},{8,14},{10,12},{12,10},{14,8},{16,22},{18,... | collective-permute-start | bytes 147464 | tf_op jit(solution)/shard_map/ppermute | solution.py:362
  26.6 4.2 %collective-permute-start.4 = (f16[96,256]{1,0:T(8,128)(2,1)S(1)}, f16[96,256]{1,0:T(8,128)(2,1)S(1)}, u32[]{:S(2)}, u32[]{:S(2)}) collective-permute-start(f16[96,256]{1,0:T(8,128)(2,1)S(1)} %convert_element_type.54), channel_id=1, source_target_pairs={{0,8},{2,10},{4,12},{6,14},{8,0},{10,2},{12,4},{14,6},{16,24},{18,... | collective-permute-start | bytes 147464 | tf_op jit(solution)/shard_map/ppermute | solution.py:362
  30.8 6.0 %collective-permute-start.5 = (f16[96,256]{1,0:T(8,128)(2,1)S(1)}, f16[96,256]{1,0:T(8,128)(2,1)S(1)}, u32[]{:S(2)}, u32[]{:S(2)}) collective-permute-start(f16[96,256]{1,0:T(8,128)(2,1)S(1)} %convert_element_type.56), channel_id=1, source_target_pairs={{0,24},{2,26},{4,28},{6,30},{8,16},{10,18},{12,20},{14,22},{16,8},... | collective-permute-start | bytes 147464 | tf_op jit(solution)/shard_map/ppermute | solution.py:362
  36.9 7.6 %collective-permute-start.6 = (f16[80,256]{1,0:T(8,128)(2,1)S(1)}, f16[80,256]{1,0:T(8,128)(2,1)S(1)}, u32[]{:S(2)}, u32[]{:S(2)}) collective-permute-start(f16[80,256]{1,0:T(8,128)(2,1)S(1)} %convert_element_type.58), channel_id=1, source_target_pairs={{0,2},{2,0},{4,6},{6,4},{8,10},{10,8},{12,14},{14,12},{16,18},{18,... | collective-permute-start | bytes 122888 | tf_op jit(solution)/shard_map/ppermute | solution.py:362
  37.5 7.0 %collective-permute-start.7 = (f16[80,256]{1,0:T(8,128)(2,1)S(1)}, f16[80,256]{1,0:T(8,128)(2,1)S(1)}, u32[]{:S(2)}, u32[]{:S(2)}) collective-permute-start(f16[80,256]{1,0:T(8,128)(2,1)S(1)} %convert_element_type.60), channel_id=1, source_target_pairs={{0,4},{2,6},{4,0},{6,2},{8,12},{10,14},{12,8},{14,10},{16,20},{18,... | collective-permute-start | bytes 122888 | tf_op jit(solution)/shard_map/ppermute | solution.py:362
  37.8 6.7 %collective-permute-start.8 = (f16[80,256]{1,0:T(8,128)(2,1)S(1)}, f16[80,256]{1,0:T(8,128)(2,1)S(1)}, u32[]{:S(2)}, u32[]{:S(2)}) collective-permute-start(f16[80,256]{1,0:T(8,128)(2,1)S(1)} %convert_element_type.62), channel_id=1, source_target_pairs={{0,6},{2,4},{4,2},{6,0},{8,14},{10,12},{12,10},{14,8},{16,22},{18,... | collective-permute-start | bytes 122888 | tf_op jit(solution)/shard_map/ppermute | solution.py:362

commit v5 on v4

--- a/solution.py
+++ b/solution.py
@@ -106,20 +106,25 @@
     return own_blocks(wide, CHANNELS), jnp.broadcast_to(final, (8, LANES))
 
 
-def ends_kernel(side, k_ref, v_ref, w_ref, out_ref, k_buf, v_buf, w_buf, sems):
-    groups = out_ref.shape[0]
-    copies = []
-    for index, (ref, buf) in enumerate(((w_ref, w_buf), (k_ref, k_buf), (v_ref, v_buf))):
-        at = half_at(side, groups * LANES)
-        copies.append(pltpu.make_async_copy(ref.at[:, at], buf, sems.at[index]))
-        copies[-1].start()
-    for copy in copies:
-        copy.wait()
-    for group in range(groups):
-        at = pl.ds(group * LANES, LANES)
-        state, decay = ends_of(k_buf[:, at], v_buf[:, at], w_buf[:, at])
-        out_ref[group, :CHANNELS, :] = state
-        out_ref[group, CHANNELS:, :] = decay
+def ends_kernel(k_ref, v_ref, w_ref, mine_ref, theirs_ref, k_buf, v_buf, w_buf, sems):
+    groups = mine_ref.shape[0]
+    half = groups * LANES
+    copies = {}
+    for side in (1, 0):
+        at = half_at(side, half)
+        for index, (ref, buf) in enumerate(((w_ref, w_buf), (k_ref, k_buf), (v_ref, v_buf))):
+            copies[side, index] = pltpu.make_async_copy(
+                ref.at[:, at], buf.at[side], sems.at[side, index]
+            )
+            copies[side, index].start()
+    for side, out_ref in ((1, theirs_ref), (0, mine_ref)):
+        for index in range(3):
+            copies[side, index].wait()
+        for group in range(groups):
+            at = pl.ds(group * LANES, LANES)
+            state, decay = ends_of(k_buf[side, :, at], v_buf[side, :, at], w_buf[side, :, at])
+            out_ref[group, :CHANNELS, :] = state
+            out_ref[group, CHANNELS:, :] = decay
 
 
 def log_rows(groups, group):
@@ -229,17 +234,19 @@
     row = lax.broadcasted_iota(jnp.int32, shape, 0)
     later = row // (HEADS * BLOCK) * BLOCK + row % BLOCK
     strict = later > lax.broadcasted_iota(jnp.int32, shape, 1)
-    for group in range(groups):
-        at = lanes_at(side, group, groups)
-        out = pl.ds(group * LANES, LANES)
-        r, k, v, w = r_ref[:, at].astype(F32), k_ref[:, at].astype(F32), v_ref[:, at], w_ref[:, at]
-        gate = g_ref[:, at].astype(F32)
-        out_ref[2, :, out] = gate / (1.0 + jnp.exp(-gate))
-        cumul = cumulate(w)
-        before = cumul - w.astype(F32)
-        out_ref[1, :, out] = r * jnp.exp(before)
-        diagonal_high, diagonal_low = split(r * table_ref[0:1, at] * k)
-        diagonal = dot(diagonal_high, ones) + dot(diagonal_low, ones)
+    span = range(groups)
+    at = [lanes_at(side, group, groups) for group in span]
+    out = [pl.ds(group * LANES, LANES) for group in span]
+    cumuls = [cumulate(w_ref[:, at[group]]) for group in span]
+    for group in span:
+        gate = g_ref[:, at[group]].astype(F32)
+        out_ref[2, :, out[group]] = gate / (1.0 + jnp.exp(-gate))
+    scores = []
+    for group in span:
+        r, k = r_ref[:, at[group]].astype(F32), k_ref[:, at[group]].astype(F32)
+        cumul = cumuls[group]
+        before = cumul - w_ref[:, at[group]].astype(F32)
+        out_ref[1, :, out[group]] = r * jnp.exp(before)
         pieces = []
         for start in range(0, length, BLOCK):
             stop = start + BLOCK
@@ -253,16 +260,23 @@
                 k_low = jnp.concatenate([k_low, rest], axis=0)
             r_high, r_low = spread_heads(r_high, masks), spread_heads(r_low, masks)
             pieces.append(dot_nt(r_high, k_high) + dot_nt(r_low, k_high) + dot_nt(r_high, k_low))
-        s_high, s_low = split(jnp.where(strict, jnp.concatenate(pieces, axis=0), F32(0.0)))
-        wide = dot(jnp.concatenate([s_high, s_low], axis=1), jnp.concatenate([v, v], axis=0))
+        scores.append(split(jnp.where(strict, jnp.concatenate(pieces, axis=0), F32(0.0))))
+    mixes = []
+    for group in span:
+        v = v_ref[:, at[group]]
+        wide = dot(jnp.concatenate(scores[group], axis=1), jnp.concatenate([v, v], axis=0))
         step = HEADS * BLOCK
         mixed = jnp.concatenate(
             [own_blocks(wide[i * step : (i + 1) * step], BLOCK) for i in range(length // BLOCK)],
             axis=0,
         )
-        mixed = mixed + diagonal * v.astype(F32)
-        m_high, m_low = split(mixed)
-        out_ref[0, :, out] = mixed - (dot(m_high, share) + dot(m_low, share))
+        r, k = r_ref[:, at[group]].astype(F32), k_ref[:, at[group]].astype(F32)
+        diagonal_high, diagonal_low = split(r * table_ref[0:1, at[group]] * k)
+        diagonal = dot(diagonal_high, ones) + dot(diagonal_low, ones)
+        mixes.append(mixed + diagonal * v.astype(F32))
+    for group in span:
+        m_high, m_low = split(mixes[group])
+        out_ref[0, :, out[group]] = mixes[group] - (dot(m_high, share) + dot(m_low, share))
 
 
 def finish_kernel(
@@ -281,32 +295,39 @@
         for group in range(groups):
             at = pl.multiple_of(source + group * CHANNELS, ROWS)
             state_ref[pl.ds(at, ROWS), :] = piece[group * ROWS : (group + 1) * ROWS, :] * F32(1.0 / scale)
+    states = {}
+    for group in range(groups):
+        early = jnp.where(first, ends_mine[group], ends_other[group])
+        near = state_ref[group * CHANNELS : (group + 1) * CHANNELS, :]
+        far = jnp.exp(early[CHANNELS : CHANNELS + 1]) * near + early[:CHANNELS]
+        near = split(near - jnp.mean(near, axis=0, keepdims=True))
+        far = split(far - jnp.mean(far, axis=0, keepdims=True))
+        for side in range(2):
+            pick = first if side == 0 else jnp.logical_not(first)
+            states[side, group] = [
+                spread_heads(jnp.where(pick, one, two), masks) for one, two in zip(near, far)
+            ]
     copies = []
-    for group in range(groups):
-        at = lanes_at(0, group, groups)
-        out = pl.ds(group * LANES, LANES)
-        early = jnp.where(first, ends_mine[group], ends_other[group])
-        state = state_ref[group * CHANNELS : (group + 1) * CHANNELS, :]
-        for half in range(2):
-            local = core == half
-            if half == 1:
-                state = jnp.exp(early[CHANNELS : CHANNELS + 1]) * state + early[:CHANNELS]
-            s_high, s_low = split(state - jnp.mean(state, axis=0, keepdims=True))
-            s_high, s_low = spread_heads(s_high, masks), spread_heads(s_low, masks)
-            r_high, r_low = split(jnp.where(local, in_mine[1, :, out], in_other[1, :, out]))
-            mixed = jnp.where(local, in_mine[0, :, out], in_other[0, :, out])
-            mixed = mixed + (
+    for side, local in enumerate((in_mine, in_other)):
+        mixes, spreads = {}, {}
+        for group in range(groups):
+            out = pl.ds(group * LANES, LANES)
+            s_high, s_low = states[side, group]
+            r_high, r_low = split(local[1, :, out])
+            mixes[group] = local[0, :, out] + (
                 dot_nt(r_high, s_high) + dot_nt(r_low, s_high) + dot_nt(r_high, s_low)
             )
-            q_high, q_low = split(mixed * mixed)
-            spread = dot(q_high, share) + dot(q_low, share)
-            normed = mixed * lax.rsqrt(spread + 1e-5)
-            gate = jnp.where(local, in_mine[2, :, out], in_other[2, :, out])
-            gated = (normed * table_ref[1:2, at] + table_ref[2:3, at]) * gate
-            buf[half * length : (half + 1) * length, out] = gated.astype(BF16)
-        copies.append(
-            pltpu.make_async_copy(buf.at[:, out], out_ref.at[:, out], sems.at[group])
-        )
+        for group in range(groups):
+            q_high, q_low = split(mixes[group] * mixes[group])
+            spreads[group] = dot(q_high, share) + dot(q_low, share)
+        for group in range(groups):
+            at = lanes_at(0, group, groups)
+            out = pl.ds(group * LANES, LANES)
+            normed = mixes[group] * lax.rsqrt(spreads[group] + 1e-5)
+            gated = (normed * table_ref[1:2, at] + table_ref[2:3, at]) * local[2, :, out]
+            buf[side, :, out] = gated.astype(BF16)
+        rows = pl.ds(pl.multiple_of((core if side == 0 else 1 - core) * length, length), length)
+        copies.append(pltpu.make_async_copy(buf.at[side], out_ref.at[rows, :], sems.at[side]))
         copies[-1].start()
     for copy in copies:
         copy.wait()
@@ -340,17 +361,14 @@
     while STATE_STEP * length * cores * count * scale > 2.0**15:
         scale *= 0.5
 
-    def ends(side):
-        return call(
-            functools.partial(ends_kernel, side),
-            ends_shape,
-            in_specs=[hbm] * 3,
-            scratch_shapes=[pltpu.VMEM((length, half), BF16)] * 3
-            + [pltpu.SemaphoreType.DMA((3,))],
-        )(*(pltpu.with_memory_space_constraint(x, pltpu.HBM) for x in (k, v, w)))
-
-    other = lax.ppermute(ends(1), "head", swap)
-    mine = ends(0)
+    mine, theirs = call(
+        ends_kernel,
+        [ends_shape] * 2,
+        in_specs=[hbm] * 3,
+        scratch_shapes=[pltpu.VMEM((cores, length, half), BF16)] * 3
+        + [pltpu.SemaphoreType.DMA((cores, 3))],
+    )(*(pltpu.with_memory_space_constraint(x, pltpu.HBM) for x in (k, v, w)))
+    other = lax.ppermute(theirs, "head", swap)
 
     def within(side):
         return call(
@@ -395,8 +413,8 @@
         out_specs=hbm,
         scratch_shapes=[
             pltpu.VMEM((groups * CHANNELS, LANES), F32),
-            pltpu.VMEM((cores * length, half), BF16),
-            pltpu.SemaphoreType.DMA((groups,)),
+            pltpu.VMEM((cores, length, half), BF16),
+            pltpu.SemaphoreType.DMA((cores,)),
         ],
     )(*to_places(states), mine, other, in_mine, in_other, table)
 

time: 49.8 us -> 44.5 us (0.89)
  Pallas kernels: 17.1 us -> 10.6 us
  waiting for transfers between devices: 9.77 us -> 11.4 us
    pallas_call x2, Pallas kernels: 7.78 us -> 4.52 us  [within(): call(functools.partial(within_kernel, side), jax.ShapeDtypeStruct((3, len...]
    pallas_call x1, Pallas kernels: 4.68 us -> 2.61 us  [program(): call(functools.partial(finish_kernel, scale), jax.ShapeDtypeStruct((cores...]
    ppermute x1, waiting for transfers between devices: 0.01 us -> 1.66 us  [program(): other = lax.ppermute(theirs, 'head', swap)]
    pallas_call x2 -> x1, Pallas kernels: 4.26 us -> 3.09 us  [program(): call(ends_kernel, [ends_shape] * 2, in_specs=[hbm] * 3, scratch_shapes=[p...]
  transfers between devices with their start and end apart: 10 -> 10, of which waited for: 5 -> 6; matrix products, arithmetic and copies ran while one was open for 0% -> 0% of each run, Pallas kernels for 17% -> 13%
where the time goes in v5:
time: 44.5 us; the launch traced here: 44 us
  starting transfers between devices  14 us (31%)
  waiting for transfers between devices  11.4 us (26%)
  Pallas kernels  10.6 us (24%)
  local copies, waits for them, and re-layouts  7.68 us (17%)
    ppermute x8, starting transfers between devices, over_seq(): return lax.ppermute(value.astype(jnp.float16), 'seq', pairs).astype(F32)  13.3 us
    ppermute x8, waiting for transfers between devices, over_seq(): return lax.ppermute(value.astype(jnp.float16), 'seq', pairs).astype(F32)  9.75 us
    unnamed x16, local copies, waits for them, and re-layouts  5.45 us
    pallas_call x2, Pallas kernels, within(): call(functools.partial(within_kernel, side), jax.ShapeDtypeStruct((3, len...  4.52 us
    pallas_call x1, Pallas kernels, program(): call(ends_kernel, [ends_shape] * 2, in_specs=[hbm] * 3, scratch_shapes=[p...  3.09 us
    pallas_call x1, Pallas kernels, program(): call(functools.partial(finish_kernel, scale), jax.ShapeDtypeStruct((cores...  2.61 us
    another operation x3, local copies, waits for them, and re-layouts, program(): table = jnp.stack([bonus.reshape(width), gain, bias])  2.23 us
    ppermute x1, waiting for transfers between devices, program(): other = lax.ppermute(theirs, 'head', swap)  1.66 us
  transfers between devices with their start and end apart: 10, of which 6 were waited for; matrix products, arithmetic and copies ran while one was open for 0% of the time, Pallas kernels for 13%

profile of v5, /device:TPU:0, one launch (start us, length us, event | category | flops | bytes accessed | tf_op | source)
XLA Modules:
  0.0 44.0 jit_solution(2045911569500172673)
XLA Ops:
  0.0 0.7 %stack.10 = f32[1,2560]{1,0:T(1,128)S(1)} reshape(f32[2560]{0:T(1024)} %param.15) | data formatting | bytes 20480 | tf_op jit(solution)/shard_map/stack | solution.py:346
  0.7 0.7 %stack.9 = f32[1,2560]{1,0:T(1,128)S(1)} reshape(f32[2560]{0:T(1024)} %param.14) | data formatting | bytes 20480 | tf_op jit(solution)/shard_map/stack | solution.py:346
  1.4 0.8 %stack_reshape.3 = f32[1,2560]{1,0:T(1,128)S(1)} reshape(f32[40,64]{1,0:T(8,128)} %param.13) | data formatting | bytes 20480 | tf_op jit(solution)/shard_map/stack;reshape | solution.py:346
  2.3 1.1 %copy-done = bf16[128,2560]{1,0:T(8,128)(2,1)S(1)} copy-done((bf16[128,2560]{1,0:T(8,128)(2,1)S(1)}, bf16[128,2560]{1,0:T(8,128)(2,1)}, u32[]{:S(2)}) %copy-start) | copy-done | bytes 655384
  3.4 1.1 %copy-done.2 = bf16[128,2560]{1,0:T(8,128)(2,1)S(1)} copy-done((bf16[128,2560]{1,0:T(8,128)(2,1)S(1)}, bf16[128,2560]{1,0:T(8,128)(2,1)}, u32[]{:S(2)}) %copy-start.2) | copy-done | bytes 655384
  4.5 1.1 %copy-done.4 = bf16[128,2560]{1,0:T(8,128)(2,1)S(1)} copy-done((bf16[128,2560]{1,0:T(8,128)(2,1)S(1)}, bf16[128,2560]{1,0:T(8,128)(2,1)}, u32[]{:S(2)}) %copy-start.4) | copy-done | bytes 655384
  5.5 1.1 %copy-done.6 = bf16[128,2560]{1,0:T(8,128)(2,1)S(1)} copy-done((bf16[128,2560]{1,0:T(8,128)(2,1)S(1)}, bf16[128,2560]{1,0:T(8,128)(2,1)}, u32[]{:S(2)}) %copy-start.6) | copy-done | bytes 655384
  6.6 1.1 %copy-done.7 = bf16[128,2560]{1,0:T(8,128)(2,1)S(1)} copy-done((bf16[128,2560]{1,0:T(8,128)(2,1)S(1)}, bf16[128,2560]{1,0:T(8,128)(2,1)}, u32[]{:S(2)}) %copy-start.7) | copy-done | bytes 655384
  7.7 2.3 %shard_map.88 = f32[3,128,1280]{2,1,0:T(8,128)S(1)} custom-call(bf16[128,2560]{1,0:T(8,128)(2,1)S(1)} %copy-done.6, bf16[128,2560]{1,0:T(8,128)(2,1)S(1)} %copy-done, bf16[128,2560]{1,0:T(8,128)(2,1)S(1)} %copy-done.2, bf16[128,2560]{1,0:T(8,128)(2,1)S(1)} %copy-done.4, bf16[128,2560]{1,0:T(8,128)(2,1)S(1)} %copy-done.7, f32[3,2560]{1,0:T(4,128)S(1)} %pad_maximum_fusion.table_ref), custom_call_target="tpu_custom_call" | custom-call | tf_op jit(solution)/shard_map/pallas_call | solution.py:374
  10.5 3.1 %shard_map.82 = (f32[5,72,256]{2,1,0:T(8,128)S(1)}, f32[5,72,256]{2,1,0:T(8,128)S(1)}) custom-call(bf16[128,2560]{1,0:T(8,128)(2,1)} %k_ref.5, bf16[128,2560]{1,0:T(8,128)(2,1)} %v_ref.5, bf16[128,2560]{1,0:T(8,128)(2,1)} %w_ref.5), custom_call_target="tpu_custom_call" | custom-call | tf_op jit(solution)/shard_map/pallas_call | solution.py:364
  13.8 1.7 %collective-permute-done.other_ref.ends_other = f32[5,72,256]{2,1,0:T(8,128)S(1)} collective-permute-done((f32[5,72,256]{2,1,0:T(8,128)S(1)}, f32[5,72,256]{2,1,0:T(8,128)S(1)}, u32[]{:S(2)}, u32[]{:S(2)}) %collective-permute-start) | collective-permute-done | bytes 368672 | tf_op jit(solution)/shard_map/ppermute | solution.py:371
  15.6 2.7 %collective-permute-start.1 = (f16[96,256]{1,0:T(8,128)(2,1)S(1)}, f16[96,256]{1,0:T(8,128)(2,1)S(1)}, u32[]{:S(2)}, u32[]{:S(2)}) collective-permute-start(f16[96,256]{1,0:T(8,128)(2,1)S(1)} %convert_element_type.48), channel_id=1, source_target_pairs={{0,2},{2,0},{4,6},{6,4},{8,10},{10,8},{12,14},{14,12},{16,18},{18,... | collective-permute-start | bytes 147464 | tf_op jit(solution)/shard_map/ppermute | solution.py:380
  18.3 1.6 %collective-permute-start.2 = (f16[96,256]{1,0:T(8,128)(2,1)S(1)}, f16[96,256]{1,0:T(8,128)(2,1)S(1)}, u32[]{:S(2)}, u32[]{:S(2)}) collective-permute-start(f16[96,256]{1,0:T(8,128)(2,1)S(1)} %convert_element_type.50), channel_id=1, source_target_pairs={{0,4},{2,6},{4,0},{6,2},{8,12},{10,14},{12,8},{14,10},{16,20},{18,... | collective-permute-start | bytes 147464 | tf_op jit(solution)/shard_map/ppermute | solution.py:380
  19.9 0.6 %collective-permute-done.1 = f16[96,256]{1,0:T(8,128)(2,1)S(1)} collective-permute-done((f16[96,256]{1,0:T(8,128)(2,1)S(1)}, f16[96,256]{1,0:T(8,128)(2,1)S(1)}, u32[]{:S(2)}, u32[]{:S(2)}) %collective-permute-start.1) | collective-permute-done | bytes 49184 | tf_op jit(solution)/shard_map/ppermute | solution.py:380
  20.6 1.9 %collective-permute-done.2 = f16[96,256]{1,0:T(8,128)(2,1)S(1)} collective-permute-done((f16[96,256]{1,0:T(8,128)(2,1)S(1)}, f16[96,256]{1,0:T(8,128)(2,1)S(1)}, u32[]{:S(2)}, u32[]{:S(2)}) %collective-permute-start.2) | collective-permute-done | bytes 49184 | tf_op jit(solution)/shard_map/ppermute | solution.py:380
  22.4 2.5 %collective-permute-done.3 = f16[96,256]{1,0:T(8,128)(2,1)S(1)} collective-permute-done((f16[96,256]{1,0:T(8,128)(2,1)S(1)}, f16[96,256]{1,0:T(8,128)(2,1)S(1)}, u32[]{:S(2)}, u32[]{:S(2)}) %collective-permute-start.3) | collective-permute-done | bytes 49184 | tf_op jit(solution)/shard_map/ppermute | solution.py:380
  25.1 1.6 %collective-permute-start.4 = (f16[96,256]{1,0:T(8,128)(2,1)S(1)}, f16[96,256]{1,0:T(8,128)(2,1)S(1)}, u32[]{:S(2)}, u32[]{:S(2)}) collective-permute-start(f16[96,256]{1,0:T(8,128)(2,1)S(1)} %convert_element_type.54), channel_id=1, source_target_pairs={{0,8},{2,10},{4,12},{6,14},{8,0},{10,2},{12,4},{14,6},{16,24},{18,... | collective-permute-start | bytes 147464 | tf_op jit(solution)/shard_map/ppermute | solution.py:380
  26.7 2.5 %collective-permute-done.4 = f16[96,256]{1,0:T(8,128)(2,1)S(1)} collective-permute-done((f16[96,256]{1,0:T(8,128)(2,1)S(1)}, f16[96,256]{1,0:T(8,128)(2,1)S(1)}, u32[]{:S(2)}, u32[]{:S(2)}) %collective-permute-start.4) | collective-permute-done | bytes 49184 | tf_op jit(solution)/shard_map/ppermute | solution.py:380
  29.3 3.7 %collective-permute-start.5 = (f16[96,256]{1,0:T(8,128)(2,1)S(1)}, f16[96,256]{1,0:T(8,128)(2,1)S(1)}, u32[]{:S(2)}, u32[]{:S(2)}) collective-permute-start(f16[96,256]{1,0:T(8,128)(2,1)S(1)} %convert_element_type.56), channel_id=1, source_target_pairs={{0,24},{2,26},{4,28},{6,30},{8,16},{10,18},{12,20},{14,22},{16,8},... | collective-permute-start | bytes 147464 | tf_op jit(solution)/shard_map/ppermute | solution.py:380
  33.0 2.3 %collective-permute-done.5 = f16[96,256]{1,0:T(8,128)(2,1)S(1)} collective-permute-done((f16[96,256]{1,0:T(8,128)(2,1)S(1)}, f16[96,256]{1,0:T(8,128)(2,1)S(1)}, u32[]{:S(2)}, u32[]{:S(2)}) %collective-permute-start.5) | collective-permute-done | bytes 49184 | tf_op jit(solution)/shard_map/ppermute | solution.py:380
  35.3 0.6 %collective-permute-start.6 = (f16[80,256]{1,0:T(8,128)(2,1)S(1)}, f16[80,256]{1,0:T(8,128)(2,1)S(1)}, u32[]{:S(2)}, u32[]{:S(2)}) collective-permute-start(f16[80,256]{1,0:T(8,128)(2,1)S(1)} %convert_element_type.58), channel_id=1, source_target_pairs={{0,2},{2,0},{4,6},{6,4},{8,10},{10,8},{12,14},{14,12},{16,18},{18,... | collective-permute-start | bytes 122888 | tf_op jit(solution)/shard_map/ppermute | solution.py:380
  36.3 2.7 %collective-permute-start.8 = (f16[80,256]{1,0:T(8,128)(2,1)S(1)}, f16[80,256]{1,0:T(8,128)(2,1)S(1)}, u32[]{:S(2)}, u32[]{:S(2)}) collective-permute-start(f16[80,256]{1,0:T(8,128)(2,1)S(1)} %convert_element_type.62), channel_id=1, source_target_pairs={{0,6},{2,4},{4,2},{6,0},{8,14},{10,12},{12,10},{14,8},{16,22},{18,... | collective-permute-start | bytes 122888 | tf_op jit(solution)/shard_map/ppermute | solution.py:380
  39.0 2.3 %shard_map.87.in_mine = f32[3,128,1280]{2,1,0:T(8,128)S(1)} custom-call(bf16[128,2560]{1,0:T(8,128)(2,1)S(1)} %copy-done.6, bf16[128,2560]{1,0:T(8,128)(2,1)S(1)} %copy-done.1, bf16[128,2560]{1,0:T(8,128)(2,1)S(1)} %copy-done.3, bf16[128,2560]{1,0:T(8,128)(2,1)S(1)} %copy-done.5, bf16[128,2560]{1,0:T(8,128)(2,1)S(1)} %copy-done.7, ...), custom_call_target="tpu_custom_call" | custom-call | tf_op jit(solution)/shard_map/pallas_call | solution.py:374
  41.4 2.6 %shard_map.89 = bf16[256,1280]{1,0:T(8,128)(2,1)} custom-call(f32[80,256]{1,0:T(8,128)S(1)} %get-tuple-element.29.p0, f32[80,256]{1,0:T(8,128)S(1)} %convert_element_type.59.p1, f32[80,256]{1,0:T(8,128)S(1)} %convert_element_type.61.p2, f32[80,256]{1,0:T(8,128)S(1)} %convert_element_type.63.p3, f32[5,72,256]{2,1,0:T(8,128)S(1)} %get-tuple-element.19.mine_ref.ends_mine, ...), custom_call_target="tpu_custom_call" | custom-call | tf_op jit(solution)/shard_map/pallas_call | solution.py:410
  (40 shorter events, 1.6 us)
Async XLA Ops:
  2.3 1.1 %copy-start = (bf16[128,2560]{1,0:T(8,128)(2,1)S(1)}, bf16[128,2560]{1,0:T(8,128)(2,1)}, u32[]{:S(2)}) copy-start(bf16[128,2560]{1,0:T(8,128)(2,1)} %k_ref.5) | copy-start | bytes 1966084
  3.4 1.1 %copy-start.2 = (bf16[128,2560]{1,0:T(8,128)(2,1)S(1)}, bf16[128,2560]{1,0:T(8,128)(2,1)}, u32[]{:S(2)}) copy-start(bf16[128,2560]{1,0:T(8,128)(2,1)} %v_ref.5) | copy-start | bytes 1966084
  4.5 1.1 %copy-start.4 = (bf16[128,2560]{1,0:T(8,128)(2,1)S(1)}, bf16[128,2560]{1,0:T(8,128)(2,1)}, u32[]{:S(2)}) copy-start(bf16[128,2560]{1,0:T(8,128)(2,1)} %w_ref.5) | copy-start | bytes 1966084
  5.5 1.1 %copy-start.6 = (bf16[128,2560]{1,0:T(8,128)(2,1)S(1)}, bf16[128,2560]{1,0:T(8,128)(2,1)}, u32[]{:S(2)}) copy-start(bf16[128,2560]{1,0:T(8,128)(2,1)} %r_ref.3) | copy-start | bytes 1966084
  6.6 1.1 %copy-start.7 = (bf16[128,2560]{1,0:T(8,128)(2,1)S(1)}, bf16[128,2560]{1,0:T(8,128)(2,1)}, u32[]{:S(2)}) copy-start(bf16[128,2560]{1,0:T(8,128)(2,1)} %g_ref.3) | copy-start | bytes 1966084
  10.0 31.4 %collective-permute-start.9 = (f32[3,128,1280]{2,1,0:T(8,128)S(1)}, f32[3,128,1280]{2,1,0:T(8,128)S(1)}, u32[]{:S(2)}, u32[]{:S(2)}) collective-permute-start(f32[3,128,1280]{2,1,0:T(8,128)S(1)} %shard_map.88), channel_id=1, source_target_pairs={{0,1},{1,0},{2,3},{3,2},{4,5},{5,4},{6,7},{7,6},{8,9},{9,8},{10,11... | collective-permute-start | bytes 5898248 | tf_op jit(solution)/shard_map/ppermute | solution.py:393
  13.6 25.4 %copy-start.1 = (bf16[128,2560]{1,0:T(8,128)(2,1)S(1)}, bf16[128,2560]{1,0:T(8,128)(2,1)}, u32[]{:S(2)}) copy-start(bf16[128,2560]{1,0:T(8,128)(2,1)} %k_ref.5) | copy-start | bytes 1966084
  13.7 25.4 %copy-start.3 = (bf16[128,2560]{1,0:T(8,128)(2,1)S(1)}, bf16[128,2560]{1,0:T(8,128)(2,1)}, u32[]{:S(2)}) copy-start(bf16[128,2560]{1,0:T(8,128)(2,1)} %v_ref.5) | copy-start | bytes 1966084
  13.7 25.4 %copy-start.5 = (bf16[128,2560]{1,0:T(8,128)(2,1)S(1)}, bf16[128,2560]{1,0:T(8,128)(2,1)}, u32[]{:S(2)}) copy-start(bf16[128,2560]{1,0:T(8,128)(2,1)} %w_ref.5) | copy-start | bytes 1966084
  13.7 1.8 %collective-permute-start = (f32[5,72,256]{2,1,0:T(8,128)S(1)}, f32[5,72,256]{2,1,0:T(8,128)S(1)}, u32[]{:S(2)}, u32[]{:S(2)}) collective-permute-start(f32[5,72,256]{2,1,0:T(8,128)S(1)} %get-tuple-element.20), channel_id=1, source_target_pairs={{0,1},{1,0},{2,3},{3,2},{4,5},{5,4},{6,7},{7,6},{8,9},{9,8},{10,11... | collective-permute-start | bytes 1105928 | tf_op jit(solution)/shard_map/ppermute | solution.py:371
  15.6 5.0 %collective-permute-start.1 = (f16[96,256]{1,0:T(8,128)(2,1)S(1)}, f16[96,256]{1,0:T(8,128)(2,1)S(1)}, u32[]{:S(2)}, u32[]{:S(2)}) collective-permute-start(f16[96,256]{1,0:T(8,128)(2,1)S(1)} %convert_element_type.48), channel_id=1, source_target_pairs={{0,2},{2,0},{4,6},{6,4},{8,10},{10,8},{12,14},{14,12},{16,18},{18,... | collective-permute-start | bytes 147464 | tf_op jit(solution)/shard_map/ppermute | solution.py:380
  18.3 4.2 %collective-permute-start.2 = (f16[96,256]{1,0:T(8,128)(2,1)S(1)}, f16[96,256]{1,0:T(8,128)(2,1)S(1)}, u32[]{:S(2)}, u32[]{:S(2)}) collective-permute-start(f16[96,256]{1,0:T(8,128)(2,1)S(1)} %convert_element_type.50), channel_id=1, source_target_pairs={{0,4},{2,6},{4,0},{6,2},{8,12},{10,14},{12,8},{14,10},{16,20},{18,... | collective-permute-start | bytes 147464 | tf_op jit(solution)/shard_map/ppermute | solution.py:380
  19.9 5.1 %collective-permute-start.3 = (f16[96,256]{1,0:T(8,128)(2,1)S(1)}, f16[96,256]{1,0:T(8,128)(2,1)S(1)}, u32[]{:S(2)}, u32[]{:S(2)}) collective-permute-start(f16[96,256]{1,0:T(8,128)(2,1)S(1)} %convert_element_type.52), channel_id=1, source_target_pairs={{0,6},{2,4},{4,2},{6,0},{8,14},{10,12},{12,10},{14,8},{16,22},{18,... | collective-permute-start | bytes 147464 | tf_op jit(solution)/shard_map/ppermute | solution.py:380
  25.1 4.2 %collective-permute-start.4 = (f16[96,256]{1,0:T(8,128)(2,1)S(1)}, f16[96,256]{1,0:T(8,128)(2,1)S(1)}, u32[]{:S(2)}, u32[]{:S(2)}) collective-permute-start(f16[96,256]{1,0:T(8,128)(2,1)S(1)} %convert_element_type.54), channel_id=1, source_target_pairs={{0,8},{2,10},{4,12},{6,14},{8,0},{10,2},{12,4},{14,6},{16,24},{18,... | collective-permute-start | bytes 147464 | tf_op jit(solution)/shard_map/ppermute | solution.py:380
  29.3 6.0 %collective-permute-start.5 = (f16[96,256]{1,0:T(8,128)(2,1)S(1)}, f16[96,256]{1,0:T(8,128)(2,1)S(1)}, u32[]{:S(2)}, u32[]{:S(2)}) collective-permute-start(f16[96,256]{1,0:T(8,128)(2,1)S(1)} %convert_element_type.56), channel_id=1, source_target_pairs={{0,24},{2,26},{4,28},{6,30},{8,16},{10,18},{12,20},{14,22},{16,8},... | collective-permute-start | bytes 147464 | tf_op jit(solution)/shard_map/ppermute | solution.py:380
  35.3 6.0 %collective-permute-start.6 = (f16[80,256]{1,0:T(8,128)(2,1)S(1)}, f16[80,256]{1,0:T(8,128)(2,1)S(1)}, u32[]{:S(2)}, u32[]{:S(2)}) collective-permute-start(f16[80,256]{1,0:T(8,128)(2,1)S(1)} %convert_element_type.58), channel_id=1, source_target_pairs={{0,2},{2,0},{4,6},{6,4},{8,10},{10,8},{12,14},{14,12},{16,18},{18,... | collective-permute-start | bytes 122888 | tf_op jit(solution)/shard_map/ppermute | solution.py:380
  36.0 5.4 %collective-permute-start.7 = (f16[80,256]{1,0:T(8,128)(2,1)S(1)}, f16[80,256]{1,0:T(8,128)(2,1)S(1)}, u32[]{:S(2)}, u32[]{:S(2)}) collective-permute-start(f16[80,256]{1,0:T(8,128)(2,1)S(1)} %convert_element_type.60), channel_id=1, source_target_pairs={{0,4},{2,6},{4,0},{6,2},{8,12},{10,14},{12,8},{14,10},{16,20},{18,... | collective-permute-start | bytes 122888 | tf_op jit(solution)/shard_map/ppermute | solution.py:380
  36.3 5.1 %collective-permute-start.8 = (f16[80,256]{1,0:T(8,128)(2,1)S(1)}, f16[80,256]{1,0:T(8,128)(2,1)S(1)}, u32[]{:S(2)}, u32[]{:S(2)}) collective-permute-start(f16[80,256]{1,0:T(8,128)(2,1)S(1)} %convert_element_type.62), channel_id=1, source_target_pairs={{0,6},{2,4},{4,2},{6,0},{8,14},{10,12},{12,10},{14,8},{16,22},{18,... | collective-permute-start | bytes 122888 | tf_op jit(solution)/shard_map/ppermute | solution.py:380
